TPU v7x, 32 devices: a whole 2x2x4 slice. The times are simulated.
32 devices in a mesh: ctx: 16 (over z, x, core), fsdp: 2 (over y).
Axes of the slice: x: 2, y: 2, z: 4, core: 2. Of those that a mesh axis runs over, the one named last changes fastest.
Arguments:
- tokens: bfloat16 [2, 2048, 1024], P('fsdp', 'ctx'), may hold values from -6 to 6
- cotangent: bfloat16 [2, 2048, 1024], P('fsdp', 'ctx'), may hold values from -6 to 6
- gain_attn: float32 [1024], replicated, may hold values from 0.5 to 1.5
- gain_mlp: float32 [1024], replicated, may hold values from 0.5 to 1.5
- qkv_weight: bfloat16 [3072, 1024], P('fsdp'), may hold values from -2 to 2
- out_weight: bfloat16 [1024, 1024], P('fsdp'), may hold values from -0.625 to 0.625
- in_weight: bfloat16 [5248, 1024], P('fsdp'), may hold values from -0.1875 to 0.1875
- down_weight: bfloat16 [1024, 2624], P('fsdp'), may hold values from -0.125 to 0.125
Outputs:
- output: float32 [2, 2048, 1024], P('fsdp', 'ctx')
- grad_input: float32 [2, 2048, 1024], P('fsdp', 'ctx')
- grad_qkv: float32 [3072, 1024], P(('ctx', 'fsdp'))
- grad_out_proj: float32 [1024, 1024], P(('ctx', 'fsdp'))
- grad_in_proj: float32 [5248, 1024], P(('ctx', 'fsdp'))
- grad_down: float32 [1024, 2624], P(('ctx', 'fsdp'))
- grad_gain_attn: float32 [1024], P(('ctx', 'fsdp'))
- grad_gain_mlp: float32 [1024], P(('ctx', 'fsdp'))
All inputs are finite; a program needn't handle non-finite values.
Results may differ from a plain program's by a relative error of at most 0.015.
Values may be sent and summed in bfloat16 or wider, within the bound.
A program may use at most 256 MiB of HBM per device.

v0:
```python
import math

import jax
import jax.numpy as jnp
from jax import lax
from jax.sharding import PartitionSpec as P

HEAD_DIM = 64


EPSILON = 1e-05
ROPE_BASE = 160000.0


def normalize(tensor):
    centred = tensor - jnp.mean(tensor, axis=-1, keepdims=True)
    inv_std = lax.rsqrt(jnp.mean(centred * centred, axis=-1, keepdims=True) + EPSILON)
    return (centred * inv_std, inv_std)


def norm_back(grad_norm, normed, inv_std):
    return inv_std * (
        grad_norm
        - jnp.mean(grad_norm, axis=-1, keepdims=True)
        - normed * jnp.mean(grad_norm * normed, axis=-1, keepdims=True)
    )


def gelu_pair(tensor):
    cumul = 0.5 * (1.0 + jax.scipy.special.erf(tensor * 0.7071067811865476))
    density = jnp.exp(-0.5 * tensor * tensor) * 0.3989422804014327
    return (tensor * cumul, cumul + tensor * density)


def rope_tables(offset, length, head_size):
    positions = (offset + jnp.arange(length, dtype=jnp.int32)).astype(jnp.float32)
    inverse = ROPE_BASE ** (
        -jnp.arange(0, head_size, 2, dtype=jnp.int32).astype(jnp.float32) / head_size
    )
    angles = positions[:, None] * inverse[None, :]
    angles = jnp.concatenate([angles, angles], axis=-1)
    return (jnp.cos(angles)[:, None, :], jnp.sin(angles)[:, None, :])


def rotate(tensor, cos_table, sine_table):
    middle = tensor.shape[-1] // 2
    turned = jnp.concatenate([-tensor[..., middle:], tensor[..., :middle]], axis=-1)
    return tensor * cos_table + turned * sine_table


def rotate_back(gradient, cos_table, sine_table):
    middle = gradient.shape[-1] // 2
    scaled = gradient * sine_table
    turned = jnp.concatenate([scaled[..., middle:], -scaled[..., :middle]], axis=-1)
    return gradient * cos_table + turned


def rows_product(left, right):
    return lax.dot_general(
        left, right, (((1,), (1,)), ((), ())), preferred_element_type=jnp.float32
    )


def rows_contract(left, right):
    return lax.dot_general(
        left, right, (((0,), (0,)), ((), ())), preferred_element_type=jnp.float32
    )


def per_device(
    tokens, cotangent, gain_attn, gain_mlp, qkv_weight, out_weight, in_weight, down_weight
):
    f32 = jnp.float32
    bf16 = jnp.bfloat16
    qkv_full, out_full, in_full, down_full = (
        lax.all_gather(qkv_weight, "fsdp", axis=0, tiled=True),
        lax.all_gather(out_weight, "fsdp", axis=0, tiled=True),
        lax.all_gather(in_weight, "fsdp", axis=0, tiled=True),
        lax.all_gather(down_weight, "fsdp", axis=0, tiled=True),
    )
    tok_rows = tokens.shape[1]
    width = tokens.shape[2]
    hidden = down_full.shape[1]
    head_size = HEAD_DIM
    head_count = width // head_size
    scale = head_size ** (-0.5)
    offset = lax.axis_index("ctx") * tok_rows
    cos_table, sine_table = rope_tables(offset, tok_rows, head_size)
    resid = tokens[0].astype(f32)
    normed_a, inv_a = normalize(resid)
    act_a = (normed_a * gain_attn).astype(bf16)
    packed = rows_product(act_a, qkv_full)
    query_heads = rotate(
        packed[:, :width].reshape(tok_rows, head_count, head_size), cos_table, sine_table
    ).astype(bf16)
    key_heads = rotate(
        packed[:, width : 2 * width].reshape(tok_rows, head_count, head_size), cos_table, sine_table
    ).astype(bf16)
    value_send = packed[:, 2 * width :].astype(bf16)
    key_send = key_heads.reshape(tok_rows, width)
    value_heads = value_send.reshape(tok_rows, head_count, head_size)
    start_state = (
        jnp.zeros((tok_rows, head_count, head_size), f32),
        jnp.full((head_count, tok_rows), -1e30, f32),
        jnp.zeros((head_count, tok_rows), f32),
    )
    key_piece = lax.all_gather(key_send, "ctx", axis=0, tiled=True)
    value_piece = lax.all_gather(value_send, "ctx", axis=0, tiled=True)
    length = key_piece.shape[0]
    step_len = math.gcd(length, 1024)

    def attend_block(block_num, running):
        weighted, row_max, row_sum = running
        key_blk = lax.dynamic_slice_in_dim(key_piece, block_num * step_len, step_len, 0).reshape(
            step_len, head_count, head_size
        )
        value_blk = lax.dynamic_slice_in_dim(
            value_piece, block_num * step_len, step_len, 0
        ).reshape(step_len, head_count, head_size)
        scores = (
            jnp.einsum("qhd,khd->hqk", query_heads, key_blk, preferred_element_type=f32) * scale
        )
        new_max = jnp.maximum(row_max, jnp.max(scores, axis=-1))
        shrink = jnp.exp(row_max - new_max)
        weights = jnp.exp(scores - new_max[..., None])
        row_sum = row_sum * shrink + jnp.sum(weights, axis=-1)
        weighted = weighted * shrink.T[:, :, None] + jnp.einsum(
            "hqk,khd->qhd", weights.astype(bf16), value_blk, preferred_element_type=f32
        )
        return (weighted, new_max, row_sum)

    weighted, row_max, row_sum = lax.fori_loop(0, length // step_len, attend_block, start_state)
    log_sum = row_max + jnp.log(row_sum)
    mixed = (weighted / row_sum.T[:, :, None]).reshape(tok_rows, width).astype(bf16)
    middle = resid + rows_product(mixed, out_full)
    normed_m, inv_m = normalize(middle)
    act_m = (normed_m * gain_mlp).astype(bf16)
    inner = rows_product(act_m, in_full)
    gelu_val, gelu_slope = gelu_pair(inner[:, :hidden])
    gated = (gelu_val * inner[:, hidden:]).astype(bf16)
    output = middle + rows_product(gated, down_full)
    cot_rows = cotangent[0]
    grad_down = rows_contract(cot_rows, gated)
    grad_gated = jnp.dot(cot_rows, down_full, preferred_element_type=f32)
    grad_inner = jnp.concatenate(
        [grad_gated * inner[:, hidden:] * gelu_slope, grad_gated * gelu_val], axis=1
    ).astype(bf16)
    grad_in = rows_contract(grad_inner, act_m)
    grad_act_m = jnp.dot(grad_inner, in_full, preferred_element_type=f32)
    grad_gain_m = jnp.sum(grad_act_m * normed_m, axis=0)
    grad_middle = cot_rows.astype(f32) + norm_back(grad_act_m * gain_mlp, normed_m, inv_m)
    grad_mid_bf = grad_middle.astype(bf16)
    grad_out = rows_contract(grad_mid_bf, mixed)
    grad_mixed = jnp.dot(grad_mid_bf, out_full, preferred_element_type=f32).astype(bf16)
    grad_heads = grad_mixed.reshape(tok_rows, head_count, head_size)
    delta_rows = jnp.sum(
        grad_heads.astype(f32) * mixed.reshape(tok_rows, head_count, head_size).astype(f32), axis=-1
    )
    delta = delta_rows.T
    zeros_heads = jnp.zeros((tok_rows, head_count, head_size), f32)
    query_key_piece = lax.all_gather(key_send, "ctx", axis=0, tiled=True)
    query_value_piece = lax.all_gather(value_send, "ctx", axis=0, tiled=True)
    length = query_key_piece.shape[0]
    query_step_len = math.gcd(length, 1024)

    def query_grad_block(block_num, grad_query):
        key_blk = lax.dynamic_slice_in_dim(
            query_key_piece, block_num * query_step_len, query_step_len, 0
        ).reshape(query_step_len, head_count, head_size)
        value_blk = lax.dynamic_slice_in_dim(
            query_value_piece, block_num * query_step_len, query_step_len, 0
        ).reshape(query_step_len, head_count, head_size)
        scores = (
            jnp.einsum("qhd,khd->hqk", query_heads, key_blk, preferred_element_type=f32) * scale
        )
        probs = jnp.exp(scores - log_sum[..., None])
        grad_probs = jnp.einsum("qhd,khd->hqk", grad_heads, value_blk, preferred_element_type=f32)
        grad_scores = (probs * (grad_probs - delta[..., None])).astype(bf16)
        return (
            grad_query
            + jnp.einsum("hqk,khd->qhd", grad_scores, key_blk, preferred_element_type=f32) * scale
        )

    grad_query = lax.fori_loop(0, length // query_step_len, query_grad_block, zeros_heads)
    query_send = query_heads.reshape(tok_rows, width).astype(f32)
    grad_send = grad_mixed.astype(f32)
    query_piece = lax.all_gather(query_send, "ctx", axis=0, tiled=True)
    grad_piece = lax.all_gather(grad_send, "ctx", axis=0, tiled=True)
    log_piece = lax.all_gather(log_sum.T, "ctx", axis=0, tiled=True)
    delta_piece = lax.all_gather(delta_rows, "ctx", axis=0, tiled=True)
    length = query_piece.shape[0]
    key_step_len = math.gcd(length, 1024)

    def key_grad_block(block_num, running):
        grad_keys, grad_values = running
        query_blk = (
            lax.dynamic_slice_in_dim(query_piece, block_num * key_step_len, key_step_len, 0)
            .astype(bf16)
            .reshape(key_step_len, head_count, head_size)
        )
        grad_blk = (
            lax.dynamic_slice_in_dim(grad_piece, block_num * key_step_len, key_step_len, 0)
            .astype(bf16)
            .reshape(key_step_len, head_count, head_size)
        )
        log_blk = lax.dynamic_slice_in_dim(log_piece, block_num * key_step_len, key_step_len, 0).T
        delta_blk = lax.dynamic_slice_in_dim(
            delta_piece, block_num * key_step_len, key_step_len, 0
        ).T
        scores = (
            jnp.einsum("qhd,khd->hqk", query_blk, key_heads, preferred_element_type=f32) * scale
        )
        probs = jnp.exp(scores - log_blk[..., None])
        grad_values = grad_values + jnp.einsum(
            "hqk,qhd->khd", probs.astype(bf16), grad_blk, preferred_element_type=f32
        )
        grad_probs = jnp.einsum("qhd,khd->hqk", grad_blk, value_heads, preferred_element_type=f32)
        grad_scores = (probs * (grad_probs - delta_blk[..., None])).astype(bf16)
        grad_keys = (
            grad_keys
            + jnp.einsum("hqk,qhd->khd", grad_scores, query_blk, preferred_element_type=f32) * scale
        )
        return (grad_keys, grad_values)

    grad_keys, grad_values = lax.fori_loop(
        0, length // key_step_len, key_grad_block, (zeros_heads, zeros_heads)
    )
    grad_query = rotate_back(grad_query, cos_table, sine_table)
    grad_keys = rotate_back(grad_keys, cos_table, sine_table)
    grad_packed = jnp.concatenate(
        [
            grad_query.reshape(tok_rows, width),
            grad_keys.reshape(tok_rows, width),
            grad_values.reshape(tok_rows, width),
        ],
        axis=1,
    ).astype(bf16)
    grad_qkv = rows_contract(grad_packed, act_a)
    grad_act_a = jnp.dot(grad_packed, qkv_full, preferred_element_type=f32)
    grad_gain_a = jnp.sum(grad_act_a * normed_a, axis=0)
    grad_input = grad_middle + norm_back(grad_act_a * gain_attn, normed_a, inv_a)
    owned = (
        lax.psum_scatter(grad_qkv, ("ctx", "fsdp"), scatter_dimension=0, tiled=True),
        lax.psum_scatter(grad_out, ("ctx", "fsdp"), scatter_dimension=0, tiled=True),
        lax.psum_scatter(grad_in, ("ctx", "fsdp"), scatter_dimension=0, tiled=True),
        lax.psum_scatter(grad_down, ("ctx", "fsdp"), scatter_dimension=0, tiled=True),
        lax.psum_scatter(grad_gain_a, ("ctx", "fsdp"), scatter_dimension=0, tiled=True),
        lax.psum_scatter(grad_gain_m, ("ctx", "fsdp"), scatter_dimension=0, tiled=True),
    )
    return (
        output[None],
        grad_input[None],
        owned[0],
        owned[1],
        owned[2],
        owned[3],
        owned[4],
        owned[5],
    )


def solution(mesh):
    return jax.shard_map(
        per_device,
        mesh=mesh,
        in_specs=(
            P("fsdp", "ctx", None),
            P("fsdp", "ctx", None),
            P(),
            P(),
            P("fsdp", None),
            P("fsdp", None),
            P("fsdp", None),
            P("fsdp", None),
        ),
        out_specs=(
            P("fsdp", "ctx", None),
            P("fsdp", "ctx", None),
            P(("ctx", "fsdp"), None),
            P(("ctx", "fsdp"), None),
            P(("ctx", "fsdp"), None),
            P(("ctx", "fsdp"), None),
            P(("ctx", "fsdp")),
            P(("ctx", "fsdp")),
        ),
        check_vma=False,
    )
```

profile of v0, /device:TPU:0, one launch (start us, length us, event | category | flops | bytes accessed | tf_op | source)
XLA Modules:
  0.0 1277.4 jit_solution(7228493947482920155)
XLA Ops:
  9.6 83.1 %all-gather.9.cloned.1.call-done = bf16[3072,1024]{1,0:T(8,128)(2,1)} async-done(((bf16[1536,1024]{1,0:T(8,128)(2,1)}), bf16[3072,1024]{1,0:T(8,128)(2,1)}) %all-gather.9.cloned.1.call-update) | async-done | bytes 6291472 | tf_op jit(solution)/shard_map/all_gather | solution.py:76
  109.2 47.2 %all-gather.11.cloned.1.call-done = bf16[2048,1024]{1,0:T(8,128)(2,1)} async-done(((bf16[128,1024]{1,0:T(8,128)(2,1)}), bf16[2048,1024]{1,0:T(8,128)(2,1)}) %all-gather.11.cloned.1.call-update) | async-done | bytes 4194320 | tf_op jit(solution)/shard_map/all_gather | solution.py:107
  162.9 44.6 %all-gather.13.cloned.1.call-done = bf16[2048,1024]{1,0:T(8,128)(2,1)} async-done(((bf16[128,1024]{1,0:T(8,128)(2,1)}), bf16[2048,1024]{1,0:T(8,128)(2,1)}) %all-gather.13.cloned.1.call-update) | async-done | bytes 4194320 | tf_op jit(solution)/shard_map/all_gather | solution.py:108
  207.5 6.5 copy.64
  214.0 29.9 %while.48 = (s32[]{:T(128)}, f32[128,16,64]{0,2,1:T(8,128)S(1)}, f32[16,128]{1,0:T(8,128)S(1)}, f32[16,128]{1,0:T(8,128)S(1)}, bf16[2048,1024]{0,1:T(8,128)(2,1)...) while((s32[]{:T(128)}, f32[128,16,64]{0,2,1:T(8,128)S(1)}, ...), condition=%wide.region_5.0_spmd.clone, body=%wide.region_2.0_spmd.clone.sunk | while | flops 554053632 | bytes 72745168 | solution.py:132
  246.8 127.6 %all-gather.17.cloned.1.call-done = bf16[5248,1024]{1,0:T(8,128)(2,1)} async-done(((bf16[2624,1024]{1,0:T(8,128)(2,1)}), bf16[5248,1024]{1,0:T(8,128)(2,1)}) %all-gather.17.cloned.1.call-update) | async-done | bytes 10747920 | tf_op jit(solution)/shard_map/all_gather | solution.py:78
  374.4 9.3 fusion.87
  383.7 62.2 %all-gather.19.cloned.1.call-done = bf16[1024,2624]{0,1:T(8,128)(2,1)} async-done(((bf16[512,2624]{0,1:T(8,128)(2,1)}), bf16[1024,2624]{0,1:T(8,128)(2,1)}) %all-gather.19.cloned.1.call-update) | async-done | bytes 5373968 | tf_op jit(solution)/shard_map/all_gather | solution.py:79
  451.2 7.2 multiply_reduce_fusion
  462.7 7.7 convolution_bitcast_fusion
  470.4 12.1 copy.78
  485.7 21.9 %all_gather.39 = f32[2048,16]{0,1:T(8,128)S(1)} all-gather(f32[128,16]{0,1:T(8,128)S(1)} %bitcast.218), channel_id=1, replica_groups=mesh['ctx'=16,'fsdp'=2] {'ctx'}, dimensions={0}, use_global_device_ids=true | all-gather | bytes 139264 | tf_op jit(solution)/shard_map/all_gather | solution.py:189
  508.6 18.3 %all_gather.41 = f32[2048,16]{0,1:T(8,128)S(1)} all-gather(f32[128,16]{0,1:T(8,128)S(1)} %multiply_reduce_fusion.1), channel_id=1, replica_groups=mesh['ctx'=16,'fsdp'=2] {'ctx'}, dimensions={0}, use_global_device_ids=true | all-gather | bytes 139264 | tf_op jit(solution)/shard_map/all_gather | solution.py:190
  527.0 33.3 %while.49 = (s32[]{:T(128)}, f32[128,16,64]{0,2,1:T(8,128)}, bf16[2048,1024]{0,1:T(8,128)(2,1)}, bf16[128,16,64]{0,2,1:T(8,128)(2,1)S(1)}, f32[16,128]{1,0:T(8,1...) while((s32[]{:T(128)}, f32[128,16,64]{0,2,1:T(8,128)}, ...), condition=%wide.region_12.0_spmd.clone, body=%wide.region_11.0_spmd.clone.sunk | while | flops 816185344 | bytes 33079508 | solution.py:184
  535.7 8.0 fusion.157
  552.3 8.0 fusion.157
  560.3 73.2 %while.50 = (s32[]{:T(128)}, f32[128,16,64]{0,2,1:T(8,128)}, f32[128,16,64]{0,2,1:T(8,128)S(1)}, bf16[2048,1024]{1,0:T(8,128)(2,1)}, bf16[128,16,64]{0,2,1:T(8,1...) while((s32[]{:T(128)}, f32[128,16,64]{0,2,1:T(8,128)}, ...), condition=%wide.region_14.0_spmd.clone, body=%wide.region_13.0_spmd.clone.sunk | while | flops 1091174400 | bytes 53412036 | solution.py:225
  584.9 10.8 fusion.166
  617.3 10.8 fusion.166
  644.2 9.2 fusion.50
  653.4 548.9 %fusion = f32[168,1024]{1,0:T(8,128)} fusion(f32[5248,1024]{1,0:T(8,128)} %fusion.50), kind=kCustom, calls=%all-reduce-scatter | all-reduce-scatter fusion | flops 5505025 | bytes 22183936
  1204.1 7.4 collective-permute-start
  1216.0 6.9 collective-permute-done
  1231.0 37.4 %all-reduce.4 = (f32[1024]{0:T(1024)S(1)}, f32[1024]{0:T(1024)S(1)}) all-reduce(f32[1024]{0:T(1024)S(1)} %get-tuple-element.613, f32[1024]{0:T(1024)S(1)} %copy-done.43), channel_id=6, replica_groups=mesh['ctx'=16,'fsdp'=2] {'ctx','fsdp'}, use_global_device_ids=true, to_apply=%region_22.0.clone | all-reduce | flops 2048 | bytes 16384
  (208 shorter events, 158.8 us)
Async XLA Ops:
  7.2 85.5 %copy-start.29 = (f32[1024]{0:T(1024)S(1)}, f32[1024]{0:T(1024)}, u32[]{:S(2)}) copy-start(f32[1024]{0:T(1024)} %param.16) | copy-start | bytes 12292
  7.2 85.5 %all-gather.9.cloned.1.call-start = ((), (), s32[]{:S(2)}) async-start(), calls=%async_computation.3 | async-start | bytes 9437184 | tf_op jit(solution)/shard_map/all_gather | solution.py:76
  7.9 148.5 %all-gather.11.cloned.1.call-start = ((), (), s32[]{:S(2)}) async-start(), calls=%async_computation.4 | async-start | bytes 4456448 | tf_op jit(solution)/shard_map/all_gather | solution.py:107
  8.2 92.0 %copy-start.25 = (f32[128,64]{0,1:T(8,128)}, f32[128,64]{0,1:T(8,128)S(1)}, u32[]{:S(2)}) copy-start(f32[128,64]{0,1:T(8,128)S(1)} %get-tuple-element.704) | copy-start | bytes 98308
  8.2 92.0 %copy-start.27 = (f32[128,64]{0,1:T(8,128)}, f32[128,64]{0,1:T(8,128)S(1)}, u32[]{:S(2)}) copy-start(f32[128,64]{0,1:T(8,128)S(1)} %get-tuple-element.703) | copy-start | bytes 98308
  9.3 88.3 %copy-start.35 = (f32[128]{0:T(128)}, f32[128]{0:T(128)S(1)}, u32[]{:S(2)}) copy-start(f32[128]{0:T(128)S(1)} %broadcast_multiply_fusion.8) | copy-start | bytes 1540
  9.6 88.1 %copy-start.37 = (f32[128]{0:T(128)}, f32[128]{0:T(128)S(1)}, u32[]{:S(2)}) copy-start(f32[128]{0:T(128)S(1)} %add_rsqrt_fusion.1) | copy-start | bytes 1540
  105.9 101.7 %all-gather.13.cloned.1.call-start = ((), (), s32[]{:S(2)}) async-start(), calls=%async_computation.5 | async-start | bytes 4456448 | tf_op jit(solution)/shard_map/all_gather | solution.py:108
  106.7 137.4 %all-gather.15.cloned.1.call-start = ((), (), s32[]{:S(2)}) async-start(), calls=%async_computation.6 | async-start | bytes 3145728 | tf_op jit(solution)/shard_map/all_gather | solution.py:77
  107.2 267.2 %all-gather.17.cloned.1.call-start = ((), (), s32[]{:S(2)}) async-start(), calls=%async_computation.7 | async-start | bytes 16121856 | tf_op jit(solution)/shard_map/all_gather | solution.py:78
  107.8 338.0 %all-gather.19.cloned.1.call-start = ((), (), s32[]{:S(2)}) async-start(), calls=%async_computation.8 | async-start | bytes 8060928 | tf_op jit(solution)/shard_map/all_gather | solution.py:79
  108.4 451.9 %all-gather.21.cloned.1.call-start = ((), (), s32[]{:S(2)}) async-start(), calls=%async_computation.9 | async-start | bytes 4456448 | tf_op jit(solution)/shard_map/all_gather | solution.py:187
  109.2 451.1 %all-gather.23.cloned.1.call-start = ((), (), s32[]{:S(2)}) async-start(), calls=%async_computation.10 | async-start | bytes 4456448 | tf_op jit(solution)/shard_map/all_gather | solution.py:188
  243.9 130.5 %copy-start.31 = (f32[1024]{0:T(1024)S(1)}, f32[1024]{0:T(1024)}, u32[]{:S(2)}) copy-start(f32[1024]{0:T(1024)} %param.17) | copy-start | bytes 12292
  246.5 211.9 %copy-start.1 = (f32[128,1024]{1,0:T(8,128)}, f32[128,1024]{1,0:T(8,128)S(1)}, u32[]{:S(2)}) copy-start(f32[128,1024]{1,0:T(8,128)S(1)} %get-tuple-element.706) | copy-start | bytes 1572868
  246.6 211.8 %copy-start.39 = (f32[128]{0:T(128)}, f32[128]{0:T(128)S(1)}, u32[]{:S(2)}) copy-start(f32[128]{0:T(128)S(1)} %broadcast_multiply_fusion.7) | copy-start | bytes 1540
  246.8 211.6 %copy-start.41 = (f32[128]{0:T(128)}, f32[128]{0:T(128)S(1)}, u32[]{:S(2)}) copy-start(f32[128]{0:T(128)S(1)} %add_rsqrt_fusion) | copy-start | bytes 1540
  246.8 199.1 %copy-start.20 = (bf16[1,128,1024]{2,1,0:T(8,128)(2,1)S(1)}, bf16[1,128,1024]{2,1,0:T(8,128)(2,1)}, u32[]{:S(2)}) copy-start(bf16[1,128,1024]{2,1,0:T(8,128)(2,1)} %param.15) | copy-start | bytes 786436
  459.9 810.8 %reduce-scatter.10.cloned.1.call-start = ((), (), s32[]{:S(2)}) async-start(), calls=%async_computation.12 | async-start | bytes 4325376 | tf_op jit(solution)/shard_map/reduce_scatter | solution.py:244
  462.7 808.0 %reduce-scatter.12.cloned.1.call-start = ((), (), s32[]{:S(2)}) async-start(), calls=%async_computation.13 | async-start | bytes 11354112
  482.5 788.2 %reduce-scatter.8.cloned.1.call-start = ((), (), s32[]{:S(2)}) async-start(), calls=%async_computation.11 | async-start | bytes 12976128 | tf_op jit(solution)/shard_map/reduce_scatter | solution.py:243
  560.3 73.3 %copy-start.28 = (f32[128,64]{0,1:T(8,128)S(1)}, f32[128,64]{0,1:T(8,128)}, u32[]{:S(2)}) copy-start(f32[128,64]{0,1:T(8,128)} %copy-done.27) | copy-start | bytes 98308
  653.4 558.2 %copy-start.3 = (f32[128,5248]{1,0:T(8,128)S(1)}, f32[128,5248]{1,0:T(8,128)}, u32[]{:S(2)}) copy-start(f32[128,5248]{1,0:T(8,128)} %fusion.87) | copy-start | bytes 8060932
  1204.1 18.8 %collective-permute-start = (f32[124,1024]{1,0:T(8,128)}, f32[124,1024]{1,0:T(8,128)}, u32[]{:S(2)}, u32[]{:S(2)}) collective-permute-start(f32[124,1024]{1,0:T(8,128)} %slice.67), channel_id=1, source_target_pairs={{0,1},{1,2},{2,3},{3,4},{4,5},{5,6},{6,7},{7,8},{8,9},{9,10},{10,1... | collective-permute-start | bytes 1523720
  (34 other events, 186.4 us)
Sparse Core Ops, SparseCore 0:
  9.5 83.0 all-gather.8
  106.0 50.3 all-gather.10
  158.6 48.9 all-gather.12
  208.9 31.6 all-gather.14
  242.0 132.4 all-gather.16
  375.8 70.0 all-gather.18
  448.0 50.7 all-gather.20
  501.0 49.2 all-gather.22
  553.2 161.7 reduce-scatter.9
  721.4 178.7 reduce-scatter.11
  906.9 197.6 reduce-scatter.7
where the time goes:
time: 1290 us; the launch traced here: 1280 us
  blocking collectives  627 us (49%)
  waiting for transfers between devices  375 us (29%)
  matrix products  152 us (12%)
  local copies, waits for them, and re-layouts  81.8 us (6%)
  between operations  14.7 us (1%)
    unnamed x2, blocking collectives  586 us
    all_gather x1, waiting for transfers between devices, per_device(): lax.all_gather(in_weight, 'fsdp', axis=0, tiled=True)  128 us
    all_gather x1, waiting for transfers between devices, per_device(): lax.all_gather(qkv_weight, 'fsdp', axis=0, tiled=True)  83.1 us
    all_gather x1, waiting for transfers between devices, per_device(): lax.all_gather(down_weight, 'fsdp', axis=0, tiled=True)  62.2 us
    all_gather x1, waiting for transfers between devices, per_device(): key_piece = lax.all_gather(key_send, 'ctx', axis=0, tiled=True)  47.2 us
    all_gather x1, waiting for transfers between devices, per_device(): value_piece = lax.all_gather(value_send, 'ctx', axis=0, tiled=True)  44.6 us
    unnamed x92, local copies, waits for them, and re-layouts  36 us
    dot_general x4, matrix products, rows_contract(): lax.dot_general(left, right, (((0,), (0,)), ((), ())), preferred_element_...  26 us
  transfers between devices with their start and end apart: 12, of which 6 were waited for; matrix products, arithmetic and copies ran while one was open for 61% of the time, Pallas kernels for 0%

commit v1 on v0

--- a/solution.py
+++ b/solution.py
@@ -1,8 +1,11 @@
+import functools
 import math
 
 import jax
 import jax.numpy as jnp
 from jax import lax
+from jax.experimental import pallas as pl
+from jax.experimental.pallas import tpu as pltpu
 from jax.sharding import PartitionSpec as P
 
 HEAD_DIM = 64
@@ -67,7 +70,7 @@
     )
 
 
-def per_device(
+def gathered_layer(
     tokens, cotangent, gain_attn, gain_mlp, qkv_weight, out_weight, in_weight, down_weight
 ):
     f32 = jnp.float32
@@ -259,9 +262,789 @@
     )
 
 
+MESH = pl.DeviceIdType.MESH
+VMEM_LIMIT = 60 * 1024 * 1024
+
+
+def matmul(left, right, left_dim, right_dim):
+    return lax.dot_general(
+        left, right, (((left_dim,), (right_dim,)), ((), ())), preferred_element_type=jnp.float32
+    )
+
+
+class Place:
+    def __init__(self, count):
+        self.count, self.line = count, count // 4
+        self.me = lax.axis_index("ctx")
+        self.z, self.x, self.core = self.me // 4, self.me // 2 % 2, self.me % 2
+
+    def slot(self, z, x, core):
+        return z * 4 + x * 2 + core
+
+    def far(self, step):
+        last = self.line - 1
+        low = 2 * self.z < self.line
+        own = jnp.where(low, self.z, last - self.z)
+        at = jnp.where(
+            step < last - own, last - step, jnp.where(step == last, own, step - (last - own))
+        )
+        return jnp.where(low, at, last - at)
+
+    def near(self, step):
+        return self.far(self.line - 1 - step)
+
+    def meet(self):
+        barrier = pltpu.get_barrier_semaphore()
+
+        @pl.loop(1, self.count)
+        def _(shift):
+            pl.semaphore_signal(
+                barrier, inc=1, device_id={"ctx": (self.me + shift) % self.count}, device_id_type=MESH
+            )
+
+        pl.semaphore_wait(barrier, self.count - 1)
+
+    def copy(self, src, dst, send, recv, to):
+        return pltpu.make_async_remote_copy(
+            src_ref=src, dst_ref=dst, send_sem=send, recv_sem=recv,
+            device_id={"ctx": to}, device_id_type=MESH,
+        )
+
+
+class Gather:
+    def __init__(self, place, buf, sems):
+        self.p, self.buf = place, buf
+        self.up_s, self.up_r, self.dn_s, self.dn_r, self.x_s, self.x_r, self.c_s, self.c_r = sems
+
+    @staticmethod
+    def sems(line):
+        return [pltpu.SemaphoreType.DMA((line,))] * 6 + [pltpu.SemaphoreType.DMA((2 * line,))] * 2
+
+    def over(self, z, x, core, send, recv, to):
+        at = self.buf.at[self.p.slot(z, x, core)]
+        return self.p.copy(at, at, send, recv, to)
+
+    def up(self, z):
+        p = self.p
+        return self.over(z, p.x, p.core, self.up_s.at[z], self.up_r.at[z], (p.me + 4) % p.count)
+
+    def down(self, z):
+        p = self.p
+        return self.over(z, p.x, p.core, self.dn_s.at[z], self.dn_r.at[z], (p.me + p.count - 4) % p.count)
+
+    def across(self, z):
+        p = self.p
+        return self.over(z, p.x, p.core, self.x_s.at[z], self.x_r.at[z], p.slot(p.z, 1 - p.x, p.core))
+
+    def beside(self, z, x):
+        p = self.p
+        at = z * 2 + x
+        return self.over(z, x, p.core, self.c_s.at[at], self.c_r.at[at], p.slot(p.z, p.x, 1 - p.core))
+
+    def arrive(self, z):
+        p = self.p
+
+        @pl.when(z < p.z)
+        def _():
+            self.up(z).wait_recv()
+
+        @pl.when(z > p.z)
+        def _():
+            self.down(z).wait_recv()
+
+        @pl.when((z <= p.z) & (p.z < p.line - 1))
+        def _():
+            self.up(z).start()
+
+        @pl.when((z >= p.z) & (p.z > 0))
+        def _():
+            self.down(z).start()
+
+        self.across(z).start()
+        self.beside(z, p.x).start()
+
+    def arrive_across(self, z):
+        self.across(z).wait_recv()
+        self.beside(z, 1 - self.p.x).start()
+
+    def part(self, turn, use=None):
+        p = self.p
+        step, part = turn // 4, turn % 4
+        z = jnp.where(part == 0, p.near(step), p.near(step - 1))
+
+        @pl.when(jnp.where(part == 0, step < p.line, step > 0))
+        def _():
+            @pl.when(part == 0)
+            def _():
+                self.arrive(z)
+
+            @pl.when(part == 1)
+            def _():
+                self.arrive_across(z)
+
+            x = jnp.where(part % 2 == 0, p.x, 1 - p.x)
+
+            @pl.when(part >= 2)
+            def _():
+                self.beside(z, x).wait_recv()
+
+            if use is not None:
+                use(z, x, jnp.where(part < 2, p.core, 1 - p.core))
+
+    def sent(self):
+        p = self.p
+
+        @pl.loop(0, p.line)
+        def _(z):
+            @pl.when((z <= p.z) & (p.z < p.line - 1))
+            def _():
+                self.up(z).wait_send()
+
+            @pl.when((z >= p.z) & (p.z > 0))
+            def _():
+                self.down(z).wait_send()
+
+            self.across(z).wait_send()
+            self.beside(z, 0).wait_send()
+            self.beside(z, 1).wait_send()
+
+
+class Halve:
+    def __init__(self, place, whole, got, sums, sems):
+        self.p, self.whole, self.got, self.sums = place, whole, got, sums
+        self.c_s, self.c_r = sems
+
+    @staticmethod
+    def sems(line):
+        return [pltpu.SemaphoreType.DMA((2 * line,))] * 2
+
+    def beside(self, z, x):
+        p, at = self.p, z * 2 + x
+        return p.copy(
+            self.whole.at[p.slot(z, x, 1 - p.core)], self.got.at[at], self.c_s.at[at], self.c_r.at[at],
+            p.slot(p.z, p.x, 1 - p.core),
+        )
+
+    def add(self, z):
+        p = self.p
+        for x in range(2):
+            at = z * 2 + x
+            self.beside(z, x).wait_recv()
+            self.sums[at] = (
+                self.whole[p.slot(z, x, p.core)].astype(jnp.float32) + self.got[at].astype(jnp.float32)
+            ).astype(self.sums.dtype)
+
+    def sent(self):
+        @pl.loop(0, 2 * self.p.line)
+        def _(at):
+            self.beside(at // 2, at % 2).wait_send()
+
+
+class Settle:
+    def __init__(self, place, sums, bufs, sems):
+        self.p, self.sums = place, sums
+        self.got, self.total, self.low, self.high = bufs
+        self.x_s, self.x_r, self.up_s, self.up_r, self.dn_s, self.dn_r = sems
+
+    @staticmethod
+    def sems(line):
+        return [pltpu.SemaphoreType.DMA((line,))] * 6
+
+    @staticmethod
+    def bufs(line, block):
+        return [pltpu.VMEM((line,) + block, jnp.bfloat16)] * 4
+
+    def across(self, z):
+        p = self.p
+        return p.copy(
+            self.sums.at[z * 2 + 1 - p.x], self.got.at[z], self.x_s.at[z], self.x_r.at[z],
+            p.slot(p.z, 1 - p.x, p.core),
+        )
+
+    def up(self, z):
+        p = self.p
+        return p.copy(self.total.at[z], self.low.at[z], self.up_s.at[z], self.up_r.at[z], (p.me + 4) % p.count)
+
+    def down(self, z):
+        p = self.p
+        return p.copy(
+            self.total.at[z], self.high.at[z], self.dn_s.at[z], self.dn_r.at[z], (p.me + p.count - 4) % p.count
+        )
+
+    def pass_on(self, z):
+        p, f32 = self.p, jnp.float32
+        self.across(z).wait_recv()
+        self.total[z] = (
+            self.sums[z * 2 + p.x].astype(f32) + self.got[z].astype(f32)
+        ).astype(self.total.dtype)
+
+        @pl.when(z > p.z)
+        def _():
+            @pl.when(p.z > 0)
+            def _():
+                self.up(z).wait_recv()
+                self.total[z] = (self.total[z].astype(f32) + self.low[z].astype(f32)).astype(self.total.dtype)
+
+            self.up(z).start()
+
+        @pl.when(z < p.z)
+        def _():
+            @pl.when(p.z < p.line - 1)
+            def _():
+                self.down(z).wait_recv()
+                self.total[z] = (self.total[z].astype(f32) + self.high[z].astype(f32)).astype(self.total.dtype)
+
+            self.down(z).start()
+
+    def finish(self, out):
+        p, f32 = self.p, jnp.float32
+        out[...] = self.total[p.z].astype(f32)
+
+        @pl.when(p.z > 0)
+        def _():
+            self.up(p.z).wait_recv()
+            out[...] += self.low[p.z].astype(f32)
+
+        @pl.when(p.z < p.line - 1)
+        def _():
+            self.down(p.z).wait_recv()
+            out[...] += self.high[p.z].astype(f32)
+
+    def sent(self):
+        p = self.p
+
+        @pl.loop(0, p.line)
+        def _(z):
+            self.across(z).wait_send()
+
+            @pl.when(z > p.z)
+            def _():
+                self.up(z).wait_send()
+
+            @pl.when(z < p.z)
+            def _():
+                self.down(z).wait_send()
+
+
+class Exchange:
+    def __init__(self, place, src, dst, sems):
+        self.p, self.src, self.dst = place, src, dst
+        self.s, self.r = sems
+
+    @staticmethod
+    def sems(count):
+        return [pltpu.SemaphoreType.DMA((count,))] * 2
+
+    def to(self, j):
+        return self.p.copy(self.src.at[j], self.dst.at[self.p.me], self.s.at[j], self.r.at[self.p.me], j)
+
+    def send(self, j):
+        @pl.when(j != self.p.me)
+        def _():
+            self.to(j).start()
+
+        @pl.when(j == self.p.me)
+        def _():
+            self.dst[j] = self.src[j]
+
+    def arrived(self):
+        p = self.p
+
+        @pl.loop(1, p.count)
+        def _(shift):
+            j = (p.me + shift) % p.count
+            p.copy(self.src.at[j], self.dst.at[j], self.s.at[j], self.r.at[j], j).wait_recv()
+
+    def sent(self):
+        p = self.p
+
+        @pl.loop(1, p.count)
+        def _(shift):
+            self.to((p.me + shift) % p.count).wait_send()
+
+
+def turn(value):
+    half = value.shape[0] // 2
+    return jnp.concatenate([-value[half:], value[:half]], axis=0)
+
+
+def turn_back(value):
+    half = value.shape[0] // 2
+    return jnp.concatenate([value[half:], -value[:half]], axis=0)
+
+
+def attend_kernel(
+    count, act, cot, weight, cos, sine,
+    act_all, cot_all, query_t, keys_t, keys, values, mixed_own, log_sum, mixed,
+    values_t, load_sem, *sems
+):
+    f32, bf16 = jnp.float32, jnp.bfloat16
+    p = Place(count)
+    rows, head = act.shape[0], keys_t.shape[0]
+    n = 8
+    first = Gather(p, act_all, sems[:n])
+    second = Gather(p, cot_all, sems[n : 2 * n])
+    trade = Exchange(p, mixed_own, mixed, sems[2 * n :])
+    loads = [
+        pltpu.make_async_copy(act, act_all.at[p.me], load_sem.at[0]),
+        pltpu.make_async_copy(cot, cot_all.at[p.me], load_sem.at[1]),
+    ]
+    for load in loads:
+        load.start()
+    p.meet()
+    for load in loads:
+        load.wait()
+
+    def project(z, x, core):
+        at = p.slot(z, x, core)
+        lanes = pl.ds(pl.multiple_of(at * rows, rows), rows)
+        packed = matmul(weight[...], act_all[at], 1, 1)
+        c, s = cos[:, lanes], sine[:, lanes]
+        query, key = packed[:head], packed[head : 2 * head]
+        query_t[:, lanes] = (query * c + turn(query) * s).astype(bf16)
+        key = key * c + turn(key) * s
+        keys_t[:, lanes] = key.astype(bf16)
+        values_t[:, lanes] = packed[2 * head :].astype(bf16)
+        keys[lanes, :] = key.T.astype(bf16)
+        values[lanes, :] = packed[2 * head :].T.astype(bf16)
+
+    @pl.loop(0, 4 * p.line + 4)
+    def _(at):
+        first.part(at, project)
+
+    def gather_more(step):
+        for part in range(4):
+            second.part(step * 4 + part)
+
+    gather_more(0)
+    wide = 2 * rows
+    blocks = count // 2
+    scale = head ** (-0.5)
+
+    def attend(i):
+        block = (p.me // 2 + i) % blocks
+        lanes = pl.ds(pl.multiple_of(block * wide, wide), wide)
+        scores = matmul(keys[...], query_t[:, lanes], 1, 0) * scale
+        top = jnp.max(scores, axis=0, keepdims=True)
+        weights = jnp.exp(scores - top)
+        total = jnp.sum(weights, axis=0, keepdims=True)
+        log_sum[:, lanes] = top + jnp.log(total)
+        out = (matmul(values_t[...], weights.astype(bf16), 1, 0) / total).astype(bf16)
+        mixed_own[2 * block] = out[:, :rows]
+        mixed_own[2 * block + 1] = out[:, rows:]
+        trade.send(2 * block)
+        trade.send(2 * block + 1)
+
+    @pl.loop(0, blocks // 2)
+    def _(i):
+        attend(i)
+
+    gather_more(1)
+
+    @pl.loop(blocks // 2, blocks)
+    def _(i):
+        attend(i)
+
+    for step in range(2, p.line):
+        gather_more(step)
+    trade.arrived()
+    gather_more(p.line)
+    first.sent()
+    second.sent()
+    trade.sent()
+
+
+def feed_kernel(
+    count, act, cot_all, weight, down,
+    grad_act, out_sums, grad_weight, grad_down,
+    act_all, gated, inner_grad, grad_part, out_part, grad_got, grad_sums, out_got, load_sem, *rest
+):
+    f32, bf16 = jnp.float32, jnp.bfloat16
+    p = Place(count)
+    rows, group = act.shape[0], down.shape[1]
+    bufs, sems = rest[:4], rest[4:]
+    gather = Gather(p, act_all, sems[:8])
+    halve = Halve(p, grad_part, grad_got, grad_sums, sems[8:10])
+    settle = Settle(p, grad_sums, bufs, sems[10:16])
+    halve_out = Halve(p, out_part, out_got, out_sums, sems[16:18])
+    load = pltpu.make_async_copy(act, act_all.at[p.me], load_sem)
+    load.start()
+    p.meet()
+    load.wait()
+
+    def feed(z, x, core):
+        at = p.slot(z, x, core)
+        inner = matmul(act_all[at], weight[...], 1, 1)
+        grad_gated = matmul(cot_all[at], down[...], 1, 0)
+        value, gate = inner[:, :group], inner[:, group:]
+        gelu_val, gelu_slope = gelu_pair(value)
+        token = pl.ds(pl.multiple_of(at * rows, rows), rows)
+        out = (gelu_val * gate).astype(bf16)
+        gated[token, :] = out
+        grads = jnp.concatenate(
+            [grad_gated * gate * gelu_slope, grad_gated * gelu_val], axis=1
+        ).astype(bf16)
+        inner_grad[token, :] = grads
+        grad_part[at] = matmul(grads, weight[...], 1, 0).astype(bf16)
+
+        @pl.when(core != p.core)
+        def _():
+            halve.beside(z, x).start()
+
+        out_part[at] = matmul(out, down[...], 1, 1).astype(bf16)
+
+        @pl.when(core != p.core)
+        def _():
+            halve_out.beside(z, x).start()
+
+    @pl.loop(0, 4 * p.line + 4)
+    def _(at):
+        gather.part(at, feed)
+
+    @pl.loop(0, p.line)
+    def _(step):
+        z = p.far(step)
+        halve.add(z)
+        settle.across(z).start()
+
+    def grad_chunk(step):
+        token = pl.ds(pl.multiple_of(step * 4 * rows, 4 * rows), 4 * rows)
+        acts = jnp.concatenate([act_all[4 * step + i] for i in range(4)], axis=0)
+        cots = jnp.concatenate([cot_all[4 * step + i] for i in range(4)], axis=0)
+        return matmul(inner_grad[token, :], acts, 0, 0), matmul(cots, gated[token, :], 0, 0)
+
+    grad_weight[...], grad_down[...] = grad_chunk(0)
+
+    @pl.loop(0, p.line)
+    def _(step):
+        settle.pass_on(p.far(step))
+
+        @pl.when(step > 0)
+        def _():
+            more = grad_chunk(step)
+            grad_weight[...] += more[0]
+            grad_down[...] += more[1]
+
+        halve_out.add(step)
+
+    settle.finish(grad_act)
+    gather.sent()
+    halve.sent()
+    halve_out.sent()
+    settle.sent()
+
+
+def attend_back_kernel(
+    count, grad_mixed, out_sums, query_t, keys_t, keys, values, mixed_own, log_sum, act_all, weight, cos, sine,
+    grad_act, out_total, grad_weight,
+    grad_own, grad_keys, grad_values, grad_packed, grad_part, grad_got, grad_sums, *rest
+):
+    f32, bf16 = jnp.float32, jnp.bfloat16
+    p = Place(count)
+    rows, head = grad_mixed.shape[2], keys_t.shape[0]
+    bufs, out_bufs, sems = rest[:4], rest[4:8], rest[8:]
+    trade = Exchange(p, grad_mixed, grad_own, sems[:2])
+    halve = Halve(p, grad_part, grad_got, grad_sums, sems[2:4])
+    settle = Settle(p, grad_sums, bufs, sems[4:10])
+    settle_out = Settle(p, out_sums, out_bufs, sems[10:16])
+    p.meet()
+
+    @pl.loop(0, count)
+    def _(shift):
+        trade.send((p.me + shift) % count)
+
+    @pl.loop(0, p.line)
+    def _(step):
+        settle_out.across(p.far(step)).start()
+
+    grad_keys[...] = jnp.zeros_like(grad_keys)
+    grad_values[...] = jnp.zeros_like(grad_values)
+    trade.arrived()
+    wide = 2 * rows
+    scale = head ** (-0.5)
+
+    def back(i):
+        lanes = pl.ds(pl.multiple_of(i * wide, wide), wide)
+        query = query_t[:, lanes]
+        grad = jnp.concatenate([grad_own[2 * i], grad_own[2 * i + 1]], axis=1)
+        own = jnp.concatenate([mixed_own[2 * i], mixed_own[2 * i + 1]], axis=1)
+        delta = jnp.sum(grad.astype(f32) * own.astype(f32), axis=0, keepdims=True)
+        scores = matmul(keys[...], query, 1, 0) * scale
+        probs = jnp.exp(scores - log_sum[:, lanes])
+        grad_values[...] += matmul(probs.astype(bf16), grad, 1, 1)
+        grad_probs = matmul(values[...], grad, 1, 0)
+        grad_scores = (probs * (grad_probs - delta)).astype(bf16)
+        grad_keys[...] += matmul(grad_scores, query, 1, 1)
+        grad_query = matmul(keys_t[...], grad_scores, 1, 0) * scale
+        back_query = grad_query * cos[:, lanes] + turn_back(grad_query * sine[:, lanes])
+        grad_packed[:head, lanes] = back_query.astype(bf16)
+
+    @pl.loop(0, count // 2)
+    def _(i):
+        back(i)
+
+    @pl.loop(0, p.line)
+    def _(step):
+        settle_out.pass_on(p.far(step))
+
+    grad_key = grad_keys[...].T * scale
+    grad_packed[head : 2 * head, :] = (grad_key * cos[...] + turn_back(grad_key * sine[...])).astype(bf16)
+    grad_packed[2 * head :, :] = grad_values[...].T.astype(bf16)
+
+    @pl.loop(0, p.line)
+    def _(step):
+        z = p.far(step)
+        for at in range(4):
+            lanes = pl.ds(pl.multiple_of((z * 4 + at) * rows, rows), rows)
+            grad_part[z * 4 + at] = matmul(grad_packed[:, lanes], weight[...], 0, 0).astype(bf16)
+        halve.beside(z, 0).start()
+        halve.beside(z, 1).start()
+
+    @pl.loop(0, p.line)
+    def _(step):
+        z = p.far(step)
+        halve.add(z)
+        settle.across(z).start()
+
+    def grad_chunk(step):
+        lanes = pl.ds(pl.multiple_of(step * 4 * rows, 4 * rows), 4 * rows)
+        acts = jnp.concatenate([act_all[4 * step + i] for i in range(4)], axis=0)
+        return matmul(grad_packed[:, lanes], acts, 1, 0)
+
+    grad_weight[...] = grad_chunk(0)
+
+    @pl.loop(0, p.line)
+    def _(step):
+        settle.pass_on(p.far(step))
+
+        @pl.when(step > 0)
+        def _():
+            grad_weight[...] += grad_chunk(step)
+
+    settle_out.finish(out_total)
+    settle.finish(grad_act)
+    trade.sent()
+    halve.sent()
+    settle.sent()
+    settle_out.sent()
+
+
+def run_kernel(body, outs, scratch, collective, flops, args):
+    vmem = pl.BlockSpec(memory_space=pltpu.VMEM)
+    return pl.pallas_call(
+        body,
+        out_shape=outs,
+        in_specs=[vmem] * len(args),
+        out_specs=[vmem] * len(outs),
+        scratch_shapes=scratch,
+        compiler_params=pltpu.CompilerParams(
+            collective_id=collective, has_side_effects=True, vmem_limit_bytes=VMEM_LIMIT
+        ),
+        cost_estimate=pl.CostEstimate(flops=flops, bytes_accessed=20_000_000, transcendentals=0),
+        name=body.func.__name__,
+    )(*args)
+
+
+def shaped(shape, kind):
+    return jax.ShapeDtypeStruct(shape, kind)
+
+
+def attend(count, act, cot, weight, cos, sine):
+    bf16, f32 = jnp.bfloat16, jnp.float32
+    rows, width = act.shape
+    head, length, line = weight.shape[0] // 3, rows * count, count // 4
+    blocks = shaped((count, rows, width), bf16)
+    tall, flat = shaped((head, length), bf16), shaped((length, head), bf16)
+    heads = shaped((count, head, rows), bf16)
+    return run_kernel(
+        functools.partial(attend_kernel, count),
+        [blocks, blocks, tall, tall, flat, flat, heads, shaped((1, length), f32), heads],
+        [pltpu.VMEM((head, length), bf16), pltpu.SemaphoreType.DMA((2,))]
+        + Gather.sems(line) * 2 + Exchange.sems(count),
+        0, 10_000_000_000, [act, cot, weight, cos, sine],
+    )
+
+
+def feed(count, act, cot_all, weight, down):
+    bf16, f32 = jnp.bfloat16, jnp.float32
+    rows, width = act.shape
+    group, length, line = down.shape[1], rows * count, count // 4
+    block = (rows, width)
+    whole, half = pltpu.VMEM((count,) + block, bf16), pltpu.VMEM((2 * line,) + block, bf16)
+    return run_kernel(
+        functools.partial(feed_kernel, count),
+        [shaped(block, f32), shaped((2 * line,) + block, bf16), shaped(weight.shape, f32), shaped(down.shape, f32)],
+        [whole, pltpu.VMEM((length, group), bf16), pltpu.VMEM((length, 2 * group), bf16), whole, whole,
+         half, half, half, pltpu.SemaphoreType.DMA]
+        + Settle.bufs(line, block)
+        + Gather.sems(line) + Halve.sems(line) + Settle.sems(line) + Halve.sems(line),
+        1, 20_000_000_000, [act, cot_all, weight, down],
+    )
+
+
+def attend_back(count, grad_mixed, out_sums, kept, act_all, weight, cos, sine):
+    bf16, f32 = jnp.bfloat16, jnp.float32
+    rows, width = act_all.shape[1:]
+    head, length, line = weight.shape[0] // 3, rows * count, count // 4
+    block = (rows, width)
+    whole, half = pltpu.VMEM((count,) + block, bf16), pltpu.VMEM((2 * line,) + block, bf16)
+    flat = pltpu.VMEM((length, head), f32)
+    return run_kernel(
+        functools.partial(attend_back_kernel, count),
+        [shaped(block, f32), shaped(block, f32), shaped(weight.shape, f32)],
+        [pltpu.VMEM((count, head, rows), bf16), flat, flat, pltpu.VMEM((3 * head, length), bf16), whole, half, half]
+        + Settle.bufs(line, block) * 2
+        + Exchange.sems(count) + Halve.sems(line) + Settle.sems(line) * 2,
+        2, 20_000_000_000, [grad_mixed, out_sums, *kept, act_all, weight, cos, sine],
+    )
+
+
+def swap_perm(count, stride):
+    return [(i, i + stride if (i // stride) % 2 == 0 else i - stride) for i in range(count)]
+
+
+def line_perm(count, stride, shift):
+    return [(i, (i + shift * stride) % count) for i in range(count)]
+
+
+def pick(cond, first, second):
+    return jnp.where(cond, first, second)
+
+
+def scatter_sum(partial):
+    count = lax.axis_size("ctx")
+    index = lax.axis_index("ctx")
+    line = count // 4
+    line_pos = index // 4
+    f32 = jnp.float32
+    rest = partial.reshape((line, 2, 2) + partial.shape[1:])
+    for stride in (1, 2):
+        axis = 2 if stride == 1 else 1
+        mine = lax.rem(index // stride, 2)
+        keep = lax.dynamic_index_in_dim(rest, mine, axis, keepdims=False)
+        send = lax.dynamic_index_in_dim(rest, 1 - mine, axis, keepdims=False)
+        got = lax.ppermute(send, "ctx", swap_perm(count, stride))
+        rest = (keep.astype(f32) + got.astype(f32)).astype(partial.dtype)
+    total = lax.dynamic_index_in_dim(rest, line_pos, 0, keepdims=False).astype(f32)
+    for shift in range(1, line):
+        send = lax.dynamic_index_in_dim(rest, lax.rem(line_pos + shift, line), 0, keepdims=False)
+        total = total + lax.ppermute(send, "ctx", line_perm(count, 4, shift)).astype(f32)
+    return total
+
+
+def pair_halves(low, high):
+    second = lax.axis_index("fsdp") == 1
+    send = pick(second, low, high)
+    keep = pick(second, high, low)
+    return keep + lax.ppermute(send, "fsdp", [(0, 1), (1, 0)])
+
+
+def pair_rows(mine):
+    other = lax.ppermute(mine, "fsdp", [(0, 1), (1, 0)])
+    second = lax.axis_index("fsdp") == 1
+    return pick(second, other, mine), pick(second, mine, other)
+
+
+def tensor_layer(
+    tokens, cotangent, gain_attn, gain_mlp, qkv_weight, out_weight, in_weight, down_weight
+):
+    f32 = jnp.float32
+    bf16 = jnp.bfloat16
+    count = lax.axis_size("ctx")
+    devices = count * lax.axis_size("fsdp")
+    index = lax.axis_index("ctx")
+    pair = lax.axis_index("fsdp")
+    place = index * 2 + pair
+    rows, width = tokens.shape[1], tokens.shape[2]
+    length = rows * count
+    head_size = width // count
+    hidden = in_weight.shape[0]
+    group = hidden // count
+    padding = -group % 128
+    unit = width // devices
+
+    half_rows = qkv_weight.shape[0]
+
+    def head_rows(part):
+        start = part * width + index * head_size
+        owner = start // half_rows
+        own = lax.dynamic_slice_in_dim(qkv_weight, start - owner * half_rows, head_size, 0)
+        return owner == pair, own
+
+    owned = [head_rows(part) for part in range(3)]
+    got = lax.ppermute(jnp.stack([own for _, own in owned]), "fsdp", [(0, 1), (1, 0)])
+    qkv_head = jnp.concatenate([jnp.where(here, own, got[i]) for i, (here, own) in enumerate(owned)], axis=0)
+    in_mine = lax.dynamic_slice_in_dim(in_weight, index * group, group, 0)
+    in_both = jnp.concatenate([jnp.pad(part, ((0, padding), (0, 0))) for part in pair_rows(in_mine)], axis=0)
+    down_mine = lax.dynamic_slice_in_dim(down_weight, index * group, group, 1)
+    down_cols = jnp.concatenate([jnp.pad(part, ((0, 0), (0, padding))) for part in pair_rows(down_mine)], axis=0)
+    out_full = jnp.concatenate(pair_rows(out_weight), axis=0)
+
+    cos_table, sine_table = rope_tables(0, length, head_size)
+    cos_table, sine_table = cos_table[:, 0].T, sine_table[:, 0].T
+    resid = tokens[0].astype(f32)
+    normed_a, inv_a = normalize(resid)
+    act_a = (normed_a * gain_attn).astype(bf16)
+    cot_rows = cotangent[0]
+    act_all, cot_all, *kept, mixed = attend(count, act_a, cot_rows, qkv_head, cos_table, sine_table)
+    mixed = mixed.reshape(width, rows)
+    middle = resid + matmul(mixed, out_full, 0, 1)
+    normed_m, inv_m = normalize(middle)
+    act_m = (normed_m * gain_mlp).astype(bf16)
+    grad_act_m, out_sums, grad_in_both, grad_down_cols = feed(count, act_m, cot_all, in_both, down_cols)
+
+    grad_middle = cot_rows.astype(f32) + norm_back(grad_act_m * gain_mlp, normed_m, inv_m)
+    grad_mid_bf = grad_middle.astype(bf16)
+    grad_mixed = matmul(out_full, grad_mid_bf, 0, 1).astype(bf16).reshape(count, head_size, rows)
+
+    padded = group + padding
+    grad_in_half = pair_halves(grad_in_both[:group], grad_in_both[padded : padded + group])
+    grad_in = lax.ppermute(
+        grad_in_half,
+        ("ctx", "fsdp"),
+        [(c * 2 + y, y * count + c) for c in range(count) for y in range(2)],
+    )
+    grad_down_cols = grad_down_cols[:, :group].reshape(count, 2, unit, group)
+    grad_down_half = pair_halves(grad_down_cols[:, 0], grad_down_cols[:, 1])
+    grad_down = lax.all_to_all(grad_down_half, "ctx", 0, 0).transpose(1, 0, 2).reshape(unit, hidden)
+    grad_out_part = matmul(grad_mid_bf, mixed, 0, 1).reshape(count, 2, unit, width)
+    grad_out = scatter_sum(pair_halves(grad_out_part[:, 0], grad_out_part[:, 1]).astype(bf16))
+
+    grad_act_a, out_total, grad_qkv_head = attend_back(
+        count, grad_mixed, out_sums, kept, act_all, qkv_head, cos_table, sine_table
+    )
+    output = middle + out_total
+    grad_qkv_head = grad_qkv_head.reshape(3, 2, unit, width)
+    grad_units = pair_halves(grad_qkv_head[:, 0], grad_qkv_head[:, 1])
+    inverse = pow(3, -1, devices)
+    slots = []
+    for slot in range(3):
+        owner = lax.rem((place - slot + devices) * inverse, devices)
+        piece = lax.dynamic_index_in_dim(grad_units, (3 * owner + slot) // devices, 0, keepdims=False)
+        slots.append(
+            lax.ppermute(
+                piece, ("ctx", "fsdp"), [((3 * o + slot) % devices, o) for o in range(devices)]
+            )
+        )
+    grad_qkv = jnp.concatenate(slots, axis=0)
+    grad_gain_m = jnp.sum(grad_act_m * normed_m, axis=0)
+    grad_gain_a = jnp.sum(grad_act_a * normed_a, axis=0)
+    grad_input = grad_middle + norm_back(grad_act_a * gain_attn, normed_a, inv_a)
+    gains = jnp.stack([grad_gain_a, grad_gain_m]).reshape(2, devices, unit).transpose(1, 0, 2)
+    gains = jnp.sum(lax.all_to_all(gains, ("ctx", "fsdp"), 0, 0), axis=0)
+    return (output[None], grad_input[None], grad_qkv, grad_out, grad_in, grad_down, gains[0], gains[1])
+
+
 def solution(mesh):
+
+    def layer(*arrays):
+        one_head_each = arrays[0].shape[2] == HEAD_DIM * mesh.shape["ctx"]
+        if one_head_each and mesh.shape["fsdp"] == 2 and mesh.shape["ctx"] % 4 == 0:
+            return tensor_layer(*arrays)
+        return gathered_layer(*arrays)
+
     return jax.shard_map(
-        per_device,
+        layer,
         mesh=mesh,
         in_specs=(
             P("fsdp", "ctx", None),

time: 1290 us -> 392 us (0.30)
  blocking collectives: 627 us -> 0 us
  waiting for transfers between devices: 375 us -> 55.6 us
  Pallas kernels: 0 us -> 231 us
  matrix products: 152 us -> 3.09 us
  local copies, waits for them, and re-layouts: 81.8 us -> 11 us
  starting transfers between devices: 7.84 us -> 52.5 us
  other arithmetic: 11 us -> 36 us
  between operations: 14.7 us -> 1.29 us
    unnamed x2 -> x0, blocking collectives: 586 us -> none
    all_gather x8 -> x0, waiting for transfers between devices: 365 us -> none  [the longest x1 128 us: per_device(): lax.all_gather(in_weight, 'fsdp', axis=0, tiled=True)]
    pallas_call x0 -> x3, Pallas kernels: none -> 231 us  [run_kernel(): pl.pallas_call(body, out_shape=outs, in_specs=[vmem] * len(args), out_spe...]
    dot_general x26 -> x3, matrix products: 152 us -> 3.09 us  [matmul(): lax.dot_general(left, right, (((left_dim,), (right_dim,)), ((), ())), pre...]
    ppermute x0 -> x17, waiting for transfers between devices: none -> 55.6 us  [the longest x3 35.9 us: pair_rows(): other = lax.ppermute(mine, 'fsdp', [(0, 1), (1, 0)])]
    ppermute x0 -> x17, starting transfers between devices: none -> 44.1 us  [the longest x3 20.5 us: scatter_sum(): lax.ppermute(send, 'ctx', line_perm(count, 4, shift)).astype(f32)]
    all_gather x2 -> x0, blocking collectives: 40.2 us -> none  [the longest x1 21.9 us: per_device(): log_piece = lax.all_gather(log_sum.T, 'ctx', axis=0, tiled=True)]
    dynamic_slice x10 -> x4, local copies, waits for them, and re-layouts: 36.6 us -> 2.05 us  [the longest x1 1.07 us: tensor_layer(): in_mine = lax.dynamic_slice_in_dim(in_weight, index * group, group, 0)]
  transfers between devices with their start and end apart: 12 -> 19, of which waited for: 6 -> 5; matrix products, arithmetic and copies ran while one was open for 61% -> 9% of each run, Pallas kernels for 0% -> 39%
where the time goes in v1:
time: 392 us; the launch traced here: 391 us
  Pallas kernels  231 us (59%)
  waiting for transfers between devices  55.6 us (14%)
  starting transfers between devices  52.5 us (13%)
  other arithmetic  36 us (9%)
  local copies, waits for them, and re-layouts  11 us (3%)
    pallas_call x3, Pallas kernels, run_kernel(): pl.pallas_call(body, out_shape=outs, in_specs=[vmem] * len(args), out_spe...  231 us
    ppermute x3, waiting for transfers between devices, pair_rows(): other = lax.ppermute(mine, 'fsdp', [(0, 1), (1, 0)])  35.9 us
    ppermute x3, starting transfers between devices, scatter_sum(): lax.ppermute(send, 'ctx', line_perm(count, 4, shift)).astype(f32)  20.5 us
    ppermute x2, waiting for transfers between devices, scatter_sum(): got = lax.ppermute(send, 'ctx', swap_perm(count, stride))  11.1 us
    select_n x7, other arithmetic, pick(): return jnp.where(cond, first, second)  8.58 us
    ppermute x4, waiting for transfers between devices, pair_halves(): return keep + lax.ppermute(send, 'fsdp', [(0, 1), (1, 0)])  8.51 us
  transfers between devices with their start and end apart: 19, of which 5 were waited for; matrix products, arithmetic and copies ran while one was open for 9% of the time, Pallas kernels for 39%

profile of v1, /device:TPU:0, one launch (start us, length us, event | category | flops | bytes accessed | tf_op | source)
XLA Modules:
  0.0 390.8 jit_solution(14856560852357759312)
XLA Ops:
  2.0 3.1 collective-permute-start
  5.3 2.0 collective-permute-start.3
  9.2 2.7 fusion.32
  12.8 30.3 %collective-permute-done.3 = bf16[512,164]{1,0:T(8,128)(2,1)S(1)} collective-permute-done((bf16[512,164]{1,0:T(8,128)(2,1)S(1)}, bf16[512,164]{1,0:T(8,128)(2,1)S(1)}, u32[]{:S(2)}, u32[]{:S(2)}) %collective-permute-start.3) | collective-permute-done | bytes 167968 | tf_op jit(solution)/shard_map/ppermute | solution.py:943
  44.1 5.6 %collective-permute-done.2 = bf16[164,1024]{1,0:T(8,128)(2,1)S(1)} collective-permute-done((bf16[164,1024]{1,0:T(8,128)(2,1)S(1)}, bf16[164,1024]{1,0:T(8,128)(2,1)S(1)}, u32[]{:S(2)}, u32[]{:S(2)}) %collective-permute-start.2) | collective-permute-done | bytes 335904 | tf_op jit(solution)/shard_map/ppermute | solution.py:943
  54.1 81.7 %attend_kernel.1 = (bf16[16,128,1024]{2,1,0:T(8,128)(2,1)}, bf16[16,128,1024]{2,1,0:T(8,128)(2,1)}, bf16[64,2048]{1,0:T(8,128)(2,1)}, bf16[64,2048]{1,0:T(8,128)...) custom-call(bf16[128,1024]{1,0:T(8,128)(2,1)} %fusion.20.act, ...), custom_call_target="tpu_custom_call" | custom-call | flops 10000000000 | bytes 20000000 | tf_op jit(solution)/shard_map/attend_kernel/pallas_call | solution.py:834
  139.3 78.2 %feed_kernel.1 = (f32[128,1024]{1,0:T(8,128)}, bf16[8,128,1024]{2,1,0:T(8,128)(2,1)}, f32[512,1024]{1,0:T(8,128)}, f32[1024,256]{1,0:T(8,128)}) custom-call(bf16[128,1024]{1,0:T(8,128)(2,1)} %multiply_convert_fusion.act, bf16[16,128,1024]{2,1,0:T(8,128)(2,1)} %get-tuple-element.25.cot_all, bf16[512,1024]{1,0:T(8,128)(2,1)} %fusion.9.weight, ...), custom_call_target="tpu_custom_call" | custom-call | flops 20000000000 | bytes 20000000 | tf_op jit(solution)/shard_map/feed_kernel/pallas_call | solution.py:834
  222.5 2.0 select_bitcast_fusion
  226.7 71.5 %attend_back_kernel.1 = (f32[128,1024]{1,0:T(8,128)}, f32[128,1024]{1,0:T(8,128)}, f32[192,1024]{1,0:T(8,128)}) custom-call(bf16[16,64,128]{2,1,0:T(8,128)(2,1)} %bitcast.183, bf16[8,128,1024]{2,1,0:T(8,128)(2,1)} %get-tuple-element.27.out_sums, bf16[64,2048]{1,0:T(8,128)(2,1)} %get-tuple-element.28.query_t, bf16[64,2048]{1,0:T(8,128)(2,1)} %get-tuple-element.29.keys_t, ...), custom_call_target="tpu_custom_call" | custom-call | flops 20000000000 | bytes 20000000 | tf_op jit(solution)/shard_map/attend_back_kernel/pallas_call | solution.py:834
  300.3 2.6 all-to-all-start.1
  303.8 1.7 collective-permute-start.16
  305.5 2.3 slice_select_fusion
  313.1 3.4 fusion.2
  319.1 2.0 fusion.34
  321.1 5.9 %all-to-all-start = ((f32[16,32,164]{2,1,0:T(8,128)}), f32[16,32,164]{2,1,0:T(8,128)S(1)}, u32[]{:S(2)}, u32[]{:S(2)}) async-start(f32[16,32,164]{2,1,0:T(8,128)} %fusion.34), calls=%async_computation | async-start | bytes 1048576 | tf_op jit(solution)/shard_map/all_to_all | solution.py:1009
  327.0 6.9 %collective-permute-done.14 = f32[164,1024]{1,0:T(8,128)} collective-permute-done((f32[164,1024]{1,0:T(8,128)}, f32[164,1024]{1,0:T(8,128)}, u32[]{:S(2)}, u32[]{:S(2)}) %collective-permute-start.14) | collective-permute-done | bytes 671776 | tf_op jit(solution)/shard_map/ppermute | solution.py:939
  333.9 2.5 select_add_fusion
  336.4 6.7 %collective-permute-start.15 = (f32[164,1024]{1,0:T(8,128)}, f32[164,1024]{1,0:T(8,128)}, u32[]{:S(2)}, u32[]{:S(2)}) collective-permute-start(f32[164,1024]{1,0:T(8,128)} %select_add_fusion), channel_id=1, source_target_pairs={{0,0},{1,16},{2,1},{3,17},{4,2},{5,18},{6,3},{7,19},{8,4},{9,20},{... | collective-permute-start | bytes 2015240 | tf_op jit(solution)/shard_map/ppermute | solution.py:1002
  345.3 3.7 collective-permute-start.6
  348.9 1.9 collective-permute-start.7
  350.9 11.1 %collective-permute-done.10 = bf16[4,32,1024]{2,1,0:T(8,128)(2,1)S(1)} collective-permute-done((bf16[4,32,1024]{2,1,0:T(8,128)(2,1)S(1)}, bf16[4,32,1024]{2,1,0:T(8,128)(2,1)S(1)}, u32[]{:S(2)}, u32[]{:S(2)}) %collective-permute-start.10) | collective-permute-done | bytes 262176 | tf_op jit(solution)/shard_map/ppermute | solution.py:926
  363.6 19.6 %collective-permute-start.13 = (bf16[32,1024]{1,0:T(8,128)(2,1)S(1)}, bf16[32,1024]{1,0:T(8,128)(2,1)}, u32[]{:S(2)}, u32[]{:S(2)}) collective-permute-start(bf16[32,1024]{1,0:T(8,128)(2,1)S(1)} %get-tuple-element.66), channel_id=1, source_target_pairs={{0,24},{2,26},{4,28},{6,30},{8,0},{10,2},{12,4},{14,6},{16,8},{18,... | collective-permute-start | bytes 196616 | tf_op jit(solution)/shard_map/ppermute | solution.py:931
  385.1 2.1 reshape.119
  388.8 2.0 copy.79
  (113 shorter events, 38.2 us)
Async XLA Ops:
  2.0 49.9 %collective-permute-start = (bf16[3,64,1024]{2,1,0:T(8,128)(2,1)S(1)}, bf16[3,64,1024]{2,1,0:T(8,128)(2,1)}, u32[]{:S(2)}, u32[]{:S(2)}) collective-permute-start(bf16[3,64,1024]{2,1,0:T(8,128)(2,1)S(1)} %pad_maximum_fusion.8), channel_id=1, source_target_pairs={{0,1},{1,0},{2,3},{3,2},{4,5},{5,4},{6,7},{7,6},{8,9},{9,8},{10,11... | collective-permute-start | bytes 1179656 | tf_op jit(solution)/shard_map/ppermute | solution.py:975
  5.1 130.7 %collective-permute-start.1 = (bf16[512,1024]{1,0:T(8,128)(2,1)}, bf16[512,1024]{1,0:T(8,128)(2,1)}, u32[]{:S(2)}, u32[]{:S(2)}) collective-permute-start(bf16[512,1024]{1,0:T(8,128)(2,1)} %param.13), channel_id=1, source_target_pairs={{0,1},{1,0},{2,3},{3,2},{4,5},{5,4},{6,7},{7,6},{8,9},{9,8},{10,11... | collective-permute-start | bytes 3145736 | tf_op jit(solution)/shard_map/ppermute | solution.py:943
  5.3 37.8 %collective-permute-start.3 = (bf16[512,164]{1,0:T(8,128)(2,1)S(1)}, bf16[512,164]{1,0:T(8,128)(2,1)S(1)}, u32[]{:S(2)}, u32[]{:S(2)}) collective-permute-start(bf16[512,164]{1,0:T(8,128)(2,1)S(1)} %copy.68), channel_id=1, source_target_pairs={{0,1},{1,0},{2,3},{3,2},{4,5},{5,4},{6,7},{7,6},{8,9},{9,8},{10,11... | collective-permute-start | bytes 503816 | tf_op jit(solution)/shard_map/ppermute | solution.py:943
  8.4 41.2 %collective-permute-start.2 = (bf16[164,1024]{1,0:T(8,128)(2,1)S(1)}, bf16[164,1024]{1,0:T(8,128)(2,1)S(1)}, u32[]{:S(2)}, u32[]{:S(2)}) collective-permute-start(bf16[164,1024]{1,0:T(8,128)(2,1)S(1)} %constant_dynamic-slice_fusion.3), channel_id=1, source_target_pairs={{0,1},{1,0},{2,3},{3,2},{4,5},{5,4},{6,7},{7,6},{8,9},{9,8},{10,11... | collective-permute-start | bytes 1007624 | tf_op jit(solution)/shard_map/ppermute | solution.py:943
  54.0 81.7 %copy-start.9 = (bf16[512,1024]{1,0:T(8,128)(2,1)S(1)}, bf16[512,1024]{1,0:T(8,128)(2,1)}, u32[]{:S(2)}) copy-start(bf16[512,1024]{1,0:T(8,128)(2,1)} %param.13) | copy-start | bytes 3145732
  139.3 79.6 %copy-start.13 = (bf16[1,128,1024]{2,1,0:T(8,128)(2,1)S(1)}, bf16[1,128,1024]{2,1,0:T(8,128)(2,1)}, u32[]{:S(2)}) copy-start(bf16[1,128,1024]{2,1,0:T(8,128)(2,1)} %param.9) | copy-start | bytes 786436
  225.2 88.0 %collective-permute-start.8 = (f32[16,32,1024]{2,1,0:T(8,128)}, f32[16,32,1024]{2,1,0:T(8,128)}, u32[]{:S(2)}, u32[]{:S(2)}) collective-permute-start(f32[16,32,1024]{2,1,0:T(8,128)} %select_bitcast_fusion), channel_id=1, source_target_pairs={{0,1},{1,0},{2,3},{3,2},{4,5},{5,4},{6,7},{7,6},{8,9},{9,8},{10,11... | collective-permute-start | bytes 6291464 | tf_op jit(solution)/shard_map/ppermute | solution.py:939
  226.7 76.2 %copy-start.4 = (f32[1024,256]{1,0:T(8,128)S(1)}, f32[1024,256]{1,0:T(8,128)}, u32[]{:S(2)}) copy-start(f32[1024,256]{1,0:T(8,128)} %get-tuple-element.39) | copy-start | bytes 3145732
  300.3 12.2 %all-to-all-start.1 = ((f32[32,2,32]{2,1,0:T(2,128)}), f32[32,2,32]{2,1,0:T(2,128)S(1)}, u32[]{:S(2)}, u32[]{:S(2)}) async-start(f32[32,2,32]{2,1,0:T(2,128)} %maximum_bitcast_fusion), calls=%async_computation.1 | async-start | bytes 65536 | tf_op jit(solution)/shard_map/all_to_all | solution.py:1034
  303.8 15.3 %collective-permute-start.16 = (f32[16,32,164]{2,1,0:T(8,128)}, f32[16,32,164]{2,1,0:T(8,128)}, u32[]{:S(2)}, u32[]{:S(2)}) collective-permute-start(f32[16,32,164]{2,1,0:T(8,128)} %select_bitcast_fusion.1), channel_id=1, source_target_pairs={{0,1},{1,0},{2,3},{3,2},{4,5},{5,4},{6,7},{7,6},{8,9},{9,8},{10,11... | collective-permute-start | bytes 1007624 | tf_op jit(solution)/shard_map/ppermute | solution.py:939
  307.8 26.1 %collective-permute-start.14 = (f32[164,1024]{1,0:T(8,128)}, f32[164,1024]{1,0:T(8,128)}, u32[]{:S(2)}, u32[]{:S(2)}) collective-permute-start(f32[164,1024]{1,0:T(8,128)} %slice_select_fusion), channel_id=1, source_target_pairs={{0,1},{1,0},{2,3},{3,2},{4,5},{5,4},{6,7},{7,6},{8,9},{9,8},{10,11... | collective-permute-start | bytes 2015240 | tf_op jit(solution)/shard_map/ppermute | solution.py:939
  309.0 34.5 %collective-permute-start.4 = (f32[3,32,1024]{2,1,0:T(8,128)}, f32[3,32,1024]{2,1,0:T(8,128)}, u32[]{:S(2)}, u32[]{:S(2)}) collective-permute-start(f32[3,32,1024]{2,1,0:T(8,128)} %select_bitcast_fusion.2), channel_id=1, source_target_pairs={{0,1},{1,0},{2,3},{3,2},{4,5},{5,4},{6,7},{7,6},{8,9},{9,8},{10,11... | collective-permute-start | bytes 1179656 | tf_op jit(solution)/shard_map/ppermute | solution.py:939
  317.5 25.7 %collective-permute-start.9 = (bf16[4,2,32,1024]{3,2,0,1:T(8,128)(2,1)S(1)}, bf16[4,2,32,1024]{3,2,0,1:T(8,128)(2,1)S(1)}, u32[]{:S(2)}, u32[]{:S(2)}) collective-permute-start(bf16[4,2,32,1024]{3,2,0,1:T(8,128)(2,1)S(1)} %bitcast.179), channel_id=1, source_target_pairs={{0,2},{2,0},{4,6},{6,4},{8,10},{10,8},{12,14},{14,12},{16,18},{18,... | collective-permute-start | bytes 1572872 | tf_op jit(solution)/shard_map/ppermute | solution.py:926
  321.1 22.0 %copy-start.7 = (bf16[4,2,1,32,1024]{4,3,2,1,0:T(8,128)(2,1)S(1)}, bf16[4,2,1,32,1024]{4,3,2,1,0:T(8,128)(2,1)}, u32[]{:S(2)}) copy-start(bf16[4,2,1,32,1024]{4,3,2,1,0:T(8,128)(2,1)} %get-tuple-element.56) | copy-start | bytes 1572868
  321.1 62.9 %all-to-all-start = ((f32[16,32,164]{2,1,0:T(8,128)}), f32[16,32,164]{2,1,0:T(8,128)S(1)}, u32[]{:S(2)}, u32[]{:S(2)}) async-start(f32[16,32,164]{2,1,0:T(8,128)} %fusion.34), calls=%async_computation | async-start | bytes 1048576 | tf_op jit(solution)/shard_map/all_to_all | solution.py:1009
  336.4 50.8 %collective-permute-start.15 = (f32[164,1024]{1,0:T(8,128)}, f32[164,1024]{1,0:T(8,128)}, u32[]{:S(2)}, u32[]{:S(2)}) collective-permute-start(f32[164,1024]{1,0:T(8,128)} %select_add_fusion), channel_id=1, source_target_pairs={{0,0},{1,16},{2,1},{3,17},{4,2},{5,18},{6,3},{7,19},{8,4},{9,20},{... | collective-permute-start | bytes 2015240 | tf_op jit(solution)/shard_map/ppermute | solution.py:1002
  343.4 18.6 %collective-permute-start.10 = (bf16[4,32,1024]{2,1,0:T(8,128)(2,1)S(1)}, bf16[4,32,1024]{2,1,0:T(8,128)(2,1)S(1)}, u32[]{:S(2)}, u32[]{:S(2)}) collective-permute-start(bf16[4,32,1024]{2,1,0:T(8,128)(2,1)S(1)} %dynamic-slice_bitcast_fusion), channel_id=1, source_target_pairs={{0,4},{2,6},{4,0},{6,2},{8,12},{10,14},{12,8},{14,10},{16,20},{18,... | collective-permute-start | bytes 786440 | tf_op jit(solution)/shard_map/ppermute | solution.py:926
  344.6 19.0 %collective-permute-start.5 = (f32[32,1024]{1,0:T(8,128)S(1)}, f32[32,1024]{1,0:T(8,128)S(1)}, u32[]{:S(2)}, u32[]{:S(2)}) collective-permute-start(f32[32,1024]{1,0:T(8,128)S(1)} %get-tuple-element.62), channel_id=1, source_target_pairs={{0,0},{3,1},{6,2},{9,3},{12,4},{15,5},{18,6},{21,7},{24,8},{27,9},... | collective-permute-start | bytes 393224 | tf_op jit(solution)/shard_map/ppermute | solution.py:1025
  345.3 18.3 %collective-permute-start.6 = (f32[32,1024]{1,0:T(8,128)S(1)}, f32[32,1024]{1,0:T(8,128)S(1)}, u32[]{:S(2)}, u32[]{:S(2)}) collective-permute-start(f32[32,1024]{1,0:T(8,128)S(1)} %get-tuple-element.64), channel_id=1, source_target_pairs={{1,0},{4,1},{7,2},{10,3},{13,4},{16,5},{19,6},{22,7},{25,8},{28,9}... | collective-permute-start | bytes 393224 | tf_op jit(solution)/shard_map/ppermute | solution.py:1025
  348.9 34.3 %collective-permute-start.7 = (f32[32,1024]{1,0:T(8,128)S(1)}, f32[32,1024]{1,0:T(8,128)S(1)}, u32[]{:S(2)}, u32[]{:S(2)}) collective-permute-start(f32[32,1024]{1,0:T(8,128)S(1)} %get-tuple-element.63), channel_id=1, source_target_pairs={{2,0},{5,1},{8,2},{11,3},{14,4},{17,5},{20,6},{23,7},{26,8},{29,9}... | collective-permute-start | bytes 393224 | tf_op jit(solution)/shard_map/ppermute | solution.py:1025
  362.7 24.5 %collective-permute-start.11 = (bf16[32,1024]{1,0:T(8,128)(2,1)}, bf16[32,1024]{1,0:T(8,128)(2,1)}, u32[]{:S(2)}, u32[]{:S(2)}) collective-permute-start(bf16[32,1024]{1,0:T(8,128)(2,1)} %get-tuple-element.65), channel_id=1, source_target_pairs={{0,8},{2,10},{4,12},{6,14},{8,16},{10,18},{12,20},{14,22},{16,24},... | collective-permute-start | bytes 196616 | tf_op jit(solution)/shard_map/ppermute | solution.py:931
  363.6 23.6 %collective-permute-start.12 = (bf16[32,1024]{1,0:T(8,128)(2,1)}, bf16[32,1024]{1,0:T(8,128)(2,1)}, u32[]{:S(2)}, u32[]{:S(2)}) collective-permute-start(bf16[32,1024]{1,0:T(8,128)(2,1)} %get-tuple-element.67), channel_id=1, source_target_pairs={{0,16},{2,18},{4,20},{6,22},{8,24},{10,26},{12,28},{14,30},{16,0},... | collective-permute-start | bytes 196616 | tf_op jit(solution)/shard_map/ppermute | solution.py:931
  363.6 27.3 %copy-start.1 = (bf16[512,2624]{0,1:T(8,128)(2,1)S(1)}, bf16[512,2624]{0,1:T(8,128)(2,1)}, u32[]{:S(2)}) copy-start(bf16[512,2624]{0,1:T(8,128)(2,1)} %param.15) | copy-start | bytes 8060932
  363.6 23.6 %collective-permute-start.13 = (bf16[32,1024]{1,0:T(8,128)(2,1)S(1)}, bf16[32,1024]{1,0:T(8,128)(2,1)}, u32[]{:S(2)}, u32[]{:S(2)}) collective-permute-start(bf16[32,1024]{1,0:T(8,128)(2,1)S(1)} %get-tuple-element.66), channel_id=1, source_target_pairs={{0,24},{2,26},{4,28},{6,30},{8,0},{10,2},{12,4},{14,6},{16,8},{18,... | collective-permute-start | bytes 196616 | tf_op jit(solution)/shard_map/ppermute | solution.py:931
  (12 other events, 70.5 us)

commit v2 on v1

--- a/solution.py
+++ b/solution.py
@@ -275,7 +275,8 @@
 class Place:
     def __init__(self, count):
         self.count, self.line = count, count // 4
-        self.me = lax.axis_index("ctx")
+        self.me, self.pair = lax.axis_index("ctx"), lax.axis_index("fsdp")
+        self.owner = self.me * 2 + self.pair
         self.z, self.x, self.core = self.me // 4, self.me // 2 % 2, self.me % 2
 
     def slot(self, z, x, core):
@@ -293,7 +294,7 @@
     def near(self, step):
         return self.far(self.line - 1 - step)
 
-    def meet(self):
+    def meet(self, everyone=False):
         barrier = pltpu.get_barrier_semaphore()
 
         @pl.loop(1, self.count)
@@ -302,7 +303,29 @@
                 barrier, inc=1, device_id={"ctx": (self.me + shift) % self.count}, device_id_type=MESH
             )
 
-        pl.semaphore_wait(barrier, self.count - 1)
+        if everyone:
+            @pl.loop(0, self.count)
+            def _(to):
+                pl.semaphore_signal(
+                    barrier, inc=1, device_id={"ctx": to, "fsdp": 1 - self.pair}, device_id_type=MESH
+                )
+
+            pl.semaphore_wait(barrier, 2 * self.count - 1)
+        else:
+            pl.semaphore_signal(barrier, inc=1, device_id={"fsdp": 1 - self.pair}, device_id_type=MESH)
+            pl.semaphore_wait(barrier, self.count)
+
+    def over_pair(self, src, dst, send, recv):
+        return pltpu.make_async_remote_copy(
+            src_ref=src, dst_ref=dst, send_sem=send, recv_sem=recv,
+            device_id={"fsdp": 1 - self.pair}, device_id_type=MESH,
+        )
+
+    def to_owner(self, src, dst, send, recv, owner):
+        return pltpu.make_async_remote_copy(
+            src_ref=src, dst_ref=dst, send_sem=send, recv_sem=recv,
+            device_id={"ctx": owner // 2, "fsdp": owner % 2}, device_id_type=MESH,
+        )
 
     def copy(self, src, dst, send, recv, to):
         return pltpu.make_async_remote_copy(
@@ -563,6 +586,73 @@
             self.to((p.me + shift) % p.count).wait_send()
 
 
+class Spread:
+    def __init__(self, place, src, dst, sems):
+        self.p, self.src, self.dst = place, src, dst
+        self.s, self.r = sems
+
+    @staticmethod
+    def sems(count):
+        return [pltpu.SemaphoreType.DMA((2 * count,))] * 2
+
+    def to(self, j):
+        p = self.p
+        return p.to_owner(self.src.at[j], self.dst.at[p.owner], self.s.at[j], self.r.at[p.owner], j)
+
+    def send(self):
+        p = self.p
+        self.dst[p.owner] = self.src[p.owner]
+
+        @pl.loop(1, 2 * p.count)
+        def _(shift):
+            self.to((p.owner + shift) % (2 * p.count)).start()
+
+    def arrived(self):
+        p = self.p
+
+        @pl.loop(1, 2 * p.count)
+        def _(shift):
+            j = (p.owner + shift) % (2 * p.count)
+            p.to_owner(self.src.at[j], self.dst.at[j], self.s.at[j], self.r.at[j], j).wait_recv()
+
+    def sent(self):
+        p = self.p
+
+        @pl.loop(1, 2 * p.count)
+        def _(shift):
+            self.to((p.owner + shift) % (2 * p.count)).wait_send()
+
+
+class Deliver:
+    def __init__(self, place, src, dst, sems):
+        self.p, self.src, self.dst = place, src, dst
+        self.s, self.r = sems
+
+    def away(self, piece, owner, slot):
+        return self.p.to_owner(self.src.at[piece], self.dst.at[slot], self.s.at[piece], self.r.at[slot], owner)
+
+    def send(self, piece, owner, slot):
+        @pl.when(owner != self.p.owner)
+        def _():
+            self.away(piece, owner, slot).start()
+
+        @pl.when(owner == self.p.owner)
+        def _():
+            self.dst[slot] = self.src[piece]
+
+    def sent(self, piece, owner, slot):
+        @pl.when(owner != self.p.owner)
+        def _():
+            self.away(piece, owner, slot).wait_send()
+
+    def arrived(self, slot, source):
+        p = self.p
+
+        @pl.when(source != p.owner)
+        def _():
+            p.to_owner(self.src.at[0], self.dst.at[slot], self.s.at[0], self.r.at[slot], source).wait_recv()
+
+
 def turn(value):
     half = value.shape[0] // 2
     return jnp.concatenate([-value[half:], value[:half]], axis=0)
@@ -574,31 +664,79 @@
 
 
 def attend_kernel(
-    count, act, cot, weight, cos, sine,
-    act_all, cot_all, query_t, keys_t, keys, values, mixed_own, log_sum, mixed,
-    values_t, load_sem, *sems
+    count, act, cot, qkv_weight, in_mine, down_mine, out_mine, cos, sine,
+    act_all, cot_all, query_t, keys_t, keys, values, mixed_own, log_sum, mixed, weight, in_pair, down_pair, out_pair,
+    values_t, load_sem, part_sem, part_got, piece_sem, piece_got, *sems
 ):
     f32, bf16 = jnp.float32, jnp.bfloat16
     p = Place(count)
     rows, head = act.shape[0], keys_t.shape[0]
+    width = count * head
     n = 8
     first = Gather(p, act_all, sems[:n])
     second = Gather(p, cot_all, sems[n : 2 * n])
     trade = Exchange(p, mixed_own, mixed, sems[2 * n :])
-    loads = [
-        pltpu.make_async_copy(act, act_all.at[p.me], load_sem.at[0]),
-        pltpu.make_async_copy(cot, cot_all.at[p.me], load_sem.at[1]),
-    ]
+    pieces = [(in_mine, in_pair), (down_mine, down_pair), (out_mine, out_pair)]
+    loads = [(act, act_all.at[p.me]), (cot, cot_all.at[p.me])] + [(src, dst.at[p.pair]) for src, dst in pieces]
+    loads = [pltpu.make_async_copy(src, dst, load_sem.at[i]) for i, (src, dst) in enumerate(loads)]
     for load in loads:
         load.start()
+
+    def part_rows(part):
+        start = part * width + p.me * head
+        holder = start // qkv_weight.shape[0]
+        at = pl.ds(pl.multiple_of(start - holder * qkv_weight.shape[0], head), head)
+        return holder == p.pair, qkv_weight.at[at]
+
+    def part_copies(part):
+        here, src = part_rows(part)
+        return (
+            here,
+            pltpu.make_async_copy(src, weight.at[part], load_sem.at[5 + part]),
+            p.over_pair(src, weight.at[part], part_sem.at[part], part_got.at[part]),
+        )
+
+    swaps = [
+        p.over_pair(src, dst.at[p.pair], piece_sem.at[i], piece_got.at[i]) for i, (src, dst) in enumerate(pieces)
+    ]
+    for part in range(3):
+        here, own, away = part_copies(part)
+
+        @pl.when(here)
+        def _():
+            own.start()
+
     p.meet()
+    for part in range(3):
+        here, own, away = part_copies(part)
+
+        @pl.when(here)
+        def _():
+            away.start()
+
+    for swap in swaps:
+        swap.start()
     for load in loads:
         load.wait()
+
+    first.part(0)
+    for part in range(3):
+        here, own, away = part_copies(part)
+
+        @pl.when(here)
+        def _():
+            own.wait()
+
+        @pl.when(jnp.logical_not(here))
+        def _():
+            away.wait_recv()
+
+    head_weight = weight[...].reshape(3 * head, act.shape[1])
 
     def project(z, x, core):
         at = p.slot(z, x, core)
         lanes = pl.ds(pl.multiple_of(at * rows, rows), rows)
-        packed = matmul(weight[...], act_all[at], 1, 1)
+        packed = matmul(head_weight, act_all[at], 1, 1)
         c, s = cos[:, lanes], sine[:, lanes]
         query, key = packed[:head], packed[head : 2 * head]
         query_t[:, lanes] = (query * c + turn(query) * s).astype(bf16)
@@ -608,7 +746,9 @@
         keys[lanes, :] = key.T.astype(bf16)
         values[lanes, :] = packed[2 * head :].T.astype(bf16)
 
-    @pl.loop(0, 4 * p.line + 4)
+    project(p.z, p.x, p.core)
+
+    @pl.loop(4, 4 * p.line + 4)
     def _(at):
         first.part(at, project)
 
@@ -652,11 +792,21 @@
     first.sent()
     second.sent()
     trade.sent()
+    for part in range(3):
+        here, own, away = part_copies(part)
+
+        @pl.when(here)
+        def _():
+            away.wait_send()
+
+    for swap in swaps:
+        swap.wait()
 
 
 def feed_kernel(
-    count, act, cot_all, weight, down,
-    grad_act, out_sums, grad_weight, grad_down,
+    count, act, cot_all, in_pair, down_pair, gain,
+    grad_act, out_sums, in_grad, down_grad,
+    weight, down, grad_weight, grad_down,
     act_all, gated, inner_grad, grad_part, out_part, grad_got, grad_sums, out_got, load_sem, *rest
 ):
     f32, bf16 = jnp.float32, jnp.bfloat16
@@ -669,6 +819,12 @@
     halve_out = Halve(p, out_part, out_got, out_sums, sems[16:18])
     load = pltpu.make_async_copy(act, act_all.at[p.me], load_sem)
     load.start()
+    units, half = in_pair.shape[1], down_pair.shape[1]
+    weight[...] = jnp.zeros_like(weight)
+    down[...] = jnp.zeros_like(down)
+    for at in range(2):
+        weight[at * group : at * group + units, :] = in_pair[at]
+        down[at * half : (at + 1) * half, :units] = down_pair[at]
     p.meet()
     load.wait()
 
@@ -727,6 +883,12 @@
 
         halve_out.add(step)
 
+    for at in range(2):
+        in_grad[at] = grad_weight[at * group : at * group + units, :].astype(bf16)
+    gain_row = jnp.sum(grad_weight[...] * weight[...].astype(f32), axis=0, keepdims=True) / gain[...]
+    lane = lax.broadcasted_iota(jnp.int32, grad_down.shape, 1)
+    column = jnp.broadcast_to(gain_row, (8, gain_row.shape[1])).T[:, :1]
+    down_grad[...] = jnp.where(lane == units, column, grad_down[...]).astype(bf16).reshape(down_grad.shape)
     settle.finish(grad_act)
     gather.sent()
     halve.sent()
@@ -735,19 +897,30 @@
 
 
 def attend_back_kernel(
-    count, grad_mixed, out_sums, query_t, keys_t, keys, values, mixed_own, log_sum, act_all, weight, cos, sine,
-    grad_act, out_total, grad_weight,
-    grad_own, grad_keys, grad_values, grad_packed, grad_part, grad_got, grad_sums, *rest
+    count, grad_mixed, grad_mid, mixed, out_sums, query_t, keys_t, keys, values, mixed_own, log_sum,
+    act_all, weight, cos, sine, in_grad, down_grad, gain,
+    grad_act, out_total, qkv_out, out_out, in_out, down_out, gain_m_out, gain_a_out,
+    grad_own, grad_keys, grad_values, grad_packed, grad_part, grad_got, grad_sums, grad_weight,
+    pair_part, pair_got, proj_part, proj_got, proj_sums, in_got, down_got, qkv_part, qkv_got, gain_part, gain_got,
+    pair_s, pair_r, in_s, in_r, qkv_s, qkv_r, *rest
 ):
     f32, bf16 = jnp.float32, jnp.bfloat16
     p = Place(count)
     rows, head = grad_mixed.shape[2], keys_t.shape[0]
-    bufs, out_bufs, sems = rest[:4], rest[4:8], rest[8:]
+    width, unit = count * head, head // 2
+    bufs, out_bufs, proj_bufs, sems = rest[:4], rest[4:8], rest[8:12], rest[12:]
     trade = Exchange(p, grad_mixed, grad_own, sems[:2])
     halve = Halve(p, grad_part, grad_got, grad_sums, sems[2:4])
     settle = Settle(p, grad_sums, bufs, sems[4:10])
     settle_out = Settle(p, out_sums, out_bufs, sems[10:16])
-    p.meet()
+    halve_proj = Halve(p, proj_part, proj_got, proj_sums, sems[16:18])
+    settle_proj = Settle(p, proj_sums, proj_bufs, sems[18:24])
+    spread_down = Spread(p, down_grad, down_got, sems[24:26])
+    spread_gain = Spread(p, gain_part, gain_got, sems[26:28])
+    give_in = Deliver(p, in_grad, in_got, (in_s, in_r))
+    give_qkv = Deliver(p, qkv_part, qkv_got, (qkv_s, qkv_r))
+    swap = p.over_pair(pair_part.at[1 - p.pair], pair_got, pair_s, pair_r)
+    p.meet(True)
 
     @pl.loop(0, count)
     def _(shift):
@@ -757,6 +930,19 @@
     def _(step):
         settle_out.across(p.far(step)).start()
 
+    for part in range(2):
+        give_in.send(part, part * count + p.me, p.pair)
+    spread_down.send()
+    flat = mixed[...].reshape(width, rows)
+
+    @pl.loop(0, count // 2)
+    def _(i):
+        lanes = pl.ds(pl.multiple_of(i * 4 * unit, 4 * unit), 4 * unit)
+        piece = matmul(grad_mid[:, lanes], flat, 0, 1).astype(bf16)
+        for at in range(4):
+            pair_part[at % 2, 2 * i + at // 2] = piece[at * unit : (at + 1) * unit]
+
+    swap.start()
     grad_keys[...] = jnp.zeros_like(grad_keys)
     grad_values[...] = jnp.zeros_like(grad_values)
     trade.arrived()
@@ -787,6 +973,8 @@
     def _(step):
         settle_out.pass_on(p.far(step))
 
+    swap.wait_recv()
+    proj_part[...] = (pair_part[p.pair].astype(f32) + pair_got[...].astype(f32)).astype(bf16)
     grad_key = grad_keys[...].T * scale
     grad_packed[head : 2 * head, :] = (grad_key * cos[...] + turn_back(grad_key * sine[...])).astype(bf16)
     grad_packed[2 * head :, :] = grad_values[...].T.astype(bf16)
@@ -803,6 +991,8 @@
     @pl.loop(0, p.line)
     def _(step):
         z = p.far(step)
+        halve_proj.beside(z, 0).start()
+        halve_proj.beside(z, 1).start()
         halve.add(z)
         settle.across(z).start()
 
@@ -813,28 +1003,79 @@
 
     grad_weight[...] = grad_chunk(0)
 
+    @pl.loop(1, p.line)
+    def _(step):
+        grad_weight[...] += grad_chunk(step)
+
+    for at in range(6):
+        qkv_part[at] = grad_weight[at * unit : (at + 1) * unit, :].astype(bf16)
+    gain_row = jnp.sum(grad_weight[...] * weight[...].astype(f32), axis=0, keepdims=True) / gain[...]
+    gain_part[...] = jnp.broadcast_to(gain_row, (128, width)).T.astype(bf16).reshape(gain_part.shape)
+
+    def unit_of(at):
+        return (at // 2) * 2 * count + 2 * p.me + at % 2
+
+    for at in range(6):
+        give_qkv.send(at, unit_of(at) // 3, unit_of(at) % 3 * 2 + p.pair)
+    spread_gain.send()
+
     @pl.loop(0, p.line)
     def _(step):
-        settle.pass_on(p.far(step))
-
-        @pl.when(step > 0)
-        def _():
-            grad_weight[...] += grad_chunk(step)
-
+        z = p.far(step)
+        halve_proj.add(z)
+        settle_proj.across(z).start()
+
+    @pl.loop(0, p.line)
+    def _(step):
+        z = p.far(step)
+        settle.pass_on(z)
+        settle_proj.pass_on(z)
+
+    for side in range(2):
+        give_in.arrived(side, p.owner % count * 2 + side)
+    in_out[...] = in_got[0].astype(f32) + in_got[1].astype(f32)
+    spread_down.arrived()
+    units = in_out.shape[0]
+    gain_m = jnp.zeros((unit, down_got.shape[2]), f32)
+    for at in range(count):
+        block = down_got[2 * at].astype(f32) + down_got[2 * at + 1].astype(f32)
+        down_out[:, at * units : (at + 1) * units] = block[:, :units]
+        gain_m += block
+    gain_m_out[...] = gain_m[:, units : units + 1]
     settle_out.finish(out_total)
+    for slot in range(3):
+        source = (3 * p.owner + slot) % (2 * count) // 2 * 2
+        for side in range(2):
+            give_qkv.arrived(2 * slot + side, source + side)
+        qkv_out[slot * unit : (slot + 1) * unit, :] = qkv_got[2 * slot].astype(f32) + qkv_got[2 * slot + 1].astype(f32)
+    spread_gain.arrived()
+    gain_a = jnp.zeros(gain_got.shape[1:], f32)
+    for at in range(2 * count):
+        gain_a += gain_got[at].astype(f32)
+    gain_a_out[...] = gain_a[:, :1]
+    settle_proj.finish(out_out)
     settle.finish(grad_act)
     trade.sent()
     halve.sent()
     settle.sent()
     settle_out.sent()
-
-
-def run_kernel(body, outs, scratch, collective, flops, args):
-    vmem = pl.BlockSpec(memory_space=pltpu.VMEM)
+    halve_proj.sent()
+    settle_proj.sent()
+    spread_down.sent()
+    spread_gain.sent()
+    swap.wait_send()
+    for part in range(2):
+        give_in.sent(part, part * count + p.me, p.pair)
+    for at in range(6):
+        give_qkv.sent(at, unit_of(at) // 3, unit_of(at) % 3 * 2 + p.pair)
+
+
+def run_kernel(body, outs, scratch, collective, flops, args, outside=()):
+    vmem, anywhere = pl.BlockSpec(memory_space=pltpu.VMEM), pl.BlockSpec(memory_space=pl.ANY)
     return pl.pallas_call(
         body,
         out_shape=outs,
-        in_specs=[vmem] * len(args),
+        in_specs=[anywhere if i in outside else vmem for i in range(len(args))],
         out_specs=[vmem] * len(outs),
         scratch_shapes=scratch,
         compiler_params=pltpu.CompilerParams(
@@ -849,100 +1090,74 @@
     return jax.ShapeDtypeStruct(shape, kind)
 
 
-def attend(count, act, cot, weight, cos, sine):
+def attend(count, head, act, cot, qkv_weight, in_mine, down_mine, out_mine, cos, sine):
     bf16, f32 = jnp.bfloat16, jnp.float32
     rows, width = act.shape
-    head, length, line = weight.shape[0] // 3, rows * count, count // 4
+    length, line = rows * count, count // 4
     blocks = shaped((count, rows, width), bf16)
     tall, flat = shaped((head, length), bf16), shaped((length, head), bf16)
     heads = shaped((count, head, rows), bf16)
+    pairs = [shaped((2,) + part.shape, bf16) for part in (in_mine, down_mine, out_mine)]
+    three = pltpu.SemaphoreType.DMA((3,))
     return run_kernel(
         functools.partial(attend_kernel, count),
-        [blocks, blocks, tall, tall, flat, flat, heads, shaped((1, length), f32), heads],
-        [pltpu.VMEM((head, length), bf16), pltpu.SemaphoreType.DMA((2,))]
+        [blocks, blocks, tall, tall, flat, flat, heads, shaped((1, length), f32), heads, shaped((3, head, width), bf16)]
+        + pairs,
+        [pltpu.VMEM((head, length), bf16), pltpu.SemaphoreType.DMA((8,))] + [three] * 4
         + Gather.sems(line) * 2 + Exchange.sems(count),
-        0, 10_000_000_000, [act, cot, weight, cos, sine],
-    )
-
-
-def feed(count, act, cot_all, weight, down):
+        0, 10_000_000_000, [act, cot, qkv_weight, in_mine, down_mine, out_mine, cos, sine], (2, 5),
+    )
+
+
+def feed(count, group, act, cot_all, in_pair, down_pair, gain):
     bf16, f32 = jnp.bfloat16, jnp.float32
     rows, width = act.shape
-    group, length, line = down.shape[1], rows * count, count // 4
+    length, line = rows * count, count // 4
     block = (rows, width)
     whole, half = pltpu.VMEM((count,) + block, bf16), pltpu.VMEM((2 * line,) + block, bf16)
     return run_kernel(
         functools.partial(feed_kernel, count),
-        [shaped(block, f32), shaped((2 * line,) + block, bf16), shaped(weight.shape, f32), shaped(down.shape, f32)],
-        [whole, pltpu.VMEM((length, group), bf16), pltpu.VMEM((length, 2 * group), bf16), whole, whole,
+        [shaped(block, f32), shaped((2 * line,) + block, bf16), shaped(in_pair.shape, bf16),
+         shaped((2 * count, width // (2 * count), group), bf16)],
+        [pltpu.VMEM((2 * group, width), bf16), pltpu.VMEM((width, group), bf16),
+         pltpu.VMEM((2 * group, width), f32), pltpu.VMEM((width, group), f32),
+         whole, pltpu.VMEM((length, group), bf16), pltpu.VMEM((length, 2 * group), bf16), whole, whole,
          half, half, half, pltpu.SemaphoreType.DMA]
         + Settle.bufs(line, block)
         + Gather.sems(line) + Halve.sems(line) + Settle.sems(line) + Halve.sems(line),
-        1, 20_000_000_000, [act, cot_all, weight, down],
-    )
-
-
-def attend_back(count, grad_mixed, out_sums, kept, act_all, weight, cos, sine):
+        1, 20_000_000_000, [act, cot_all, in_pair, down_pair, gain],
+    )
+
+
+def attend_back(count, grad_mixed, grad_mid, mixed, out_sums, kept, act_all, weight, cos, sine, in_grad, down_grad, gain):
     bf16, f32 = jnp.bfloat16, jnp.float32
     rows, width = act_all.shape[1:]
     head, length, line = weight.shape[0] // 3, rows * count, count // 4
-    block = (rows, width)
-    whole, half = pltpu.VMEM((count,) + block, bf16), pltpu.VMEM((2 * line,) + block, bf16)
+    block, unit, units = (rows, width), head // 2, in_grad.shape[1]
+    piece = (unit, width)
+
+    def held(*shape):
+        return pltpu.VMEM(shape, bf16)
+
+    whole, half = held(count, *block), held(2 * line, *block)
     flat = pltpu.VMEM((length, head), f32)
+    two, six, one = pltpu.SemaphoreType.DMA((2,)), pltpu.SemaphoreType.DMA((6,)), pltpu.SemaphoreType.DMA
     return run_kernel(
         functools.partial(attend_back_kernel, count),
-        [shaped(block, f32), shaped(block, f32), shaped(weight.shape, f32)],
-        [pltpu.VMEM((count, head, rows), bf16), flat, flat, pltpu.VMEM((3 * head, length), bf16), whole, half, half]
-        + Settle.bufs(line, block) * 2
-        + Exchange.sems(count) + Halve.sems(line) + Settle.sems(line) * 2,
-        2, 20_000_000_000, [grad_mixed, out_sums, *kept, act_all, weight, cos, sine],
-    )
-
-
-def swap_perm(count, stride):
-    return [(i, i + stride if (i // stride) % 2 == 0 else i - stride) for i in range(count)]
-
-
-def line_perm(count, stride, shift):
-    return [(i, (i + shift * stride) % count) for i in range(count)]
-
-
-def pick(cond, first, second):
-    return jnp.where(cond, first, second)
-
-
-def scatter_sum(partial):
-    count = lax.axis_size("ctx")
-    index = lax.axis_index("ctx")
-    line = count // 4
-    line_pos = index // 4
-    f32 = jnp.float32
-    rest = partial.reshape((line, 2, 2) + partial.shape[1:])
-    for stride in (1, 2):
-        axis = 2 if stride == 1 else 1
-        mine = lax.rem(index // stride, 2)
-        keep = lax.dynamic_index_in_dim(rest, mine, axis, keepdims=False)
-        send = lax.dynamic_index_in_dim(rest, 1 - mine, axis, keepdims=False)
-        got = lax.ppermute(send, "ctx", swap_perm(count, stride))
-        rest = (keep.astype(f32) + got.astype(f32)).astype(partial.dtype)
-    total = lax.dynamic_index_in_dim(rest, line_pos, 0, keepdims=False).astype(f32)
-    for shift in range(1, line):
-        send = lax.dynamic_index_in_dim(rest, lax.rem(line_pos + shift, line), 0, keepdims=False)
-        total = total + lax.ppermute(send, "ctx", line_perm(count, 4, shift)).astype(f32)
-    return total
-
-
-def pair_halves(low, high):
-    second = lax.axis_index("fsdp") == 1
-    send = pick(second, low, high)
-    keep = pick(second, high, low)
-    return keep + lax.ppermute(send, "fsdp", [(0, 1), (1, 0)])
-
-
-def pair_rows(mine):
-    other = lax.ppermute(mine, "fsdp", [(0, 1), (1, 0)])
-    second = lax.axis_index("fsdp") == 1
-    return pick(second, other, mine), pick(second, mine, other)
+        [shaped(block, f32), shaped(block, f32), shaped((3 * unit, width), f32), shaped(piece, f32),
+         shaped((units, width), f32), shaped((unit, units * count), f32), shaped((unit, 1), f32), shaped((unit, 1), f32)],
+        [held(count, head, rows), flat, flat, held(3 * head, length), whole, half, half,
+         pltpu.VMEM((3 * head, width), f32),
+         held(2, count, *piece), held(count, *piece), held(count, *piece), held(2 * line, *piece), held(2 * line, *piece),
+         held(*in_grad.shape), held(*down_grad.shape), held(6, *piece), held(6, *piece),
+         held(2 * count, unit, 128), held(2 * count, unit, 128),
+         one, one, two, two, six, six]
+        + Settle.bufs(line, block) * 2 + Settle.bufs(line, piece)
+        + Exchange.sems(count) + Halve.sems(line) + Settle.sems(line) * 2
+        + Halve.sems(line) + Settle.sems(line) + Spread.sems(count) * 2,
+        2, 20_000_000_000,
+        [grad_mixed, grad_mid, mixed, out_sums, *kept, act_all, weight, cos, sine, in_grad, down_grad, gain],
+    )
 
 
 def tensor_layer(
@@ -951,34 +1166,15 @@
     f32 = jnp.float32
     bf16 = jnp.bfloat16
     count = lax.axis_size("ctx")
-    devices = count * lax.axis_size("fsdp")
     index = lax.axis_index("ctx")
-    pair = lax.axis_index("fsdp")
-    place = index * 2 + pair
     rows, width = tokens.shape[1], tokens.shape[2]
     length = rows * count
     head_size = width // count
-    hidden = in_weight.shape[0]
-    group = hidden // count
-    padding = -group % 128
-    unit = width // devices
-
-    half_rows = qkv_weight.shape[0]
-
-    def head_rows(part):
-        start = part * width + index * head_size
-        owner = start // half_rows
-        own = lax.dynamic_slice_in_dim(qkv_weight, start - owner * half_rows, head_size, 0)
-        return owner == pair, own
-
-    owned = [head_rows(part) for part in range(3)]
-    got = lax.ppermute(jnp.stack([own for _, own in owned]), "fsdp", [(0, 1), (1, 0)])
-    qkv_head = jnp.concatenate([jnp.where(here, own, got[i]) for i, (here, own) in enumerate(owned)], axis=0)
+    group = in_weight.shape[0] // count
+    padded = (group // 128 + 1) * 128
+
     in_mine = lax.dynamic_slice_in_dim(in_weight, index * group, group, 0)
-    in_both = jnp.concatenate([jnp.pad(part, ((0, padding), (0, 0))) for part in pair_rows(in_mine)], axis=0)
     down_mine = lax.dynamic_slice_in_dim(down_weight, index * group, group, 1)
-    down_cols = jnp.concatenate([jnp.pad(part, ((0, 0), (0, padding))) for part in pair_rows(down_mine)], axis=0)
-    out_full = jnp.concatenate(pair_rows(out_weight), axis=0)
 
     cos_table, sine_table = rope_tables(0, length, head_size)
     cos_table, sine_table = cos_table[:, 0].T, sine_table[:, 0].T
@@ -986,53 +1182,29 @@
     normed_a, inv_a = normalize(resid)
     act_a = (normed_a * gain_attn).astype(bf16)
     cot_rows = cotangent[0]
-    act_all, cot_all, *kept, mixed = attend(count, act_a, cot_rows, qkv_head, cos_table, sine_table)
-    mixed = mixed.reshape(width, rows)
-    middle = resid + matmul(mixed, out_full, 0, 1)
+    act_all, cot_all, *kept, mixed, qkv_head, in_pair, down_pair, out_pair = attend(
+        count, head_size, act_a, cot_rows, qkv_weight, in_mine, down_mine, out_weight, cos_table, sine_table
+    )
+    qkv_head = qkv_head.reshape(3 * head_size, width)
+    out_full = out_pair.reshape(width, width)
+    middle = resid + matmul(mixed.reshape(width, rows), out_full, 0, 1)
     normed_m, inv_m = normalize(middle)
     act_m = (normed_m * gain_mlp).astype(bf16)
-    grad_act_m, out_sums, grad_in_both, grad_down_cols = feed(count, act_m, cot_all, in_both, down_cols)
+    grad_act_m, out_sums, in_grad, down_grad = feed(count, padded, act_m, cot_all, in_pair, down_pair, gain_mlp[None])
 
     grad_middle = cot_rows.astype(f32) + norm_back(grad_act_m * gain_mlp, normed_m, inv_m)
     grad_mid_bf = grad_middle.astype(bf16)
     grad_mixed = matmul(out_full, grad_mid_bf, 0, 1).astype(bf16).reshape(count, head_size, rows)
-
-    padded = group + padding
-    grad_in_half = pair_halves(grad_in_both[:group], grad_in_both[padded : padded + group])
-    grad_in = lax.ppermute(
-        grad_in_half,
-        ("ctx", "fsdp"),
-        [(c * 2 + y, y * count + c) for c in range(count) for y in range(2)],
-    )
-    grad_down_cols = grad_down_cols[:, :group].reshape(count, 2, unit, group)
-    grad_down_half = pair_halves(grad_down_cols[:, 0], grad_down_cols[:, 1])
-    grad_down = lax.all_to_all(grad_down_half, "ctx", 0, 0).transpose(1, 0, 2).reshape(unit, hidden)
-    grad_out_part = matmul(grad_mid_bf, mixed, 0, 1).reshape(count, 2, unit, width)
-    grad_out = scatter_sum(pair_halves(grad_out_part[:, 0], grad_out_part[:, 1]).astype(bf16))
-
-    grad_act_a, out_total, grad_qkv_head = attend_back(
-        count, grad_mixed, out_sums, kept, act_all, qkv_head, cos_table, sine_table
+    grad_act_a, out_total, grad_qkv, grad_out, grad_in, grad_down, grad_gain_m, grad_gain_a = attend_back(
+        count, grad_mixed, grad_mid_bf, mixed, out_sums, kept, act_all, qkv_head, cos_table, sine_table,
+        in_grad, down_grad, gain_attn[None],
     )
     output = middle + out_total
-    grad_qkv_head = grad_qkv_head.reshape(3, 2, unit, width)
-    grad_units = pair_halves(grad_qkv_head[:, 0], grad_qkv_head[:, 1])
-    inverse = pow(3, -1, devices)
-    slots = []
-    for slot in range(3):
-        owner = lax.rem((place - slot + devices) * inverse, devices)
-        piece = lax.dynamic_index_in_dim(grad_units, (3 * owner + slot) // devices, 0, keepdims=False)
-        slots.append(
-            lax.ppermute(
-                piece, ("ctx", "fsdp"), [((3 * o + slot) % devices, o) for o in range(devices)]
-            )
-        )
-    grad_qkv = jnp.concatenate(slots, axis=0)
-    grad_gain_m = jnp.sum(grad_act_m * normed_m, axis=0)
-    grad_gain_a = jnp.sum(grad_act_a * normed_a, axis=0)
     grad_input = grad_middle + norm_back(grad_act_a * gain_attn, normed_a, inv_a)
-    gains = jnp.stack([grad_gain_a, grad_gain_m]).reshape(2, devices, unit).transpose(1, 0, 2)
-    gains = jnp.sum(lax.all_to_all(gains, ("ctx", "fsdp"), 0, 0), axis=0)
-    return (output[None], grad_input[None], grad_qkv, grad_out, grad_in, grad_down, gains[0], gains[1])
+    return (
+        output[None], grad_input[None], grad_qkv, grad_out, grad_in, grad_down,
+        grad_gain_a.reshape(-1), grad_gain_m.reshape(-1),
+    )
 
 
 def solution(mesh):

time: 392 us -> 298 us (0.76)
  waiting for transfers between devices: 55.6 us -> 0 us
  starting transfers between devices: 52.5 us -> 0 us
  Pallas kernels: 231 us -> 268 us
  other arithmetic: 36 us -> 18.9 us
  local copies, waits for them, and re-layouts: 11 us -> 5.72 us
    ppermute x17 -> x0, waiting for transfers between devices: 55.6 us -> none  [the longest x3 35.9 us: pair_rows(): other = lax.ppermute(mine, 'fsdp', [(0, 1), (1, 0)])]
    ppermute x17 -> x0, starting transfers between devices: 44.1 us -> none  [the longest x3 20.5 us: scatter_sum(): lax.ppermute(send, 'ctx', line_perm(count, 4, shift)).astype(f32)]
    pallas_call x3, Pallas kernels: 231 us -> 268 us  [run_kernel(): pl.pallas_call(body, out_shape=outs, in_specs=[anywhere if i in outside e...]
    select_n x8 -> x0, other arithmetic: 9.91 us -> none  [the longest x7 8.58 us: pick(): return jnp.where(cond, first, second)]
    all_to_all x2 -> x0, starting transfers between devices: 8.42 us -> none  [the longest x1 5.85 us: tensor_layer(): lax.all_to_all(grad_down_half, 'ctx', 0, 0).transpose(1, 0, 2)]
    add x4 -> x0, other arithmetic: 7.14 us -> none  [the longest x3 5.54 us: pair_halves(): return keep + lax.ppermute(send, 'fsdp', [(0, 1), (1, 0)])]
  transfers between devices with their start and end apart: 19 -> 0, of which waited for: 5 -> 0; matrix products, arithmetic and copies ran while one was open for 9% -> 0% of each run, Pallas kernels for 39% -> 0%
where the time goes in v2:
time: 298 us
  Pallas kernels  268 us (90%)
  other arithmetic  18.9 us (6%)
  local copies, waits for them, and re-layouts  5.72 us (2%)
  matrix products  4.06 us (1%)
    pallas_call x3, Pallas kernels, run_kernel(): pl.pallas_call(body, out_shape=outs, in_specs=[anywhere if i in outside e...  268 us

profile of v2, /device:TPU:0, one launch (start us, length us, event | category | flops | bytes accessed | tf_op | source)
XLA Modules:
  0.0 297.8 jit_solution(7268179346486139012)
XLA Ops:
  0.7 1.2 convert_reduce_fusion
  1.9 1.2 fusion.12
  3.1 0.8 copy.18.down_mine
  4.1 1.9 fusion.6.act
  6.0 1.8 constant_dynamic-slice_fusion.1.in_mine
  7.8 2.6 fusion.16
  10.4 85.1 %attend_kernel.1 = (bf16[16,128,1024]{2,1,0:T(8,128)(2,1)}, bf16[16,128,1024]{2,1,0:T(8,128)(2,1)}, bf16[64,2048]{1,0:T(8,128)(2,1)}, bf16[64,2048]{1,0:T(8,128)...) custom-call(bf16[128,1024]{1,0:T(8,128)(2,1)} %fusion.6.act, ...), custom_call_target="tpu_custom_call" | custom-call | flops 10000000000 | bytes 20000000 | tf_op jit(solution)/shard_map/attend_kernel/pallas_call | solution.py:1075
  95.5 2.6 fusion.18
  98.1 0.2 multiply_reduce_fusion.1
  98.3 0.8 multiply_convert_fusion.act
  99.2 77.6 %feed_kernel.1 = (f32[128,1024]{1,0:T(8,128)}, bf16[8,128,1024]{2,1,0:T(8,128)(2,1)}, bf16[2,164,1024]{2,1,0:T(8,128)(2,1)}, bf16[32,32,256]{2,1,0:T(8,128)(2,1)}) custom-call(bf16[128,1024]{1,0:T(8,128)(2,1)} %multiply_convert_fusion.act, bf16[16,128,1024]{2,1,0:T(8,128)(2,1)} %get-tuple-element.35.cot_all, ...), custom_call_target="tpu_custom_call" | custom-call | flops 20000000000 | bytes 20000000 | tf_op jit(solution)/shard_map/feed_kernel/pallas_call | solution.py:1075
  176.8 1.4 multiply_reduce_fusion.3
  178.2 1.4 fusion.17
  179.6 1.5 convolution_convert_fusion
  181.1 105.6 %attend_back_kernel.1 = (f32[128,1024]{1,0:T(8,128)}, f32[128,1024]{1,0:T(8,128)}, f32[96,1024]{1,0:T(8,128)}, f32[32,1024]{1,0:T(8,128)}, f32[164,1024]{1,0:T(8...) custom-call(bf16[16,64,128]{2,1,0:T(8,128)(2,1)} %bitcast.53, bf16[128,1024]{1,0:T(8,128)(2,1)} %copy-done.3, ...), custom_call_target="tpu_custom_call" | custom-call | flops 20000000000 | bytes 20000000 | tf_op jit(solution)/shard_map/attend_back_kernel/pallas_call | solution.py:1075
  286.7 1.9 add_bitcast_fusion
  288.6 1.3 reduce.1
  290.0 1.3 reduce.2
  291.3 1.4 multiply_reduce_fusion.2
  292.7 2.1 fusion.11
  294.8 0.7 copy.23
  295.6 0.7 copy.24
  296.3 0.8 copy.25
  297.1 0.7 copy.26
  (33 shorter events, 0.2 us)
Async XLA Ops:
  0.6 2.5 copy-start
  10.4 85.1 %copy-start.2 = (bf16[1,128,1024]{2,1,0:T(8,128)(2,1)S(1)}, bf16[1,128,1024]{2,1,0:T(8,128)(2,1)}, u32[]{:S(2)}) copy-start(bf16[1,128,1024]{2,1,0:T(8,128)(2,1)} %param.8) | copy-start | bytes 786436
  95.5 2.8 copy-start.8
  99.2 77.6 %copy-start.9 = (f32[1024]{0:T(1024)S(1)}, f32[1024]{0:T(1024)}, u32[]{:S(2)}) copy-start(f32[1024]{0:T(1024)} %param.11) | copy-start | bytes 12292
  176.8 2.8 copy-start.1
  179.6 1.5 copy-start.3
  181.1 110.2 %copy-start.10 = (f32[1024]{0:T(1024)S(1)}, f32[1024]{0:T(1024)}, u32[]{:S(2)}) copy-start(f32[1024]{0:T(1024)} %param.10) | copy-start | bytes 12292
  291.3 3.5 %copy-start.5 = (f32[96,1024]{1,0:T(8,128)S(1)}, f32[96,1024]{1,0:T(8,128)}, u32[]{:S(2)}) copy-start(f32[96,1024]{1,0:T(8,128)} %get-tuple-element.80) | copy-start | bytes 1179652
  291.3 4.3 %copy-start.7 = (f32[32,1024]{1,0:T(8,128)S(1)}, f32[32,1024]{1,0:T(8,128)}, u32[]{:S(2)}) copy-start(f32[32,1024]{1,0:T(8,128)} %get-tuple-element.81) | copy-start | bytes 393220
  291.3 4.9 %copy-start.4 = (f32[164,1024]{1,0:T(8,128)S(1)}, f32[164,1024]{1,0:T(8,128)}, u32[]{:S(2)}) copy-start(f32[164,1024]{1,0:T(8,128)} %get-tuple-element.82) | copy-start | bytes 2015236
  292.7 4.4 %copy-start.6 = (f32[32,2624]{1,0:T(8,128)S(1)}, f32[32,2624]{1,0:T(8,128)}, u32[]{:S(2)}) copy-start(f32[32,2624]{1,0:T(8,128)} %get-tuple-element.83) | copy-start | bytes 1007620

commit v3 on v2

--- a/solution.py
+++ b/solution.py
@@ -463,9 +463,93 @@
             self.beside(at // 2, at % 2).wait_send()
 
 
+class Quad:
+    def __init__(self, place, buf, sems):
+        self.p, self.buf = place, buf
+        self.s, self.r = sems
+
+    @staticmethod
+    def sems():
+        return [pltpu.SemaphoreType.DMA((3,))] * 2
+
+    def over(self, x, to, at):
+        piece = self.buf.at[x * 2 + self.p.core]
+        return self.p.copy(piece, piece, self.s.at[at], self.r.at[at], to)
+
+    def across(self):
+        p = self.p
+        return self.over(p.x, p.slot(p.z, 1 - p.x, p.core), 0)
+
+    def beside(self):
+        p = self.p
+        return self.over(p.x, p.slot(p.z, p.x, 1 - p.core), 1)
+
+    def beside_next(self):
+        p = self.p
+        return self.over(1 - p.x, p.slot(p.z, p.x, 1 - p.core), 2)
+
+    def start(self):
+        self.across().start()
+        self.beside().start()
+
+    def relay(self):
+        self.across().wait_recv()
+        self.beside_next().start()
+
+    def sent(self):
+        self.across().wait_send()
+        self.beside().wait_send()
+        self.beside_next().wait_send()
+
+
+class QuadSum:
+    def __init__(self, place, whole, bufs, sems):
+        self.p, self.whole = place, whole
+        self.got, self.sums, self.far = bufs
+        self.s, self.r = sems
+
+    @staticmethod
+    def sems():
+        return [pltpu.SemaphoreType.DMA((3,))] * 2
+
+    @staticmethod
+    def bufs(block):
+        return [pltpu.VMEM((2,) + block, jnp.bfloat16)] * 2 + [pltpu.VMEM(block, jnp.bfloat16)]
+
+    def beside(self, x):
+        p = self.p
+        return p.copy(
+            self.whole.at[x * 2 + 1 - p.core], self.got.at[x], self.s.at[x], self.r.at[x],
+            p.slot(p.z, p.x, 1 - p.core),
+        )
+
+    def across(self):
+        p = self.p
+        return p.copy(
+            self.sums.at[1 - p.x], self.far, self.s.at[2], self.r.at[2], p.slot(p.z, 1 - p.x, p.core)
+        )
+
+    def add(self, x):
+        f32 = jnp.float32
+        self.beside(x).wait_recv()
+        self.sums[x] = (
+            self.whole[x * 2 + self.p.core].astype(f32) + self.got[x].astype(f32)
+        ).astype(self.sums.dtype)
+
+    def finish(self, out):
+        f32 = jnp.float32
+        self.across().wait_recv()
+        out[...] = self.sums[self.p.x].astype(f32) + self.far[...].astype(f32)
+
+    def sent(self):
+        self.beside(0).wait_send()
+        self.beside(1).wait_send()
+        self.across().wait_send()
+
+
 class Settle:
-    def __init__(self, place, sums, bufs, sems):
-        self.p, self.sums = place, sums
+    def __init__(self, place, sums, bufs, sems, pairwise=False):
+        self.p, self.sums, self.pairwise = place, sums, pairwise
         self.got, self.total, self.low, self.high = bufs
         self.x_s, self.x_r, self.up_s, self.up_r, self.dn_s, self.dn_r = sems
 
@@ -477,8 +561,16 @@
     def bufs(line, block):
         return [pltpu.VMEM((line,) + block, jnp.bfloat16)] * 4
 
+    def kept(self, z):
+        p = self.p
+        return p.pair * p.line + z if self.pairwise else z * 2 + p.x
+
     def across(self, z):
         p = self.p
+        if self.pairwise:
+            return p.over_pair(
+                self.sums.at[(1 - p.pair) * p.line + z], self.got.at[z], self.x_s.at[z], self.x_r.at[z]
+            )
         return p.copy(
             self.sums.at[z * 2 + 1 - p.x], self.got.at[z], self.x_s.at[z], self.x_r.at[z],
             p.slot(p.z, 1 - p.x, p.core),
@@ -498,7 +590,7 @@
         p, f32 = self.p, jnp.float32
         self.across(z).wait_recv()
         self.total[z] = (
-            self.sums[z * 2 + p.x].astype(f32) + self.got[z].astype(f32)
+            self.sums[self.kept(z)].astype(f32) + self.got[z].astype(f32)
         ).astype(self.total.dtype)
 
         @pl.when(z > p.z)
@@ -521,17 +613,18 @@
 
     def finish(self, out):
         p, f32 = self.p, jnp.float32
-        out[...] = self.total[p.z].astype(f32)
-
         @pl.when(p.z > 0)
         def _():
             self.up(p.z).wait_recv()
-            out[...] += self.low[p.z].astype(f32)
 
         @pl.when(p.z < p.line - 1)
         def _():
             self.down(p.z).wait_recv()
-            out[...] += self.high[p.z].astype(f32)
+
+        total = self.total[p.z].astype(f32)
+        total += jnp.where(p.z > 0, self.low[p.z].astype(f32), 0.0)
+        total += jnp.where(p.z < p.line - 1, self.high[p.z].astype(f32), 0.0)
+        out[...] = total.astype(out.dtype)
 
     def sent(self):
         p = self.p
@@ -653,19 +746,21 @@
             p.to_owner(self.src.at[0], self.dst.at[slot], self.s.at[0], self.r.at[slot], source).wait_recv()
 
 
-def turn(value):
+def rotate_rows(value, cos, sine):
     half = value.shape[0] // 2
-    return jnp.concatenate([-value[half:], value[:half]], axis=0)
-
-
-def turn_back(value):
-    half = value.shape[0] // 2
-    return jnp.concatenate([value[half:], -value[:half]], axis=0)
+    first, second = value[:half], value[half:]
+    return jnp.concatenate([first * cos - second * sine, second * cos + first * sine], axis=0)
+
+
+def rotate_rows_back(grad, cos, sine):
+    half = grad.shape[0] // 2
+    first, second = grad[:half], grad[half:]
+    return jnp.concatenate([first * cos + second * sine, second * cos - first * sine], axis=0)
 
 
 def attend_kernel(
-    count, act, cot, qkv_weight, in_mine, down_mine, out_mine, cos, sine,
-    act_all, cot_all, query_t, keys_t, keys, values, mixed_own, log_sum, mixed, weight, in_pair, down_pair, out_pair,
+    count, act, cot, qkv_weight, in_weight, down_mine, out_mine, cos, sine,
+    act_all, cot_all, query_t, keys_t, keys, values, mixed_own, log_sum, mixed, weight, in_other, down_other, out_pair,
     values_t, load_sem, part_sem, part_got, piece_sem, piece_got, *sems
 ):
     f32, bf16 = jnp.float32, jnp.bfloat16
@@ -674,10 +769,11 @@
     width = count * head
     n = 8
     first = Gather(p, act_all, sems[:n])
-    second = Gather(p, cot_all, sems[n : 2 * n])
-    trade = Exchange(p, mixed_own, mixed, sems[2 * n :])
-    pieces = [(in_mine, in_pair), (down_mine, down_pair), (out_mine, out_pair)]
-    loads = [(act, act_all.at[p.me]), (cot, cot_all.at[p.me])] + [(src, dst.at[p.pair]) for src, dst in pieces]
+    second = Quad(p, cot_all, sems[n : n + 2])
+    trade = Exchange(p, mixed_own, mixed, sems[n + 2 :])
+    half = out_mine.shape[0] // 2
+    part_half = pl.ds(pl.multiple_of(p.core * half, half), half)
+    loads = [(act, act_all.at[p.me]), (cot, cot_all.at[p.x * 2 + p.core]), (out_mine, out_pair.at[p.pair])]
     loads = [pltpu.make_async_copy(src, dst, load_sem.at[i]) for i, (src, dst) in enumerate(loads)]
     for load in loads:
         load.start()
@@ -692,13 +788,25 @@
         here, src = part_rows(part)
         return (
             here,
-            pltpu.make_async_copy(src, weight.at[part], load_sem.at[5 + part]),
+            pltpu.make_async_copy(src, weight.at[part], load_sem.at[3 + part]),
             p.over_pair(src, weight.at[part], part_sem.at[part], part_got.at[part]),
         )
 
+    units, columns, down_rows = in_other.shape[0], in_other.shape[1] // 2, down_other.shape[0] // 2
+    in_rows = pl.ds(pl.multiple_of((p.x * 2 + p.core) * units, 16), units)
+    in_cols = pl.ds(pl.multiple_of(p.z % 2 * columns, columns), columns)
+    down_part = pl.ds(pl.multiple_of(p.z % 2 * down_rows, down_rows), down_rows)
+    in_here, down_here = in_other.at[:, in_cols], down_other.at[down_part]
     swaps = [
-        p.over_pair(src, dst.at[p.pair], piece_sem.at[i], piece_got.at[i]) for i, (src, dst) in enumerate(pieces)
+        p.over_pair(out_mine.at[part_half], out_pair.at[p.pair, part_half], piece_sem.at[0], piece_got.at[0]),
+        p.over_pair(in_weight.at[in_rows, in_cols], in_here, piece_sem.at[1], piece_got.at[1]),
+        p.over_pair(down_mine.at[down_part], down_here, piece_sem.at[2], piece_got.at[2]),
     ]
+    next_z = p.me + 4 - p.z % 2 * 8
+    in_share = p.copy(in_here, in_here, piece_sem.at[4], piece_got.at[4], next_z)
+    down_share = p.copy(down_here, down_here, piece_sem.at[5], piece_got.at[5], next_z)
+    out_rest = out_pair.at[1 - p.pair, part_half]
+    share = p.copy(out_rest, out_rest, piece_sem.at[3], piece_got.at[3], p.slot(p.z, p.x, 1 - p.core))
     for part in range(3):
         here, own, away = part_copies(part)
 
@@ -739,8 +847,8 @@
         packed = matmul(head_weight, act_all[at], 1, 1)
         c, s = cos[:, lanes], sine[:, lanes]
         query, key = packed[:head], packed[head : 2 * head]
-        query_t[:, lanes] = (query * c + turn(query) * s).astype(bf16)
-        key = key * c + turn(key) * s
+        query_t[:, lanes] = rotate_rows(query, c, s).astype(bf16)
+        key = rotate_rows(key, c, s)
         keys_t[:, lanes] = key.astype(bf16)
         values_t[:, lanes] = packed[2 * head :].astype(bf16)
         keys[lanes, :] = key.T.astype(bf16)
@@ -752,11 +860,7 @@
     def _(at):
         first.part(at, project)
 
-    def gather_more(step):
-        for part in range(4):
-            second.part(step * 4 + part)
-
-    gather_more(0)
+    second.start()
     wide = 2 * rows
     blocks = count // 2
     scale = head ** (-0.5)
@@ -779,16 +883,21 @@
     def _(i):
         attend(i)
 
-    gather_more(1)
+    second.relay()
+    swaps[0].wait_recv()
+    share.start()
 
     @pl.loop(blocks // 2, blocks)
     def _(i):
         attend(i)
 
-    for step in range(2, p.line):
-        gather_more(step)
+    swaps[1].wait_recv()
+    in_share.start()
     trade.arrived()
-    gather_more(p.line)
+    second.beside().wait_recv()
+    second.beside_next().wait_recv()
+    swaps[2].wait_recv()
+    down_share.start()
     first.sent()
     second.sent()
     trade.sent()
@@ -800,139 +909,144 @@
             away.wait_send()
 
     for swap in swaps:
-        swap.wait()
+        swap.wait_send()
+    share.wait()
+    in_share.wait()
+    down_share.wait()
 
 
 def feed_kernel(
-    count, act, cot_all, in_pair, down_pair, gain,
-    grad_act, out_sums, in_grad, down_grad,
-    weight, down, grad_weight, grad_down,
-    act_all, gated, inner_grad, grad_part, out_part, grad_got, grad_sums, out_got, load_sem, *rest
+    count, act, cot_all, in_weight, in_other, down_mine, down_other, gain,
+    grad_act, out_total, in_grad, down_grad,
+    weight, down, act_all, gated, inner_grad, grad_part, out_part, load_sem, *rest
 ):
     f32, bf16 = jnp.float32, jnp.bfloat16
     p = Place(count)
     rows, group = act.shape[0], down.shape[1]
-    bufs, sems = rest[:4], rest[4:]
-    gather = Gather(p, act_all, sems[:8])
-    halve = Halve(p, grad_part, grad_got, grad_sums, sems[8:10])
-    settle = Settle(p, grad_sums, bufs, sems[10:16])
-    halve_out = Halve(p, out_part, out_got, out_sums, sems[16:18])
-    load = pltpu.make_async_copy(act, act_all.at[p.me], load_sem)
+    gather = Quad(p, act_all, rest[:2])
+    grad_sum = QuadSum(p, grad_part, rest[2:5], rest[8:10])
+    out_sum = QuadSum(p, out_part, rest[5:8], rest[10:12])
+    units, half = in_other.shape[0], down_other.shape[0]
+    in_rows = pl.ds(pl.multiple_of((p.x * 2 + p.core) * units, 16), units)
+    own_at = pl.ds(pl.multiple_of(p.pair * group, group), units)
+    other_at = pl.ds(pl.multiple_of((1 - p.pair) * group, group), units)
+    load = pltpu.make_async_copy(act, act_all.at[p.x * 2 + p.core], load_sem.at[0])
+    weights = [
+        pltpu.make_async_copy(in_weight.at[in_rows], weight.at[own_at], load_sem.at[1]),
+        pltpu.make_async_copy(in_other, weight.at[other_at], load_sem.at[2]),
+    ]
     load.start()
-    units, half = in_pair.shape[1], down_pair.shape[1]
-    weight[...] = jnp.zeros_like(weight)
-    down[...] = jnp.zeros_like(down)
-    for at in range(2):
-        weight[at * group : at * group + units, :] = in_pair[at]
-        down[at * half : (at + 1) * half, :units] = down_pair[at]
+    for copy in weights:
+        copy.start()
     p.meet()
     load.wait()
-
-    def feed(z, x, core):
-        at = p.slot(z, x, core)
-        inner = matmul(act_all[at], weight[...], 1, 1)
-        grad_gated = matmul(cot_all[at], down[...], 1, 0)
+    gather.start()
+    down[...] = jnp.zeros_like(down)
+    down[pl.ds(pl.multiple_of(p.pair * half, half), half), :units] = down_mine[...]
+    down[pl.ds(pl.multiple_of((1 - p.pair) * half, half), half), :units] = down_other[...]
+    for at in range(2):
+        weight[at * group + units : (at + 1) * group, :] = jnp.zeros((group - units, weight.shape[1]), bf16)
+    for copy in weights:
+        copy.wait()
+    gather.beside().wait_recv()
+
+    @pl.loop(0, 2)
+    def _(step):
+        x = jnp.where(step == 0, p.x, 1 - p.x)
+
+        @pl.when(step == 1)
+        def _():
+            gather.relay()
+            gather.beside_next().wait_recv()
+
+        acts = jnp.concatenate([act_all[2 * x], act_all[2 * x + 1]], axis=0)
+        cots = jnp.concatenate([cot_all[2 * x], cot_all[2 * x + 1]], axis=0)
+        inner = matmul(acts, weight[...], 1, 1)
+        grad_gated = matmul(cots, down[...], 1, 0)
         value, gate = inner[:, :group], inner[:, group:]
         gelu_val, gelu_slope = gelu_pair(value)
-        token = pl.ds(pl.multiple_of(at * rows, rows), rows)
+        token = pl.ds(pl.multiple_of(x * 2 * rows, 2 * rows), 2 * rows)
         out = (gelu_val * gate).astype(bf16)
         gated[token, :] = out
         grads = jnp.concatenate(
             [grad_gated * gate * gelu_slope, grad_gated * gelu_val], axis=1
         ).astype(bf16)
         inner_grad[token, :] = grads
-        grad_part[at] = matmul(grads, weight[...], 1, 0).astype(bf16)
-
-        @pl.when(core != p.core)
-        def _():
-            halve.beside(z, x).start()
-
-        out_part[at] = matmul(out, down[...], 1, 1).astype(bf16)
-
-        @pl.when(core != p.core)
-        def _():
-            halve_out.beside(z, x).start()
-
-    @pl.loop(0, 4 * p.line + 4)
-    def _(at):
-        gather.part(at, feed)
-
-    @pl.loop(0, p.line)
-    def _(step):
-        z = p.far(step)
-        halve.add(z)
-        settle.across(z).start()
-
-    def grad_chunk(step):
-        token = pl.ds(pl.multiple_of(step * 4 * rows, 4 * rows), 4 * rows)
-        acts = jnp.concatenate([act_all[4 * step + i] for i in range(4)], axis=0)
-        cots = jnp.concatenate([cot_all[4 * step + i] for i in range(4)], axis=0)
-        return matmul(inner_grad[token, :], acts, 0, 0), matmul(cots, gated[token, :], 0, 0)
-
-    grad_weight[...], grad_down[...] = grad_chunk(0)
-
-    @pl.loop(0, p.line)
-    def _(step):
-        settle.pass_on(p.far(step))
-
-        @pl.when(step > 0)
-        def _():
-            more = grad_chunk(step)
-            grad_weight[...] += more[0]
-            grad_down[...] += more[1]
-
-        halve_out.add(step)
-
+        part = matmul(grads, weight[...], 1, 0).astype(bf16)
+        grad_part[2 * x], grad_part[2 * x + 1] = part[:rows], part[rows:]
+        grad_sum.beside(x).start()
+        part = matmul(out, down[...], 1, 1).astype(bf16)
+        out_part[2 * x], out_part[2 * x + 1] = part[:rows], part[rows:]
+        out_sum.beside(x).start()
+
+    grad_sum.add(1 - p.x)
+    grad_sum.across().start()
+    grad_sum.add(p.x)
+    out_sum.add(1 - p.x)
+    out_sum.across().start()
+    out_sum.add(p.x)
+    acts = act_all[...].reshape(4 * rows, act.shape[1])
+    cots = cot_all[...].reshape(4 * rows, act.shape[1])
+    quarter = units // 4
+    gain_row = jnp.zeros((1, act.shape[1]), f32)
     for at in range(2):
-        in_grad[at] = grad_weight[at * group : at * group + units, :].astype(bf16)
-    gain_row = jnp.sum(grad_weight[...] * weight[...].astype(f32), axis=0, keepdims=True) / gain[...]
-    lane = lax.broadcasted_iota(jnp.int32, grad_down.shape, 1)
+        piece = matmul(inner_grad[:, at * group : (at + 1) * group], acts, 0, 0)
+        gain_row += jnp.sum(piece * weight[at * group : (at + 1) * group, :].astype(f32), axis=0, keepdims=True)
+        for k in range(4):
+            in_grad[k % 2 * p.line + at * 2 + k // 2] = piece[k * quarter : (k + 1) * quarter].astype(bf16)
+    piece = matmul(cots, gated[...], 0, 0)
+    lane = lax.broadcasted_iota(jnp.int32, piece.shape, 1)
+    gain_row = gain_row / gain[...]
     column = jnp.broadcast_to(gain_row, (8, gain_row.shape[1])).T[:, :1]
-    down_grad[...] = jnp.where(lane == units, column, grad_down[...]).astype(bf16).reshape(down_grad.shape)
-    settle.finish(grad_act)
+    piece = jnp.where(lane == units, column, piece).astype(bf16)
+    unit = act.shape[1] // (2 * count)
+    for z in range(p.line):
+        for r in range(4):
+            for y in range(2):
+                start = ((z * 4 + r) * 2 + y) * unit
+                down_grad[y * p.line + z, r] = piece[start : start + unit]
+    grad_sum.finish(grad_act)
+    out_sum.finish(out_total)
     gather.sent()
-    halve.sent()
-    halve_out.sent()
-    settle.sent()
+    grad_sum.sent()
+    out_sum.sent()
 
 
 def attend_back_kernel(
-    count, grad_mixed, grad_mid, mixed, out_sums, query_t, keys_t, keys, values, mixed_own, log_sum,
+    count, grad_mixed, grad_mid, mixed, query_t, keys_t, keys, values, mixed_own, log_sum,
     act_all, weight, cos, sine, in_grad, down_grad, gain,
-    grad_act, out_total, qkv_out, out_out, in_out, down_out, gain_m_out, gain_a_out,
+    grad_act, qkv_out, out_out, in_out, down_out, gain_m_out, gain_a_out,
     grad_own, grad_keys, grad_values, grad_packed, grad_part, grad_got, grad_sums, grad_weight,
-    pair_part, pair_got, proj_part, proj_got, proj_sums, in_got, down_got, qkv_part, qkv_got, gain_part, gain_got,
-    pair_s, pair_r, in_s, in_r, qkv_s, qkv_r, *rest
+    pair_part, pair_core, pair_sums, pair_got, proj_sums, in_sum, in_got, down_sum, down_got,
+    qkv_part, qkv_got, gain_part, gain_got,
+    pair_s, pair_r, in_s, in_r, down_s, down_r, qkv_s, qkv_r, *rest
 ):
     f32, bf16 = jnp.float32, jnp.bfloat16
     p = Place(count)
     rows, head = grad_mixed.shape[2], keys_t.shape[0]
     width, unit = count * head, head // 2
-    bufs, out_bufs, proj_bufs, sems = rest[:4], rest[4:8], rest[8:12], rest[12:]
+    bufs, proj_bufs, in_bufs, down_bufs, sems = rest[:4], rest[4:8], rest[8:12], rest[12:16], rest[16:]
     trade = Exchange(p, grad_mixed, grad_own, sems[:2])
     halve = Halve(p, grad_part, grad_got, grad_sums, sems[2:4])
     settle = Settle(p, grad_sums, bufs, sems[4:10])
-    settle_out = Settle(p, out_sums, out_bufs, sems[10:16])
-    halve_proj = Halve(p, proj_part, proj_got, proj_sums, sems[16:18])
-    settle_proj = Settle(p, proj_sums, proj_bufs, sems[18:24])
-    spread_down = Spread(p, down_grad, down_got, sems[24:26])
-    spread_gain = Spread(p, gain_part, gain_got, sems[26:28])
-    give_in = Deliver(p, in_grad, in_got, (in_s, in_r))
+    halve_proj = Halve(p, pair_part, pair_core, pair_sums, sems[10:12])
+    settle_proj = Settle(p, proj_sums, proj_bufs, sems[12:18])
+    settle_in = Settle(p, in_grad, in_bufs, sems[18:24], True)
+    settle_down = Settle(p, down_grad, down_bufs, sems[24:30], True)
+    spread_gain = Spread(p, gain_part, gain_got, sems[30:32])
+    give_in = Deliver(p, in_sum, in_got, (in_s, in_r))
+    give_down = Deliver(p, down_sum, down_got, (down_s, down_r))
     give_qkv = Deliver(p, qkv_part, qkv_got, (qkv_s, qkv_r))
-    swap = p.over_pair(pair_part.at[1 - p.pair], pair_got, pair_s, pair_r)
+
+    def swap(at):
+        return p.over_pair(pair_sums.at[at, 1 - p.pair], pair_got.at[at], pair_s.at[at], pair_r.at[at])
+
     p.meet(True)
 
     @pl.loop(0, count)
     def _(shift):
         trade.send((p.me + shift) % count)
 
-    @pl.loop(0, p.line)
-    def _(step):
-        settle_out.across(p.far(step)).start()
-
-    for part in range(2):
-        give_in.send(part, part * count + p.me, p.pair)
-    spread_down.send()
     flat = mixed[...].reshape(width, rows)
 
     @pl.loop(0, count // 2)
@@ -940,9 +1054,24 @@
         lanes = pl.ds(pl.multiple_of(i * 4 * unit, 4 * unit), 4 * unit)
         piece = matmul(grad_mid[:, lanes], flat, 0, 1).astype(bf16)
         for at in range(4):
-            pair_part[at % 2, 2 * i + at // 2] = piece[at * unit : (at + 1) * unit]
-
-    swap.start()
+            pair_part[2 * i + at // 2, at % 2] = piece[at * unit : (at + 1) * unit]
+
+    @pl.loop(0, 2 * p.line)
+    def _(at):
+        halve_proj.beside(at // 2, at % 2).start()
+
+    @pl.loop(0, p.line)
+    def _(step):
+        z = p.far(step)
+        halve_proj.add(z)
+        swap(2 * z).start()
+        swap(2 * z + 1).start()
+
+    @pl.loop(0, p.line)
+    def _(step):
+        settle_in.across(p.far(step)).start()
+        settle_down.across(p.far(step)).start()
+
     grad_keys[...] = jnp.zeros_like(grad_keys)
     grad_values[...] = jnp.zeros_like(grad_values)
     trade.arrived()
@@ -962,21 +1091,31 @@
         grad_scores = (probs * (grad_probs - delta)).astype(bf16)
         grad_keys[...] += matmul(grad_scores, query, 1, 1)
         grad_query = matmul(keys_t[...], grad_scores, 1, 0) * scale
-        back_query = grad_query * cos[:, lanes] + turn_back(grad_query * sine[:, lanes])
+        back_query = rotate_rows_back(grad_query, cos[:, lanes], sine[:, lanes])
         grad_packed[:head, lanes] = back_query.astype(bf16)
 
     @pl.loop(0, count // 2)
     def _(i):
         back(i)
 
+        @pl.when(i == count // 4)
+        def _():
+            settle_in.pass_on(p.far(0))
+            settle_down.pass_on(p.far(0))
+
     @pl.loop(0, p.line)
     def _(step):
-        settle_out.pass_on(p.far(step))
-
-    swap.wait_recv()
-    proj_part[...] = (pair_part[p.pair].astype(f32) + pair_got[...].astype(f32)).astype(bf16)
+        z = p.far(step)
+        for x in range(2):
+            at = 2 * z + x
+            swap(at).wait_recv()
+            proj_sums[at] = (pair_sums[at, p.pair].astype(f32) + pair_got[at].astype(f32)).astype(bf16)
+        settle_proj.across(z).start()
+
+    settle_in.pass_on(p.far(1))
+    settle_down.pass_on(p.far(1))
     grad_key = grad_keys[...].T * scale
-    grad_packed[head : 2 * head, :] = (grad_key * cos[...] + turn_back(grad_key * sine[...])).astype(bf16)
+    grad_packed[head : 2 * head, :] = rotate_rows_back(grad_key, cos[...], sine[...]).astype(bf16)
     grad_packed[2 * head :, :] = grad_values[...].T.astype(bf16)
 
     @pl.loop(0, p.line)
@@ -991,8 +1130,6 @@
     @pl.loop(0, p.line)
     def _(step):
         z = p.far(step)
-        halve_proj.beside(z, 0).start()
-        halve_proj.beside(z, 1).start()
         halve.add(z)
         settle.across(z).start()
 
@@ -1010,7 +1147,9 @@
     for at in range(6):
         qkv_part[at] = grad_weight[at * unit : (at + 1) * unit, :].astype(bf16)
     gain_row = jnp.sum(grad_weight[...] * weight[...].astype(f32), axis=0, keepdims=True) / gain[...]
-    gain_part[...] = jnp.broadcast_to(gain_row, (128, width)).T.astype(bf16).reshape(gain_part.shape)
+    for at in range(2 * count):
+        chunk = at * unit // 128 * 128
+        gain_part[at] = gain_row[:, chunk : chunk + 128]
 
     def unit_of(at):
         return (at // 2) * 2 * count + 2 * p.me + at % 2
@@ -1018,12 +1157,6 @@
     for at in range(6):
         give_qkv.send(at, unit_of(at) // 3, unit_of(at) % 3 * 2 + p.pair)
     spread_gain.send()
-
-    @pl.loop(0, p.line)
-    def _(step):
-        z = p.far(step)
-        halve_proj.add(z)
-        settle_proj.across(z).start()
 
     @pl.loop(0, p.line)
     def _(step):
@@ -1031,52 +1164,70 @@
         settle.pass_on(z)
         settle_proj.pass_on(z)
 
-    for side in range(2):
-        give_in.arrived(side, p.owner % count * 2 + side)
-    in_out[...] = in_got[0].astype(f32) + in_got[1].astype(f32)
-    spread_down.arrived()
+        @pl.when(step > 1)
+        def _():
+            settle_in.pass_on(z)
+            settle_down.pass_on(z)
+
     units = in_out.shape[0]
-    gain_m = jnp.zeros((unit, down_got.shape[2]), f32)
-    for at in range(count):
-        block = down_got[2 * at].astype(f32) + down_got[2 * at + 1].astype(f32)
-        down_out[:, at * units : (at + 1) * units] = block[:, :units]
-        gain_m += block
-    gain_m_out[...] = gain_m[:, units : units + 1]
-    settle_out.finish(out_total)
+    r = p.x * 2 + p.core
+    piece_owner = p.z // 2 * count + r * 4 + p.z % 2 * 2 + p.pair
+    settle_in.finish(in_sum.at[0])
+    give_in.send(0, piece_owner, 0)
+    settle_down.finish(down_sum)
+    for at in range(4):
+        give_down.send(at, (p.z * 4 + at) * 2 + p.pair, r)
     for slot in range(3):
         source = (3 * p.owner + slot) % (2 * count) // 2 * 2
         for side in range(2):
             give_qkv.arrived(2 * slot + side, source + side)
         qkv_out[slot * unit : (slot + 1) * unit, :] = qkv_got[2 * slot].astype(f32) + qkv_got[2 * slot + 1].astype(f32)
     spread_gain.arrived()
-    gain_a = jnp.zeros(gain_got.shape[1:], f32)
-    for at in range(2 * count):
-        gain_a += gain_got[at].astype(f32)
-    gain_a_out[...] = gain_a[:, :1]
+    gain_a = gain_got[0]
+    for at in range(1, 2 * count):
+        gain_a += gain_got[at]
+    gain_a_out[...] = gain_a
     settle_proj.finish(out_out)
     settle.finish(grad_act)
+    half, r_of, k_of = p.owner // count, p.owner % count // 4, p.owner % 4
+    source_in = ((half * 2 + k_of // 2) * 4 + r_of) * 2 + k_of % 2
+    give_in.arrived(0, source_in)
+    in_out[...] = in_got[0].astype(f32)
+    gain_m = jnp.zeros((unit, 1), f32)
+    group = 4 * units
+    for at in range(4):
+        give_down.arrived(at, (p.z * 4 + at) * 2 + p.pair)
+        block = down_got[at].astype(f32)
+        down_out[:, at * group : (at + 1) * group] = block[:, :group]
+        gain_m += block[:, group : group + 1]
+    gain_m_out[...] = jnp.broadcast_to(gain_m, (unit, 128)).T[:1]
     trade.sent()
     halve.sent()
     settle.sent()
-    settle_out.sent()
     halve_proj.sent()
     settle_proj.sent()
-    spread_down.sent()
+    settle_in.sent()
+    settle_down.sent()
     spread_gain.sent()
-    swap.wait_send()
-    for part in range(2):
-        give_in.sent(part, part * count + p.me, p.pair)
+
+    @pl.loop(0, 2 * p.line)
+    def _(at):
+        swap(at).wait_send()
+
+    give_in.sent(0, piece_owner, 0)
+    for at in range(4):
+        give_down.sent(at, (p.z * 4 + at) * 2 + p.pair, r)
     for at in range(6):
         give_qkv.sent(at, unit_of(at) // 3, unit_of(at) % 3 * 2 + p.pair)
 
 
-def run_kernel(body, outs, scratch, collective, flops, args, outside=()):
+def run_kernel(body, outs, scratch, collective, flops, args, outside=(), outs_outside=()):
     vmem, anywhere = pl.BlockSpec(memory_space=pltpu.VMEM), pl.BlockSpec(memory_space=pl.ANY)
     return pl.pallas_call(
         body,
         out_shape=outs,
         in_specs=[anywhere if i in outside else vmem for i in range(len(args))],
-        out_specs=[vmem] * len(outs),
+        out_specs=[anywhere if i in outs_outside else vmem for i in range(len(outs))],
         scratch_shapes=scratch,
         compiler_params=pltpu.CompilerParams(
             collective_id=collective, has_side_effects=True, vmem_limit_bytes=VMEM_LIMIT
@@ -1090,50 +1241,49 @@
     return jax.ShapeDtypeStruct(shape, kind)
 
 
-def attend(count, head, act, cot, qkv_weight, in_mine, down_mine, out_mine, cos, sine):
+def attend(count, head, act, cot, qkv_weight, in_weight, down_mine, out_mine, cos, sine):
     bf16, f32 = jnp.bfloat16, jnp.float32
     rows, width = act.shape
     length, line = rows * count, count // 4
     blocks = shaped((count, rows, width), bf16)
     tall, flat = shaped((head, length), bf16), shaped((length, head), bf16)
     heads = shaped((count, head, rows), bf16)
-    pairs = [shaped((2,) + part.shape, bf16) for part in (in_mine, down_mine, out_mine)]
-    three = pltpu.SemaphoreType.DMA((3,))
+    pairs = [shaped((in_weight.shape[0] // 4, width), bf16), shaped(down_mine.shape, bf16), shaped((2,) + out_mine.shape, bf16)]
+    three, six = pltpu.SemaphoreType.DMA((3,)), pltpu.SemaphoreType.DMA((6,))
     return run_kernel(
         functools.partial(attend_kernel, count),
-        [blocks, blocks, tall, tall, flat, flat, heads, shaped((1, length), f32), heads, shaped((3, head, width), bf16)]
+        [blocks, shaped((4, rows, width), bf16), tall, tall, flat, flat, heads, shaped((1, length), f32), heads, shaped((3, head, width), bf16)]
         + pairs,
-        [pltpu.VMEM((head, length), bf16), pltpu.SemaphoreType.DMA((8,))] + [three] * 4
-        + Gather.sems(line) * 2 + Exchange.sems(count),
-        0, 10_000_000_000, [act, cot, qkv_weight, in_mine, down_mine, out_mine, cos, sine], (2, 5),
-    )
-
-
-def feed(count, group, act, cot_all, in_pair, down_pair, gain):
+        [pltpu.VMEM((head, length), bf16), pltpu.SemaphoreType.DMA((6,))] + [three, three, six, six]
+        + Gather.sems(line) + Quad.sems() + Exchange.sems(count),
+        0, 10_000_000_000, [act, cot, qkv_weight, in_weight, down_mine, out_mine, cos, sine], (2, 3, 4, 5), (10, 11),
+    )
+
+
+def feed(count, group, act, cot_all, in_weight, in_other, down_mine, down_other, gain):
     bf16, f32 = jnp.bfloat16, jnp.float32
     rows, width = act.shape
-    length, line = rows * count, count // 4
     block = (rows, width)
-    whole, half = pltpu.VMEM((count,) + block, bf16), pltpu.VMEM((2 * line,) + block, bf16)
+    units, line, unit = in_other.shape[0], count // 4, width // (2 * count)
+    whole = pltpu.VMEM((4,) + block, bf16)
     return run_kernel(
         functools.partial(feed_kernel, count),
-        [shaped(block, f32), shaped((2 * line,) + block, bf16), shaped(in_pair.shape, bf16),
-         shaped((2 * count, width // (2 * count), group), bf16)],
+        [shaped(block, f32), shaped(block, f32), shaped((2 * line, units // 4, width), bf16),
+         shaped((2 * line, 4, unit, group), bf16)],
         [pltpu.VMEM((2 * group, width), bf16), pltpu.VMEM((width, group), bf16),
-         pltpu.VMEM((2 * group, width), f32), pltpu.VMEM((width, group), f32),
-         whole, pltpu.VMEM((length, group), bf16), pltpu.VMEM((length, 2 * group), bf16), whole, whole,
-         half, half, half, pltpu.SemaphoreType.DMA]
-        + Settle.bufs(line, block)
-        + Gather.sems(line) + Halve.sems(line) + Settle.sems(line) + Halve.sems(line),
-        1, 20_000_000_000, [act, cot_all, in_pair, down_pair, gain],
-    )
-
-
-def attend_back(count, grad_mixed, grad_mid, mixed, out_sums, kept, act_all, weight, cos, sine, in_grad, down_grad, gain):
+         whole, pltpu.VMEM((4 * rows, group), bf16), pltpu.VMEM((4 * rows, 2 * group), bf16), whole, whole,
+         pltpu.SemaphoreType.DMA((3,))]
+        + Quad.sems() + QuadSum.bufs(block) * 2 + QuadSum.sems() * 2,
+        1, 20_000_000_000, [act, cot_all, in_weight, in_other, down_mine, down_other, gain], (2, 3),
+    )
+
+
+def attend_back(count, grad_mixed, grad_mid, mixed, kept, act_all, weight, cos, sine, in_grad, down_grad, gain):
     bf16, f32 = jnp.bfloat16, jnp.float32
     rows, width = act_all.shape[1:]
     head, length, line = weight.shape[0] // 3, rows * count, count // 4
     block, unit, units = (rows, width), head // 2, in_grad.shape[1]
+    down_block = down_grad.shape[1:]
     piece = (unit, width)
 
     def held(*shape):
@@ -1141,22 +1291,23 @@
 
     whole, half = held(count, *block), held(2 * line, *block)
     flat = pltpu.VMEM((length, head), f32)
-    two, six, one = pltpu.SemaphoreType.DMA((2,)), pltpu.SemaphoreType.DMA((6,)), pltpu.SemaphoreType.DMA
+    one, four, six, many = [pltpu.SemaphoreType.DMA((n,)) for n in (1, 4, 6, 2 * line)]
     return run_kernel(
         functools.partial(attend_back_kernel, count),
-        [shaped(block, f32), shaped(block, f32), shaped((3 * unit, width), f32), shaped(piece, f32),
-         shaped((units, width), f32), shaped((unit, units * count), f32), shaped((unit, 1), f32), shaped((unit, 1), f32)],
+        [shaped(block, f32), shaped((3 * unit, width), f32), shaped(piece, f32),
+         shaped((units, width), f32), shaped((unit, units * count), f32), shaped((1, unit), f32), shaped((1, 128), f32)],
         [held(count, head, rows), flat, flat, held(3 * head, length), whole, half, half,
          pltpu.VMEM((3 * head, width), f32),
-         held(2, count, *piece), held(count, *piece), held(count, *piece), held(2 * line, *piece), held(2 * line, *piece),
-         held(*in_grad.shape), held(*down_grad.shape), held(6, *piece), held(6, *piece),
-         held(2 * count, unit, 128), held(2 * count, unit, 128),
-         one, one, two, two, six, six]
-        + Settle.bufs(line, block) * 2 + Settle.bufs(line, piece)
-        + Exchange.sems(count) + Halve.sems(line) + Settle.sems(line) * 2
-        + Halve.sems(line) + Settle.sems(line) + Spread.sems(count) * 2,
+         held(count, 2, *piece), held(2 * line, 2, *piece), held(2 * line, 2, *piece), held(2 * line, *piece),
+         held(2 * line, *piece), held(1, units, width), held(1, units, width), held(*down_block), held(*down_block),
+         held(6, *piece), held(6, *piece), pltpu.VMEM((2 * count, 1, 128), f32), pltpu.VMEM((2 * count, 1, 128), f32),
+         many, many, one, one, four, four, six, six]
+        + Settle.bufs(line, block) + Settle.bufs(line, piece)
+        + Settle.bufs(line, (units, width)) + Settle.bufs(line, down_block)
+        + Exchange.sems(count) + (Halve.sems(line) + Settle.sems(line)) * 2
+        + Settle.sems(line) * 2 + Spread.sems(count),
         2, 20_000_000_000,
-        [grad_mixed, grad_mid, mixed, out_sums, *kept, act_all, weight, cos, sine, in_grad, down_grad, gain],
+        [grad_mixed, grad_mid, mixed, *kept, act_all, weight, cos, sine, in_grad, down_grad, gain],
     )
 
 
@@ -1170,40 +1321,45 @@
     rows, width = tokens.shape[1], tokens.shape[2]
     length = rows * count
     head_size = width // count
-    group = in_weight.shape[0] // count
+    quad = lax.rem(index, 4)
+    group = in_weight.shape[0] // 4
     padded = (group // 128 + 1) * 128
 
-    in_mine = lax.dynamic_slice_in_dim(in_weight, index * group, group, 0)
-    down_mine = lax.dynamic_slice_in_dim(down_weight, index * group, group, 1)
+    down_mine = lax.dynamic_slice_in_dim(down_weight, quad * group, group, 1)
 
     cos_table, sine_table = rope_tables(0, length, head_size)
-    cos_table, sine_table = cos_table[:, 0].T, sine_table[:, 0].T
+    cos_table, sine_table = cos_table[:, 0, : head_size // 2].T, sine_table[:, 0, : head_size // 2].T
     resid = tokens[0].astype(f32)
     normed_a, inv_a = normalize(resid)
     act_a = (normed_a * gain_attn).astype(bf16)
     cot_rows = cotangent[0]
-    act_all, cot_all, *kept, mixed, qkv_head, in_pair, down_pair, out_pair = attend(
-        count, head_size, act_a, cot_rows, qkv_weight, in_mine, down_mine, out_weight, cos_table, sine_table
+    act_all, cot_all, *kept, mixed, qkv_head, in_other, down_other, out_pair = attend(
+        count, head_size, act_a, cot_rows, qkv_weight, in_weight, down_mine, out_weight, cos_table, sine_table
     )
     qkv_head = qkv_head.reshape(3 * head_size, width)
     out_full = out_pair.reshape(width, width)
     middle = resid + matmul(mixed.reshape(width, rows), out_full, 0, 1)
     normed_m, inv_m = normalize(middle)
     act_m = (normed_m * gain_mlp).astype(bf16)
-    grad_act_m, out_sums, in_grad, down_grad = feed(count, padded, act_m, cot_all, in_pair, down_pair, gain_mlp[None])
+    grad_act_m, out_total, in_grad, down_grad = feed(
+        count, padded, act_m, cot_all, in_weight, in_other, down_mine, down_other, gain_mlp[None]
+    )
 
     grad_middle = cot_rows.astype(f32) + norm_back(grad_act_m * gain_mlp, normed_m, inv_m)
     grad_mid_bf = grad_middle.astype(bf16)
     grad_mixed = matmul(out_full, grad_mid_bf, 0, 1).astype(bf16).reshape(count, head_size, rows)
-    grad_act_a, out_total, grad_qkv, grad_out, grad_in, grad_down, grad_gain_m, grad_gain_a = attend_back(
-        count, grad_mixed, grad_mid_bf, mixed, out_sums, kept, act_all, qkv_head, cos_table, sine_table,
+    grad_act_a, grad_qkv, grad_out, grad_in, grad_down, grad_gain_m, grad_gain_a = attend_back(
+        count, grad_mixed, grad_mid_bf, mixed, kept, act_all, qkv_head, cos_table, sine_table,
         in_grad, down_grad, gain_attn[None],
     )
+    unit = width // (2 * count)
+    lane = lax.rem((index * 2 + lax.axis_index("fsdp")) * unit, 128)
+    grad_gain_a = lax.dynamic_slice_in_dim(grad_gain_a[0], lane, unit)
     output = middle + out_total
     grad_input = grad_middle + norm_back(grad_act_a * gain_attn, normed_a, inv_a)
     return (
         output[None], grad_input[None], grad_qkv, grad_out, grad_in, grad_down,
-        grad_gain_a.reshape(-1), grad_gain_m.reshape(-1),
+        grad_gain_a, grad_gain_m[0],
     )
 
 

time: 298 us -> 257 us (0.86); the launches traced: 298 us -> 253 us
  Pallas kernels: 268 us -> 227 us
  other arithmetic: 18.9 us -> 14.9 us
    pallas_call x3, Pallas kernels: 268 us -> 227 us  [run_kernel(): pl.pallas_call(body, out_shape=outs, in_specs=[anywhere if i in outside e...]
where the time goes in v3:
time: 257 us; the launch traced here: 253 us
  Pallas kernels  227 us (88%)
  other arithmetic  14.9 us (6%)
  local copies, waits for them, and re-layouts  6.1 us (2%)
  matrix products  4.06 us (2%)
    pallas_call x3, Pallas kernels, run_kernel(): pl.pallas_call(body, out_shape=outs, in_specs=[anywhere if i in outside e...  227 us

profile of v3, /device:TPU:0, one launch (start us, length us, event | category | flops | bytes accessed | tf_op | source)
XLA Modules:
  0.0 252.8 jit_solution(4158548073523648167)
XLA Ops:
  0.6 0.0 copy-start
  0.7 1.2 convert_reduce_fusion
  1.9 1.2 fusion.12
  3.1 0.1 multiply_bitcast_fusion
  3.2 1.9 fusion.6.act
  5.1 2.4 fusion.17
  7.6 1.2 copy.17.down_mine
  8.8 84.6 %attend_kernel.1 = (bf16[16,128,1024]{2,1,0:T(8,128)(2,1)}, bf16[4,128,1024]{2,1,0:T(8,128)(2,1)}, bf16[64,2048]{1,0:T(8,128)(2,1)}, bf16[64,2048]{1,0:T(8,128)(...) custom-call(bf16[128,1024]{1,0:T(8,128)(2,1)} %fusion.6.act, ...), custom_call_target="tpu_custom_call" | custom-call | flops 10000000000 | bytes 20000000 | tf_op jit(solution)/shard_map/attend_kernel/pallas_call | solution.py:1226
  93.4 2.6 %fusion.19 = (f32[128]{0:T(128)S(1)}, f32[128,1024]{1,0:T(8,128)S(1)}) fusion(bf16[1024,128]{1,0:T(8,128)(2,1)} %bitcast.64, bf16[1024,1024]{1,0:T(8,128)(2,1)} %bitcast.60, bf16[1,128,1024]{2,1,0:T(8,128)(2,1)S(1)} %copy-done.2), kind=kOutput, calls=%fused_computation.47 | convolution fusion | flops 268828544 | bytes 3146240 | tf_op jit(solution)/shard_map/dot_general | solution.py:270
  96.0 0.2 multiply_reduce_fusion.1
  96.2 0.8 multiply_convert_fusion.act
  97.1 34.4 %feed_kernel.1 = (f32[128,1024]{1,0:T(8,128)}, f32[128,1024]{1,0:T(8,128)}, bf16[8,164,1024]{2,1,0:T(8,128)(2,1)}, bf16[8,4,32,768]{3,2,1,0:T(8,128)(2,1)}) custom-call(bf16[128,1024]{1,0:T(8,128)(2,1)} %multiply_convert_fusion.act, bf16[4,128,1024]{2,1,0:T(8,128)(2,1)} %get-tuple-element.34.cot_all, bf16[2624,1024]{1,0:T(8,128)(2,1)} %in_weight.3, ...), custom_call_target="tpu_custom_call" | custom-call | flops 20000000000 | bytes 20000000 | tf_op jit(solution)/shard_map/feed_kernel/pallas_call | solution.py:1226
  131.5 1.4 multiply_reduce_fusion.3
  132.9 2.2 fusion.18
  135.2 1.5 convolution_convert_fusion
  136.6 107.9 %attend_back_kernel.1 = (f32[128,1024]{1,0:T(8,128)}, f32[96,1024]{1,0:T(8,128)}, f32[32,1024]{1,0:T(8,128)}, f32[164,1024]{1,0:T(8,128)}, f32[32,2624]{1,0:T(8,...) custom-call(bf16[16,64,128]{2,1,0:T(8,128)(2,1)} %bitcast.62, bf16[128,1024]{1,0:T(8,128)(2,1)} %copy-done.3, ...), custom_call_target="tpu_custom_call" | custom-call | flops 20000000000 | bytes 20000000 | tf_op jit(solution)/shard_map/attend_back_kernel/pallas_call | solution.py:1226
  244.6 1.3 dynamic-slice_bitcast_fusion
  245.9 1.3 multiply_reduce_fusion.2
  247.2 2.1 fusion.11
  249.3 0.7 copy.23
  250.1 0.7 copy.24
  250.7 0.8 copy.25
  251.6 0.7 copy.26
  252.3 0.5 copy.27
  (33 shorter events, 0.1 us)
Async XLA Ops:
  0.6 6.9 %copy-start = (bf16[512,2624]{0,1:T(8,128)(2,1)S(1)}, bf16[512,2624]{0,1:T(8,128)(2,1)}, u32[]{:S(2)}) copy-start(bf16[512,2624]{0,1:T(8,128)(2,1)} %param.15) | copy-start | bytes 8060932
  8.8 84.6 %copy-start.2 = (bf16[1,128,1024]{2,1,0:T(8,128)(2,1)S(1)}, bf16[1,128,1024]{2,1,0:T(8,128)(2,1)}, u32[]{:S(2)}) copy-start(bf16[1,128,1024]{2,1,0:T(8,128)(2,1)} %param.8) | copy-start | bytes 786436
  93.4 2.8 %copy-start.8 = (f32[1024]{0:T(1024)S(1)}, f32[1024]{0:T(1024)}, u32[]{:S(2)}) copy-start(f32[1024]{0:T(1024)} %param.11) | copy-start | bytes 12292
  97.1 34.4 %copy-start.9 = (f32[1024]{0:T(1024)S(1)}, f32[1024]{0:T(1024)}, u32[]{:S(2)}) copy-start(f32[1024]{0:T(1024)} %param.11) | copy-start | bytes 12292
  131.5 3.7 %copy-start.1 = (bf16[2,512,1024]{2,1,0:T(8,128)(2,1)S(1)}, bf16[2,512,1024]{2,1,0:T(8,128)(2,1)}, u32[]{:S(2)}) copy-start(bf16[2,512,1024]{2,1,0:T(8,128)(2,1)} %get-tuple-element.33) | copy-start | bytes 6291460
  135.2 1.5 copy-start.3
  136.6 109.2 %copy-start.10 = (f32[1024]{0:T(1024)S(1)}, f32[1024]{0:T(1024)}, u32[]{:S(2)}) copy-start(f32[1024]{0:T(1024)} %param.10) | copy-start | bytes 12292
  244.6 4.8 %copy-start.5 = (f32[96,1024]{1,0:T(8,128)S(1)}, f32[96,1024]{1,0:T(8,128)}, u32[]{:S(2)}) copy-start(f32[96,1024]{1,0:T(8,128)} %get-tuple-element.79) | copy-start | bytes 1179652
  244.6 5.5 %copy-start.7 = (f32[32,1024]{1,0:T(8,128)S(1)}, f32[32,1024]{1,0:T(8,128)}, u32[]{:S(2)}) copy-start(f32[32,1024]{1,0:T(8,128)} %get-tuple-element.80) | copy-start | bytes 393220
  244.6 6.2 %copy-start.4 = (f32[164,1024]{1,0:T(8,128)S(1)}, f32[164,1024]{1,0:T(8,128)}, u32[]{:S(2)}) copy-start(f32[164,1024]{1,0:T(8,128)} %get-tuple-element.81) | copy-start | bytes 2015236
  247.2 4.4 %copy-start.6 = (f32[32,2624]{1,0:T(8,128)S(1)}, f32[32,2624]{1,0:T(8,128)}, u32[]{:S(2)}) copy-start(f32[32,2624]{1,0:T(8,128)} %get-tuple-element.82) | copy-start | bytes 1007620
  247.2 5.1 %copy-start.11 = (f32[1,32]{1,0:T(1,128)S(1)}, f32[1,32]{1,0:T(1,128)}, u32[]{:S(2)}) copy-start(f32[1,32]{1,0:T(1,128)} %get-tuple-element.55) | copy-start | bytes 388

commit v4 on v3

--- a/solution.py
+++ b/solution.py
@@ -759,21 +759,21 @@
 
 
 def attend_kernel(
-    count, act, cot, qkv_weight, in_weight, down_mine, out_mine, cos, sine,
-    act_all, cot_all, query_t, keys_t, keys, values, mixed_own, log_sum, mixed, weight, in_other, down_other, out_pair,
+    count, tokens, cot, gain_attn, gain_mlp, qkv_weight, in_weight, down_mine, out_mine,
+    normed_a, inv_a, normed_m, inv_m, middle, act_m, cos, sine, act_all, cot_all, query_t, keys_t, keys, values, mixed_own, log_sum, mixed, weight, in_other, down_other, out_pair,
     values_t, load_sem, part_sem, part_got, piece_sem, piece_got, *sems
 ):
     f32, bf16 = jnp.float32, jnp.bfloat16
     p = Place(count)
-    rows, head = act.shape[0], keys_t.shape[0]
-    width = count * head
+    rows, width = tokens.shape
+    head = keys_t.shape[0]
     n = 8
     first = Gather(p, act_all, sems[:n])
     second = Quad(p, cot_all, sems[n : n + 2])
     trade = Exchange(p, mixed_own, mixed, sems[n + 2 :])
     half = out_mine.shape[0] // 2
     part_half = pl.ds(pl.multiple_of(p.core * half, half), half)
-    loads = [(act, act_all.at[p.me]), (cot, cot_all.at[p.x * 2 + p.core]), (out_mine, out_pair.at[p.pair])]
+    loads = [(cot, cot_all.at[p.x * 2 + p.core]), (out_mine, out_pair.at[p.pair])]
     loads = [pltpu.make_async_copy(src, dst, load_sem.at[i]) for i, (src, dst) in enumerate(loads)]
     for load in loads:
         load.start()
@@ -792,19 +792,17 @@
             p.over_pair(src, weight.at[part], part_sem.at[part], part_got.at[part]),
         )
 
-    units, columns, down_rows = in_other.shape[0], in_other.shape[1] // 2, down_other.shape[0] // 2
+    units, columns = in_other.shape[0], in_other.shape[1] // 2
     in_rows = pl.ds(pl.multiple_of((p.x * 2 + p.core) * units, 16), units)
     in_cols = pl.ds(pl.multiple_of(p.z % 2 * columns, columns), columns)
-    down_part = pl.ds(pl.multiple_of(p.z % 2 * down_rows, down_rows), down_rows)
-    in_here, down_here = in_other.at[:, in_cols], down_other.at[down_part]
+    in_here = in_other.at[:, in_cols]
     swaps = [
         p.over_pair(out_mine.at[part_half], out_pair.at[p.pair, part_half], piece_sem.at[0], piece_got.at[0]),
         p.over_pair(in_weight.at[in_rows, in_cols], in_here, piece_sem.at[1], piece_got.at[1]),
-        p.over_pair(down_mine.at[down_part], down_here, piece_sem.at[2], piece_got.at[2]),
+        p.over_pair(down_mine, down_other, piece_sem.at[2], piece_got.at[2]),
     ]
     next_z = p.me + 4 - p.z % 2 * 8
     in_share = p.copy(in_here, in_here, piece_sem.at[4], piece_got.at[4], next_z)
-    down_share = p.copy(down_here, down_here, piece_sem.at[5], piece_got.at[5], next_z)
     out_rest = out_pair.at[1 - p.pair, part_half]
     share = p.copy(out_rest, out_rest, piece_sem.at[3], piece_got.at[3], p.slot(p.z, p.x, 1 - p.core))
     for part in range(3):
@@ -822,12 +820,20 @@
         def _():
             away.start()
 
-    for swap in swaps:
-        swap.start()
+    for at in (1, 0, 2):
+        swaps[at].start()
+    resid = tokens[...].astype(f32)
+    normed, inv = normalize(resid)
+    normed_a[...], inv_a[...] = normed, inv
+    act_all[p.me] = (normed * gain_attn[...]).astype(bf16)
     for load in loads:
         load.wait()
 
     first.part(0)
+    position = lax.broadcasted_iota(jnp.int32, cos.shape, 1).astype(f32)
+    entry = lax.broadcasted_iota(jnp.int32, (cos.shape[0], 1), 0).astype(f32)
+    angles = position * jnp.exp(entry * (-2.0 * math.log(ROPE_BASE) / head))
+    cos[...], sine[...] = jnp.cos(angles), jnp.sin(angles)
     for part in range(3):
         here, own, away = part_copies(part)
 
@@ -839,7 +845,7 @@
         def _():
             away.wait_recv()
 
-    head_weight = weight[...].reshape(3 * head, act.shape[1])
+    head_weight = weight[...].reshape(3 * head, width)
 
     def project(z, x, core):
         at = p.slot(z, x, core)
@@ -861,6 +867,8 @@
         first.part(at, project)
 
     second.start()
+    swaps[1].wait_recv()
+    in_share.start()
     wide = 2 * rows
     blocks = count // 2
     scale = head ** (-0.5)
@@ -891,13 +899,17 @@
     def _(i):
         attend(i)
 
-    swaps[1].wait_recv()
-    in_share.start()
     trade.arrived()
+    share.wait_recv()
+    flat = mixed[...].reshape(width, rows)
+    total = tokens[...].astype(f32) + matmul(flat, out_pair[...].reshape(width, width), 0, 1)
+    middle[...] = total
+    normed, inv = normalize(total)
+    normed_m[...], inv_m[...] = normed, inv
+    act_m[...] = (normed * gain_mlp[...]).astype(bf16)
     second.beside().wait_recv()
     second.beside_next().wait_recv()
     swaps[2].wait_recv()
-    down_share.start()
     first.sent()
     second.sent()
     trade.sent()
@@ -910,15 +922,14 @@
 
     for swap in swaps:
         swap.wait_send()
-    share.wait()
+    share.wait_send()
     in_share.wait()
-    down_share.wait()
 
 
 def feed_kernel(
-    count, act, cot_all, in_weight, in_other, down_mine, down_other, gain,
-    grad_act, out_total, in_grad, down_grad,
-    weight, down, act_all, gated, inner_grad, grad_part, out_part, load_sem, *rest
+    count, act, cot_all, in_weight, in_other, down_mine, down_other, gain, out_pair, normed, inv, middle,
+    output, grad_middle, grad_mid, grad_mixed, in_grad, down_grad,
+    grad_act, out_total, weight, down, act_all, gated, inner_grad, grad_part, out_part, load_sem, *rest
 ):
     f32, bf16 = jnp.float32, jnp.bfloat16
     p = Place(count)
@@ -1006,7 +1017,15 @@
                 start = ((z * 4 + r) * 2 + y) * unit
                 down_grad[y * p.line + z, r] = piece[start : start + unit]
     grad_sum.finish(grad_act)
+    cot = cot_all[p.x * 2 + p.core].astype(f32)
+    grad = cot + norm_back(grad_act[...] * gain[...], normed[...], inv[...])
+    grad_middle[...] = grad
+    grad_mid[...] = grad.astype(bf16)
+    width = act.shape[1]
+    back = matmul(grad_mid[...], out_pair[...].reshape(width, width), 1, 0)
+    grad_mixed[...] = back.T.astype(bf16).reshape(grad_mixed.shape)
     out_sum.finish(out_total)
+    output[...] = middle[...] + out_total[...]
     gather.sent()
     grad_sum.sent()
     out_sum.sent()
@@ -1014,9 +1033,9 @@
 
 def attend_back_kernel(
     count, grad_mixed, grad_mid, mixed, query_t, keys_t, keys, values, mixed_own, log_sum,
-    act_all, weight, cos, sine, in_grad, down_grad, gain,
-    grad_act, qkv_out, out_out, in_out, down_out, gain_m_out, gain_a_out,
-    grad_own, grad_keys, grad_values, grad_packed, grad_part, grad_got, grad_sums, grad_weight,
+    act_all, weight, cos, sine, in_grad, down_grad, gain, grad_middle, normed, inv,
+    grad_input, qkv_out, out_out, in_out, down_out, gain_m_out, gain_a_out,
+    grad_act, grad_own, grad_keys, grad_values, grad_packed, grad_part, grad_got, grad_sums, grad_weight,
     pair_part, pair_core, pair_sums, pair_got, proj_sums, in_sum, in_got, down_sum, down_got,
     qkv_part, qkv_got, gain_part, gain_got,
     pair_s, pair_r, in_s, in_r, down_s, down_r, qkv_s, qkv_r, *rest
@@ -1047,6 +1066,8 @@
     def _(shift):
         trade.send((p.me + shift) % count)
 
+    settle_in.across(p.far(0)).start()
+    settle_down.across(p.far(0)).start()
     flat = mixed[...].reshape(width, rows)
 
     @pl.loop(0, count // 2)
@@ -1067,7 +1088,7 @@
         swap(2 * z).start()
         swap(2 * z + 1).start()
 
-    @pl.loop(0, p.line)
+    @pl.loop(1, p.line)
     def _(step):
         settle_in.across(p.far(step)).start()
         settle_down.across(p.far(step)).start()
@@ -1098,10 +1119,24 @@
     def _(i):
         back(i)
 
-        @pl.when(i == count // 4)
-        def _():
-            settle_in.pass_on(p.far(0))
-            settle_down.pass_on(p.far(0))
+    grad_key = grad_keys[...].T * scale
+    grad_packed[head : 2 * head, :] = rotate_rows_back(grad_key, cos[...], sine[...]).astype(bf16)
+    grad_packed[2 * head :, :] = grad_values[...].T.astype(bf16)
+
+    @pl.loop(0, p.line)
+    def _(step):
+        z = p.far(step)
+        for at in range(4):
+            lanes = pl.ds(pl.multiple_of((z * 4 + at) * rows, rows), rows)
+            grad_part[z * 4 + at] = matmul(grad_packed[:, lanes], weight[...], 0, 0).astype(bf16)
+        halve.beside(z, 0).start()
+        halve.beside(z, 1).start()
+
+    @pl.loop(0, p.line)
+    def _(step):
+        z = p.far(step)
+        halve.add(z)
+        settle.across(z).start()
 
     @pl.loop(0, p.line)
     def _(step):
@@ -1112,26 +1147,8 @@
             proj_sums[at] = (pair_sums[at, p.pair].astype(f32) + pair_got[at].astype(f32)).astype(bf16)
         settle_proj.across(z).start()
 
-    settle_in.pass_on(p.far(1))
-    settle_down.pass_on(p.far(1))
-    grad_key = grad_keys[...].T * scale
-    grad_packed[head : 2 * head, :] = rotate_rows_back(grad_key, cos[...], sine[...]).astype(bf16)
-    grad_packed[2 * head :, :] = grad_values[...].T.astype(bf16)
-
-    @pl.loop(0, p.line)
-    def _(step):
-        z = p.far(step)
-        for at in range(4):
-            lanes = pl.ds(pl.multiple_of((z * 4 + at) * rows, rows), rows)
-            grad_part[z * 4 + at] = matmul(grad_packed[:, lanes], weight[...], 0, 0).astype(bf16)
-        halve.beside(z, 0).start()
-        halve.beside(z, 1).start()
-
-    @pl.loop(0, p.line)
-    def _(step):
-        z = p.far(step)
-        halve.add(z)
-        settle.across(z).start()
+    settle_in.pass_on(p.far(0))
+    settle_down.pass_on(p.far(0))
 
     def grad_chunk(step):
         lanes = pl.ds(pl.multiple_of(step * 4 * rows, 4 * rows), 4 * rows)
@@ -1164,10 +1181,15 @@
         settle.pass_on(z)
         settle_proj.pass_on(z)
 
-        @pl.when(step > 1)
+        @pl.when(step == 1)
         def _():
             settle_in.pass_on(z)
             settle_down.pass_on(z)
+
+    @pl.loop(2, p.line)
+    def _(step):
+        settle_in.pass_on(p.far(step))
+        settle_down.pass_on(p.far(step))
 
     units = in_out.shape[0]
     r = p.x * 2 + p.core
@@ -1186,9 +1208,13 @@
     gain_a = gain_got[0]
     for at in range(1, 2 * count):
         gain_a += gain_got[at]
-    gain_a_out[...] = gain_a
+    chunks = 128 // unit
+    gain_a_out[...] = sum(
+        jnp.where(p.owner % chunks == at, gain_a[:, at * unit : (at + 1) * unit], 0.0) for at in range(chunks)
+    )
     settle_proj.finish(out_out)
     settle.finish(grad_act)
+    grad_input[...] = grad_middle[...] + norm_back(grad_act[...] * gain[...], normed[...], inv[...])
     half, r_of, k_of = p.owner // count, p.owner % count // 4, p.owner % 4
     source_in = ((half * 2 + k_of // 2) * 4 + r_of) * 2 + k_of % 2
     give_in.arrived(0, source_in)
@@ -1241,26 +1267,29 @@
     return jax.ShapeDtypeStruct(shape, kind)
 
 
-def attend(count, head, act, cot, qkv_weight, in_weight, down_mine, out_mine, cos, sine):
+def attend(count, head, tokens, cot, gain_attn, gain_mlp, qkv_weight, in_weight, down_mine, out_mine):
     bf16, f32 = jnp.bfloat16, jnp.float32
-    rows, width = act.shape
+    rows, width = tokens.shape
     length, line = rows * count, count // 4
     blocks = shaped((count, rows, width), bf16)
     tall, flat = shaped((head, length), bf16), shaped((length, head), bf16)
     heads = shaped((count, head, rows), bf16)
+    block, column, table = shaped((rows, width), f32), shaped((rows, 1), f32), shaped((head // 2, length), f32)
     pairs = [shaped((in_weight.shape[0] // 4, width), bf16), shaped(down_mine.shape, bf16), shaped((2,) + out_mine.shape, bf16)]
     three, six = pltpu.SemaphoreType.DMA((3,)), pltpu.SemaphoreType.DMA((6,))
     return run_kernel(
         functools.partial(attend_kernel, count),
-        [blocks, shaped((4, rows, width), bf16), tall, tall, flat, flat, heads, shaped((1, length), f32), heads, shaped((3, head, width), bf16)]
-        + pairs,
+        [block, column, block, column, block, shaped((rows, width), bf16), table, table,
+         blocks, shaped((4, rows, width), bf16), tall, tall, flat, flat, heads, shaped((1, length), f32), heads,
+         shaped((3, head, width), bf16)] + pairs,
         [pltpu.VMEM((head, length), bf16), pltpu.SemaphoreType.DMA((6,))] + [three, three, six, six]
         + Gather.sems(line) + Quad.sems() + Exchange.sems(count),
-        0, 10_000_000_000, [act, cot, qkv_weight, in_weight, down_mine, out_mine, cos, sine], (2, 3, 4, 5), (10, 11),
-    )
-
-
-def feed(count, group, act, cot_all, in_weight, in_other, down_mine, down_other, gain):
+        0, 10_000_000_000, [tokens, cot, gain_attn, gain_mlp, qkv_weight, in_weight, down_mine, out_mine], (4, 5, 6, 7),
+        (18, 19),
+    )
+
+
+def feed(count, group, act, cot_all, in_weight, in_other, down_mine, down_other, gain, out_pair, normed, inv, middle):
     bf16, f32 = jnp.bfloat16, jnp.float32
     rows, width = act.shape
     block = (rows, width)
@@ -1268,17 +1297,17 @@
     whole = pltpu.VMEM((4,) + block, bf16)
     return run_kernel(
         functools.partial(feed_kernel, count),
-        [shaped(block, f32), shaped(block, f32), shaped((2 * line, units // 4, width), bf16),
-         shaped((2 * line, 4, unit, group), bf16)],
-        [pltpu.VMEM((2 * group, width), bf16), pltpu.VMEM((width, group), bf16),
+        [shaped(block, f32), shaped(block, f32), shaped(block, bf16), shaped((count, width // count, rows), bf16),
+         shaped((2 * line, units // 4, width), bf16), shaped((2 * line, 4, unit, group), bf16)],
+        [pltpu.VMEM(block, f32), pltpu.VMEM(block, f32), pltpu.VMEM((2 * group, width), bf16), pltpu.VMEM((width, group), bf16),
          whole, pltpu.VMEM((4 * rows, group), bf16), pltpu.VMEM((4 * rows, 2 * group), bf16), whole, whole,
          pltpu.SemaphoreType.DMA((3,))]
         + Quad.sems() + QuadSum.bufs(block) * 2 + QuadSum.sems() * 2,
-        1, 20_000_000_000, [act, cot_all, in_weight, in_other, down_mine, down_other, gain], (2, 3),
-    )
-
-
-def attend_back(count, grad_mixed, grad_mid, mixed, kept, act_all, weight, cos, sine, in_grad, down_grad, gain):
+        1, 20_000_000_000, [act, cot_all, in_weight, in_other, down_mine, down_other, gain, out_pair, normed, inv, middle], (2, 3),
+    )
+
+
+def attend_back(count, grad_mixed, grad_mid, mixed, kept, act_all, weight, cos, sine, in_grad, down_grad, gain, grad_middle, normed, inv):
     bf16, f32 = jnp.bfloat16, jnp.float32
     rows, width = act_all.shape[1:]
     head, length, line = weight.shape[0] // 3, rows * count, count // 4
@@ -1295,8 +1324,8 @@
     return run_kernel(
         functools.partial(attend_back_kernel, count),
         [shaped(block, f32), shaped((3 * unit, width), f32), shaped(piece, f32),
-         shaped((units, width), f32), shaped((unit, units * count), f32), shaped((1, unit), f32), shaped((1, 128), f32)],
-        [held(count, head, rows), flat, flat, held(3 * head, length), whole, half, half,
+         shaped((units, width), f32), shaped((unit, units * count), f32), shaped((1, unit), f32), shaped((1, unit), f32)],
+        [pltpu.VMEM(block, f32), held(count, head, rows), flat, flat, held(3 * head, length), whole, half, half,
          pltpu.VMEM((3 * head, width), f32),
          held(count, 2, *piece), held(2 * line, 2, *piece), held(2 * line, 2, *piece), held(2 * line, *piece),
          held(2 * line, *piece), held(1, units, width), held(1, units, width), held(*down_block), held(*down_block),
@@ -1307,60 +1336,58 @@
         + Exchange.sems(count) + (Halve.sems(line) + Settle.sems(line)) * 2
         + Settle.sems(line) * 2 + Spread.sems(count),
         2, 20_000_000_000,
-        [grad_mixed, grad_mid, mixed, *kept, act_all, weight, cos, sine, in_grad, down_grad, gain],
-    )
+        [grad_mixed, grad_mid, mixed, *kept, act_all, weight, cos, sine, in_grad, down_grad, gain,
+         grad_middle, normed, inv],
+    )
+
+
+def publish_kernel(*refs):
+    half = len(refs) // 2
+    for src, dst in zip(refs[:half], refs[half:]):
+        dst[...] = src[...]
+
+
+def publish(arrays):
+    vmem = pl.BlockSpec(memory_space=pltpu.VMEM)
+    return pl.pallas_call(
+        publish_kernel,
+        out_shape=[shaped(array.shape, array.dtype) for array in arrays],
+        in_specs=[vmem] * len(arrays),
+        out_specs=[vmem] * len(arrays),
+        compiler_params=pltpu.CompilerParams(vmem_limit_bytes=VMEM_LIMIT),
+    )(*arrays)
 
 
 def tensor_layer(
     tokens, cotangent, gain_attn, gain_mlp, qkv_weight, out_weight, in_weight, down_weight
 ):
-    f32 = jnp.float32
-    bf16 = jnp.bfloat16
     count = lax.axis_size("ctx")
     index = lax.axis_index("ctx")
-    rows, width = tokens.shape[1], tokens.shape[2]
-    length = rows * count
+    width = tokens.shape[2]
     head_size = width // count
-    quad = lax.rem(index, 4)
     group = in_weight.shape[0] // 4
     padded = (group // 128 + 1) * 128
 
-    down_mine = lax.dynamic_slice_in_dim(down_weight, quad * group, group, 1)
-
-    cos_table, sine_table = rope_tables(0, length, head_size)
-    cos_table, sine_table = cos_table[:, 0, : head_size // 2].T, sine_table[:, 0, : head_size // 2].T
-    resid = tokens[0].astype(f32)
-    normed_a, inv_a = normalize(resid)
-    act_a = (normed_a * gain_attn).astype(bf16)
-    cot_rows = cotangent[0]
-    act_all, cot_all, *kept, mixed, qkv_head, in_other, down_other, out_pair = attend(
-        count, head_size, act_a, cot_rows, qkv_weight, in_weight, down_mine, out_weight, cos_table, sine_table
-    )
-    qkv_head = qkv_head.reshape(3 * head_size, width)
-    out_full = out_pair.reshape(width, width)
-    middle = resid + matmul(mixed.reshape(width, rows), out_full, 0, 1)
-    normed_m, inv_m = normalize(middle)
-    act_m = (normed_m * gain_mlp).astype(bf16)
-    grad_act_m, out_total, in_grad, down_grad = feed(
-        count, padded, act_m, cot_all, in_weight, in_other, down_mine, down_other, gain_mlp[None]
-    )
-
-    grad_middle = cot_rows.astype(f32) + norm_back(grad_act_m * gain_mlp, normed_m, inv_m)
-    grad_mid_bf = grad_middle.astype(bf16)
-    grad_mixed = matmul(out_full, grad_mid_bf, 0, 1).astype(bf16).reshape(count, head_size, rows)
-    grad_act_a, grad_qkv, grad_out, grad_in, grad_down, grad_gain_m, grad_gain_a = attend_back(
-        count, grad_mixed, grad_mid_bf, mixed, kept, act_all, qkv_head, cos_table, sine_table,
-        in_grad, down_grad, gain_attn[None],
-    )
-    unit = width // (2 * count)
-    lane = lax.rem((index * 2 + lax.axis_index("fsdp")) * unit, 128)
-    grad_gain_a = lax.dynamic_slice_in_dim(grad_gain_a[0], lane, unit)
-    output = middle + out_total
-    grad_input = grad_middle + norm_back(grad_act_a * gain_attn, normed_a, inv_a)
-    return (
-        output[None], grad_input[None], grad_qkv, grad_out, grad_in, grad_down,
-        grad_gain_a, grad_gain_m[0],
-    )
+    down_mine = lax.dynamic_slice_in_dim(down_weight, lax.rem(index, 4) * group, group, 1)
+    (
+        normed_a, inv_a, normed_m, inv_m, middle, act_m, cos, sine, act_all, cot_all, *kept,
+        mixed, qkv_head, in_other, down_other, out_pair,
+    ) = attend(
+        count, head_size, tokens[0], cotangent[0], gain_attn[None], gain_mlp[None],
+        qkv_weight, in_weight, down_mine, out_weight,
+    )
+    output, grad_middle, grad_mid, grad_mixed, in_grad, down_grad = feed(
+        count, padded, act_m, cot_all, in_weight, in_other, down_mine, down_other, gain_mlp[None],
+        out_pair, normed_m, inv_m, middle,
+    )
+    grad_input, grad_qkv, grad_out, grad_in, grad_down, grad_gain_m, grad_gain_a = attend_back(
+        count, grad_mixed, grad_mid, mixed, kept, act_all, qkv_head.reshape(3 * head_size, width), cos, sine,
+        in_grad, down_grad, gain_attn[None], grad_middle, normed_a, inv_a,
+    )
+    output, grad_input, grad_qkv, grad_out, grad_in, grad_down, grad_gain_a, grad_gain_m = publish(
+        [output, grad_input, grad_qkv, grad_out, grad_in, grad_down, grad_gain_a, grad_gain_m]
+    )
+    return (output[None], grad_input[None], grad_qkv, grad_out, grad_in, grad_down, grad_gain_a[0], grad_gain_m[0])
 
 
 def solution(mesh):

time: 257 us -> 220 us (0.86)
  other arithmetic: 14.9 us -> 0 us
  Pallas kernels: 227 us -> 213 us
  matrix products: 4.06 us -> 0 us
  local copies, waits for them, and re-layouts: 6.1 us -> 3.02 us
    pallas_call x3, Pallas kernels: 227 us -> 209 us  [run_kernel(): pl.pallas_call(body, out_shape=outs, in_specs=[anywhere if i in outside e...]
    reduce_sum x5 -> x0, other arithmetic: 5.26 us -> none  [the longest x2 2.68 us: norm_back(): jnp.mean(grad_norm, axis=-1, keepdims=True)]
    convert_element_type x4 -> x0, other arithmetic: 4.96 us -> none  [the longest x1 2.23 us: tensor_layer(): grad_mid_bf = grad_middle.astype(bf16)]
    dot_general x2 -> x0, matrix products: 4.06 us -> none  [matmul(): lax.dot_general(left, right, (((left_dim,), (right_dim,)), ((), ())), pre...]
    pallas_call x0 -> x1, Pallas kernels: none -> 3.21 us  [publish(): pl.pallas_call(publish_kernel, out_shape=[shaped(array.shape, array.dtype...]
where the time goes in v4:
time: 220 us; the launch traced here: 216 us
  Pallas kernels  213 us (97%)
  local copies, waits for them, and re-layouts  3.02 us (1%)
    pallas_call x3, Pallas kernels, run_kernel(): pl.pallas_call(body, out_shape=outs, in_specs=[anywhere if i in outside e...  209 us

profile of v4, /device:TPU:0, one launch (start us, length us, event | category | flops | bytes accessed | tf_op | source)
XLA Modules:
  0.0 216.3 jit_solution(11127838511356530859)
XLA Ops:
  0.6 0.0 copy-start
  0.7 1.7 copy-done
  2.4 1.2 copy.17.down_mine
  3.7 67.2 %attend_kernel.1 = (f32[128,1024]{1,0:T(8,128)}, f32[128,1]{1,0:T(8,128)}, f32[128,1024]{1,0:T(8,128)}, f32[128,1]{1,0:T(8,128)}, f32[128,1024]{1,0:T(8,128)}, /...) custom-call(bf16[128,1024]{1,0:T(8,128)(2,1)} %bitcast.11, ...), custom_call_target="tpu_custom_call" | custom-call | flops 10000000000 | bytes 20000000 | tf_op jit(solution)/shard_map/attend_kernel/pallas_call | solution.py:1252
  70.9 37.0 %feed_kernel.1 = (f32[128,1024]{1,0:T(8,128)}, f32[128,1024]{1,0:T(8,128)}, bf16[128,1024]{1,0:T(8,128)(2,1)}, bf16[16,64,128]{2,1,0:T(8,128)(2,1)}, bf16[8,164,...) custom-call(bf16[128,1024]{1,0:T(8,128)(2,1)} %get-tuple-element.50.act, ...), custom_call_target="tpu_custom_call" | custom-call | flops 20000000000 | bytes 20000000 | tf_op jit(solution)/shard_map/feed_kernel/pallas_call | solution.py:1252
  107.9 105.2 %attend_back_kernel.1 = (f32[128,1024]{1,0:T(8,128)}, f32[96,1024]{1,0:T(8,128)}, f32[32,1024]{1,0:T(8,128)}, f32[164,1024]{1,0:T(8,128)}, f32[32,2624]{1,0:T(8,128)}, /*index=5*/f32[1,32]{1,0:T(1,128)}, f32[1,32]{1,0:T(1,128)}) custom-call(bf16[16,64,128]{2,1,0:T(8,128)(2,1)} %get-tuple-element.59.grad_mixed, bf16[128,1024]{1,0:T(8,128)(2,1)} %get-tuple-element.60.grad_mid, ...), custom_call_target="tpu_custom_call" | custom-call | flops 20000000000 | bytes 20000000 | tf_op jit(solution)/shard_map/attend_back_kernel/pallas_call | solution.py:1252
  213.1 3.2 %shard_map.143 = (f32[128,1024]{1,0:T(8,128)}, f32[128,1024]{1,0:T(8,128)}, f32[96,1024]{1,0:T(8,128)}, f32[32,1024]{1,0:T(8,128)}, f32[164,1024]{1,0:T(8,128)},...) custom-call(f32[128,1024]{1,0:T(8,128)} %get-tuple-element.58.refs_0_, ...), custom_call_target="tpu_custom_call" | custom-call | tf_op jit(solution)/shard_map/pallas_call | solution.py:1352
  (1 shorter events, 0.0 us)
Async XLA Ops:
  0.6 1.8 copy-start

commit v5 on v4

--- a/solution.py
+++ b/solution.py
@@ -760,8 +760,8 @@
 
 def attend_kernel(
     count, tokens, cot, gain_attn, gain_mlp, qkv_weight, in_weight, down_mine, out_mine,
-    normed_a, inv_a, normed_m, inv_m, middle, act_m, cos, sine, act_all, cot_all, query_t, keys_t, keys, values, mixed_own, log_sum, mixed, weight, in_other, down_other, out_pair,
-    values_t, load_sem, part_sem, part_got, piece_sem, piece_got, *sems
+    normed_a, inv_a, normed_m, inv_m, middle, act_m, cos, sine, act_out, cot_all, query_t, keys_t, keys, values, mixed_own, log_sum, mixed, weight, in_other, down_other, out_pair,
+    act_all, values_t, load_sem, part_sem, part_got, piece_sem, piece_got, *sems
 ):
     f32, bf16 = jnp.float32, jnp.bfloat16
     p = Place(count)
@@ -866,6 +866,8 @@
     def _(at):
         first.part(at, project)
 
+    keep_act = pltpu.make_async_copy(act_all, act_out, load_sem.at[2])
+    keep_act.start()
     second.start()
     swaps[1].wait_recv()
     in_share.start()
@@ -924,6 +926,7 @@
         swap.wait_send()
     share.wait_send()
     in_share.wait()
+    keep_act.wait()
 
 
 def feed_kernel(
@@ -1033,9 +1036,9 @@
 
 def attend_back_kernel(
     count, grad_mixed, grad_mid, mixed, query_t, keys_t, keys, values, mixed_own, log_sum,
-    act_all, weight, cos, sine, in_grad, down_grad, gain, grad_middle, normed, inv,
+    act_in, weight, cos, sine, in_grad, down_grad, gain, grad_middle, normed, inv,
     grad_input, qkv_out, out_out, in_out, down_out, gain_m_out, gain_a_out,
-    grad_act, grad_own, grad_keys, grad_values, grad_packed, grad_part, grad_got, grad_sums, grad_weight,
+    act_all, act_sem, grad_act, grad_own, grad_keys, grad_values, grad_packed, grad_part, grad_got, grad_sums, grad_weight,
     pair_part, pair_core, pair_sums, pair_got, proj_sums, in_sum, in_got, down_sum, down_got,
     qkv_part, qkv_got, gain_part, gain_got,
     pair_s, pair_r, in_s, in_r, down_s, down_r, qkv_s, qkv_r, *rest
@@ -1060,14 +1063,19 @@
     def swap(at):
         return p.over_pair(pair_sums.at[at, 1 - p.pair], pair_got.at[at], pair_s.at[at], pair_r.at[at])
 
+    load_act = pltpu.make_async_copy(act_in, act_all, act_sem)
+    load_act.start()
     p.meet(True)
 
     @pl.loop(0, count)
     def _(shift):
         trade.send((p.me + shift) % count)
 
-    settle_in.across(p.far(0)).start()
-    settle_down.across(p.far(0)).start()
+    @pl.loop(0, p.line)
+    def _(step):
+        settle_in.across(p.far(step)).start()
+        settle_down.across(p.far(step)).start()
+
     flat = mixed[...].reshape(width, rows)
 
     @pl.loop(0, count // 2)
@@ -1087,11 +1095,6 @@
         halve_proj.add(z)
         swap(2 * z).start()
         swap(2 * z + 1).start()
-
-    @pl.loop(1, p.line)
-    def _(step):
-        settle_in.across(p.far(step)).start()
-        settle_down.across(p.far(step)).start()
 
     grad_keys[...] = jnp.zeros_like(grad_keys)
     grad_values[...] = jnp.zeros_like(grad_values)
@@ -1119,6 +1122,11 @@
     def _(i):
         back(i)
 
+        @pl.when(i == count // 4)
+        def _():
+            settle_in.pass_on(p.far(0))
+            settle_down.pass_on(p.far(0))
+
     grad_key = grad_keys[...].T * scale
     grad_packed[head : 2 * head, :] = rotate_rows_back(grad_key, cos[...], sine[...]).astype(bf16)
     grad_packed[2 * head :, :] = grad_values[...].T.astype(bf16)
@@ -1138,6 +1146,42 @@
         halve.add(z)
         settle.across(z).start()
 
+    def grad_chunk(step):
+        lanes = pl.ds(pl.multiple_of(step * 4 * rows, 4 * rows), 4 * rows)
+        acts = jnp.concatenate([act_all[4 * step + i] for i in range(4)], axis=0)
+        return matmul(grad_packed[:, lanes], acts, 1, 0)
+
+    load_act.wait()
+    grad_weight[...] = grad_chunk(0)
+
+    @pl.loop(1, p.line)
+    def _(step):
+        grad_weight[...] += grad_chunk(step)
+
+    for at in range(6):
+        qkv_part[at] = grad_weight[at * unit : (at + 1) * unit, :].astype(bf16)
+    gain_row = jnp.sum(grad_weight[...] * weight[...].astype(f32), axis=0, keepdims=True) / gain[...]
+    for at in range(2 * count):
+        chunk = at * unit // 128 * 128
+        gain_part[at] = gain_row[:, chunk : chunk + 128]
+
+    def unit_of(at):
+        return (at // 2) * 2 * count + 2 * p.me + at % 2
+
+    for at in range(6):
+        give_qkv.send(at, unit_of(at) // 3, unit_of(at) % 3 * 2 + p.pair)
+    spread_gain.send()
+
+    @pl.loop(0, p.line)
+    def _(step):
+        z = p.far(step)
+        settle.pass_on(z)
+
+        @pl.when(step > 0)
+        def _():
+            settle_in.pass_on(z)
+            settle_down.pass_on(z)
+
     @pl.loop(0, p.line)
     def _(step):
         z = p.far(step)
@@ -1147,49 +1191,9 @@
             proj_sums[at] = (pair_sums[at, p.pair].astype(f32) + pair_got[at].astype(f32)).astype(bf16)
         settle_proj.across(z).start()
 
-    settle_in.pass_on(p.far(0))
-    settle_down.pass_on(p.far(0))
-
-    def grad_chunk(step):
-        lanes = pl.ds(pl.multiple_of(step * 4 * rows, 4 * rows), 4 * rows)
-        acts = jnp.concatenate([act_all[4 * step + i] for i in range(4)], axis=0)
-        return matmul(grad_packed[:, lanes], acts, 1, 0)
-
-    grad_weight[...] = grad_chunk(0)
-
-    @pl.loop(1, p.line)
-    def _(step):
-        grad_weight[...] += grad_chunk(step)
-
-    for at in range(6):
-        qkv_part[at] = grad_weight[at * unit : (at + 1) * unit, :].astype(bf16)
-    gain_row = jnp.sum(grad_weight[...] * weight[...].astype(f32), axis=0, keepdims=True) / gain[...]
-    for at in range(2 * count):
-        chunk = at * unit // 128 * 128
-        gain_part[at] = gain_row[:, chunk : chunk + 128]
-
-    def unit_of(at):
-        return (at // 2) * 2 * count + 2 * p.me + at % 2
-
-    for at in range(6):
-        give_qkv.send(at, unit_of(at) // 3, unit_of(at) % 3 * 2 + p.pair)
-    spread_gain.send()
-
     @pl.loop(0, p.line)
     def _(step):
-        z = p.far(step)
-        settle.pass_on(z)
-        settle_proj.pass_on(z)
-
-        @pl.when(step == 1)
-        def _():
-            settle_in.pass_on(z)
-            settle_down.pass_on(z)
-
-    @pl.loop(2, p.line)
-    def _(step):
-        settle_in.pass_on(p.far(step))
-        settle_down.pass_on(p.far(step))
+        settle_proj.pass_on(p.far(step))
 
     units = in_out.shape[0]
     r = p.x * 2 + p.core
@@ -1282,10 +1286,10 @@
         [block, column, block, column, block, shaped((rows, width), bf16), table, table,
          blocks, shaped((4, rows, width), bf16), tall, tall, flat, flat, heads, shaped((1, length), f32), heads,
          shaped((3, head, width), bf16)] + pairs,
-        [pltpu.VMEM((head, length), bf16), pltpu.SemaphoreType.DMA((6,))] + [three, three, six, six]
+        [pltpu.VMEM(blocks.shape, bf16), pltpu.VMEM((head, length), bf16), pltpu.SemaphoreType.DMA((6,))] + [three, three, six, six]
         + Gather.sems(line) + Quad.sems() + Exchange.sems(count),
         0, 10_000_000_000, [tokens, cot, gain_attn, gain_mlp, qkv_weight, in_weight, down_mine, out_mine], (4, 5, 6, 7),
-        (18, 19),
+        (8, 18, 19),
     )
 
 
@@ -1325,7 +1329,7 @@
         functools.partial(attend_back_kernel, count),
         [shaped(block, f32), shaped((3 * unit, width), f32), shaped(piece, f32),
          shaped((units, width), f32), shaped((unit, units * count), f32), shaped((1, unit), f32), shaped((1, unit), f32)],
-        [pltpu.VMEM(block, f32), held(count, head, rows), flat, flat, held(3 * head, length), whole, half, half,
+        [whole, pltpu.SemaphoreType.DMA, pltpu.VMEM(block, f32), held(count, head, rows), flat, flat, held(3 * head, length), whole, half, half,
          pltpu.VMEM((3 * head, width), f32),
          held(count, 2, *piece), held(2 * line, 2, *piece), held(2 * line, 2, *piece), held(2 * line, *piece),
          held(2 * line, *piece), held(1, units, width), held(1, units, width), held(*down_block), held(*down_block),
@@ -1337,7 +1341,7 @@
         + Settle.sems(line) * 2 + Spread.sems(count),
         2, 20_000_000_000,
         [grad_mixed, grad_mid, mixed, *kept, act_all, weight, cos, sine, in_grad, down_grad, gain,
-         grad_middle, normed, inv],
+         grad_middle, normed, inv], (3 + len(kept),),
     )
 
 

time: 220 us -> 209 us (0.950)
  Pallas kernels: 213 us -> 202 us
    pallas_call x3, Pallas kernels: 209 us -> 199 us  [run_kernel(): pl.pallas_call(body, out_shape=outs, in_specs=[anywhere if i in outside e...]
where the time goes in v5:
time: 209 us; the launch traced here: 206 us
  Pallas kernels  202 us (97%)
  local copies, waits for them, and re-layouts  3.02 us (1%)
    pallas_call x3, Pallas kernels, run_kernel(): pl.pallas_call(body, out_shape=outs, in_specs=[anywhere if i in outside e...  199 us

profile of v5, /device:TPU:0, one launch (start us, length us, event | category | flops | bytes accessed | tf_op | source)
XLA Modules:
  0.0 205.7 jit_solution(857379156409207561)
XLA Ops:
  0.6 0.0 copy-start
  0.7 1.7 copy-done
  2.4 1.2 copy.17.down_mine
  3.7 65.9 %attend_kernel.1 = (f32[128,1024]{1,0:T(8,128)}, f32[128,1]{1,0:T(8,128)}, f32[128,1024]{1,0:T(8,128)}, f32[128,1]{1,0:T(8,128)}, f32[128,1024]{1,0:T(8,128)}, /...) custom-call(bf16[128,1024]{1,0:T(8,128)(2,1)} %bitcast.11, ...), custom_call_target="tpu_custom_call" | custom-call | flops 10000000000 | bytes 20000000 | tf_op jit(solution)/shard_map/attend_kernel/pallas_call | solution.py:1256
  69.6 37.0 %feed_kernel.1 = (f32[128,1024]{1,0:T(8,128)}, f32[128,1024]{1,0:T(8,128)}, bf16[128,1024]{1,0:T(8,128)(2,1)}, bf16[16,64,128]{2,1,0:T(8,128)(2,1)}, bf16[8,164,...) custom-call(bf16[128,1024]{1,0:T(8,128)(2,1)} %get-tuple-element.50.act, ...), custom_call_target="tpu_custom_call" | custom-call | flops 20000000000 | bytes 20000000 | tf_op jit(solution)/shard_map/feed_kernel/pallas_call | solution.py:1256
  106.6 95.9 %attend_back_kernel.1 = (f32[128,1024]{1,0:T(8,128)}, f32[96,1024]{1,0:T(8,128)}, f32[32,1024]{1,0:T(8,128)}, f32[164,1024]{1,0:T(8,128)}, f32[32,2624]{1,0:T(8,128)}, /*index=5*/f32[1,32]{1,0:T(1,128)}, f32[1,32]{1,0:T(1,128)}) custom-call(bf16[16,64,128]{2,1,0:T(8,128)(2,1)} %get-tuple-element.59.grad_mixed, bf16[128,1024]{1,0:T(8,128)(2,1)} %get-tuple-element.60.grad_mid, ...), custom_call_target="tpu_custom_call" | custom-call | flops 20000000000 | bytes 20000000 | tf_op jit(solution)/shard_map/attend_back_kernel/pallas_call | solution.py:1256
  202.5 3.2 %shard_map.143 = (f32[128,1024]{1,0:T(8,128)}, f32[128,1024]{1,0:T(8,128)}, f32[96,1024]{1,0:T(8,128)}, f32[32,1024]{1,0:T(8,128)}, f32[164,1024]{1,0:T(8,128)},...) custom-call(f32[128,1024]{1,0:T(8,128)} %get-tuple-element.58.refs_0_, ...), custom_call_target="tpu_custom_call" | custom-call | tf_op jit(solution)/shard_map/pallas_call | solution.py:1356
  (1 shorter events, 0.0 us)
Async XLA Ops:
  0.6 1.8 copy-start

commit v6 on v5

--- a/solution.py
+++ b/solution.py
@@ -930,9 +930,9 @@
 
 
 def feed_kernel(
-    count, act, cot_all, in_weight, in_other, down_mine, down_other, gain, out_pair, normed, inv, middle,
+    count, act, cot_all, in_weight, in_other, down_mine, down_other, gain, out_in, normed, inv, middle,
     output, grad_middle, grad_mid, grad_mixed, in_grad, down_grad,
-    grad_act, out_total, weight, down, act_all, gated, inner_grad, grad_part, out_part, load_sem, *rest
+    out_pair, grad_act, out_total, weight, down, act_all, gated, inner_grad, grad_part, out_part, load_sem, *rest
 ):
     f32, bf16 = jnp.float32, jnp.bfloat16
     p = Place(count)
@@ -952,6 +952,8 @@
     load.start()
     for copy in weights:
         copy.start()
+    load_out = pltpu.make_async_copy(out_in, out_pair, load_sem.at[3])
+    load_out.start()
     p.meet()
     load.wait()
     gather.start()
@@ -1025,6 +1027,7 @@
     grad_middle[...] = grad
     grad_mid[...] = grad.astype(bf16)
     width = act.shape[1]
+    load_out.wait()
     back = matmul(grad_mid[...], out_pair[...].reshape(width, width), 1, 0)
     grad_mixed[...] = back.T.astype(bf16).reshape(grad_mixed.shape)
     out_sum.finish(out_total)
@@ -1303,11 +1306,11 @@
         functools.partial(feed_kernel, count),
         [shaped(block, f32), shaped(block, f32), shaped(block, bf16), shaped((count, width // count, rows), bf16),
          shaped((2 * line, units // 4, width), bf16), shaped((2 * line, 4, unit, group), bf16)],
-        [pltpu.VMEM(block, f32), pltpu.VMEM(block, f32), pltpu.VMEM((2 * group, width), bf16), pltpu.VMEM((width, group), bf16),
+        [pltpu.VMEM(out_pair.shape, bf16), pltpu.VMEM(block, f32), pltpu.VMEM(block, f32), pltpu.VMEM((2 * group, width), bf16), pltpu.VMEM((width, group), bf16),
          whole, pltpu.VMEM((4 * rows, group), bf16), pltpu.VMEM((4 * rows, 2 * group), bf16), whole, whole,
-         pltpu.SemaphoreType.DMA((3,))]
+         pltpu.SemaphoreType.DMA((4,))]
         + Quad.sems() + QuadSum.bufs(block) * 2 + QuadSum.sems() * 2,
-        1, 20_000_000_000, [act, cot_all, in_weight, in_other, down_mine, down_other, gain, out_pair, normed, inv, middle], (2, 3),
+        1, 20_000_000_000, [act, cot_all, in_weight, in_other, down_mine, down_other, gain, out_pair, normed, inv, middle], (2, 3, 7),
     )
 
 

time: 209 us -> 209 us (level)
  no operation moved by 1% of the time
where the time goes in v6:
time: 209 us; the launch traced here: 205 us
  Pallas kernels  201 us (96%)
  local copies, waits for them, and re-layouts  3.02 us (1%)
    pallas_call x3, Pallas kernels, run_kernel(): pl.pallas_call(body, out_shape=outs, in_specs=[anywhere if i in outside e...  198 us

profile of v6, /device:TPU:0, one launch (start us, length us, event | category | flops | bytes accessed | tf_op | source)
XLA Modules:
  0.0 205.1 jit_solution(2467559499350746844)
XLA Ops:
  0.6 0.0 copy-start
  0.7 1.7 copy-done
  2.4 1.2 copy.17.down_mine
  3.7 65.9 %attend_kernel.1 = (f32[128,1024]{1,0:T(8,128)}, f32[128,1]{1,0:T(8,128)}, f32[128,1024]{1,0:T(8,128)}, f32[128,1]{1,0:T(8,128)}, f32[128,1024]{1,0:T(8,128)}, /...) custom-call(bf16[128,1024]{1,0:T(8,128)(2,1)} %bitcast.11, ...), custom_call_target="tpu_custom_call" | custom-call | flops 10000000000 | bytes 20000000 | tf_op jit(solution)/shard_map/attend_kernel/pallas_call | solution.py:1259
  69.6 36.4 %feed_kernel.1 = (f32[128,1024]{1,0:T(8,128)}, f32[128,1024]{1,0:T(8,128)}, bf16[128,1024]{1,0:T(8,128)(2,1)}, bf16[16,64,128]{2,1,0:T(8,128)(2,1)}, bf16[8,164,...) custom-call(bf16[128,1024]{1,0:T(8,128)(2,1)} %get-tuple-element.50.act, ...), custom_call_target="tpu_custom_call" | custom-call | flops 20000000000 | bytes 20000000 | tf_op jit(solution)/shard_map/feed_kernel/pallas_call | solution.py:1259
  106.0 95.9 %attend_back_kernel.1 = (f32[128,1024]{1,0:T(8,128)}, f32[96,1024]{1,0:T(8,128)}, f32[32,1024]{1,0:T(8,128)}, f32[164,1024]{1,0:T(8,128)}, f32[32,2624]{1,0:T(8,128)}, /*index=5*/f32[1,32]{1,0:T(1,128)}, f32[1,32]{1,0:T(1,128)}) custom-call(bf16[16,64,128]{2,1,0:T(8,128)(2,1)} %get-tuple-element.59.grad_mixed, bf16[128,1024]{1,0:T(8,128)(2,1)} %get-tuple-element.60.grad_mid, ...), custom_call_target="tpu_custom_call" | custom-call | flops 20000000000 | bytes 20000000 | tf_op jit(solution)/shard_map/attend_back_kernel/pallas_call | solution.py:1259
  201.9 3.2 %shard_map.143 = (f32[128,1024]{1,0:T(8,128)}, f32[128,1024]{1,0:T(8,128)}, f32[96,1024]{1,0:T(8,128)}, f32[32,1024]{1,0:T(8,128)}, f32[164,1024]{1,0:T(8,128)},...) custom-call(f32[128,1024]{1,0:T(8,128)} %get-tuple-element.58.refs_0_, ...), custom_call_target="tpu_custom_call" | custom-call | tf_op jit(solution)/shard_map/pallas_call | solution.py:1359
  (1 shorter events, 0.0 us)
Async XLA Ops:
  0.6 1.8 copy-start
